TPU v7x, 128 devices: a whole 4x4x4 slice. The times are simulated.
128 devices in a mesh: dp: 128 (over z, y, x, core).
Axes of the slice: x: 4, y: 4, z: 4, core: 2. Of those that a mesh axis runs over, the one named last changes fastest.
Arguments:
- x_layer0: bfloat16 [128, 1024, 576], P('dp')
- x_layer1: bfloat16 [128, 1024, 576], P('dp')
- d_out: bfloat16 [128, 1024, 576], P('dp')
- g_attn: bfloat16 [2, 576], replicated
- w_q: bfloat16 [2, 576, 9, 64], replicated
- w_k: bfloat16 [2, 576, 3, 64], replicated
- w_v: bfloat16 [2, 576, 3, 64], replicated
- w_o: bfloat16 [2, 9, 64, 576], replicated
- g_ffn: bfloat16 [2, 576], replicated
- w_gate: bfloat16 [2, 576, 1536], replicated
- w_up: bfloat16 [2, 576, 1536], replicated
- w_down: bfloat16 [2, 1536, 576], replicated
Outputs:
- output 1: bfloat16 [128, 1024, 576], P('dp')
- output 2: float32 [2, 576], replicated
- output 3: float32 [2, 576, 9, 64], replicated
- output 4: float32 [2, 576, 3, 64], replicated
- output 5: float32 [2, 576, 3, 64], replicated
- output 6: float32 [2, 9, 64, 576], replicated
- output 7: float32 [2, 576], replicated
- output 8: float32 [2, 576, 1536], replicated
- output 9: float32 [2, 576, 1536], replicated
- output 10: float32 [2, 1536, 576], replicated
All inputs are finite; a program needn't handle non-finite values.
Results may differ from a plain program's by a relative error of at most 0.02.
Values sent between devices are 32-bit elements.
A program may use at most 1 GiB of HBM per device.

v0:
```python
import jax
import jax.numpy as jnp
from jax import lax
from jax.sharding import PartitionSpec as P

NORM_EPS = 1e-6
ROPE_THETA = 10000.0


def rope_tables(seq_len, head_dim):
    positions = jnp.arange(seq_len, dtype=jnp.float32)
    inv_freq = ROPE_THETA ** (-jnp.arange(0, head_dim, 2, dtype=jnp.float32) / head_dim)
    angles = positions[:, None] * inv_freq[None, :]
    return jnp.cos(angles), jnp.sin(angles)


def rotate(values, cos_t, sin_t):
    x_pairs = values.reshape(values.shape[:-1] + (values.shape[-1] // 2, 2))
    x_even = x_pairs[..., 0]
    x_odd = x_pairs[..., 1]
    cos_b = cos_t[:, None, :]
    sin_b = sin_t[:, None, :]
    turned = jnp.stack([x_even * cos_b - x_odd * sin_b, x_even * sin_b + x_odd * cos_b], axis=-1)
    return turned.reshape(values.shape)


def norm_back(x_resid, inv_rms, gain, d_normed):
    scaled = d_normed * gain
    d_resid = inv_rms * scaled - x_resid * (inv_rms ** 3) * jnp.mean(scaled * x_resid, axis=-1, keepdims=True)
    d_gain = jnp.sum(d_normed * x_resid * inv_rms, axis=(0, 1))
    return d_resid, d_gain


def layer_backward(x_in, d_out, weights, cos_t, sin_t):
    g_attn, w_q, w_k, w_v, w_o, g_ffn, w_gate, w_up, w_down = weights
    n_batch, seq_len, model_dim = x_in.shape
    n_heads = w_q.shape[1]
    kv_heads = w_k.shape[1]
    head_dim = w_q.shape[2]
    n_group = n_heads // kv_heads
    att_scale = head_dim ** -0.5
    x_resid = x_in.astype(jnp.float32)
    gain_attn = g_attn.astype(jnp.float32)
    inv_attn = lax.rsqrt(jnp.mean(x_resid * x_resid, axis=-1, keepdims=True) + NORM_EPS)
    normed = (x_resid * inv_attn * gain_attn).astype(jnp.bfloat16)
    q_pre = jnp.einsum("bsd,dnh->bsnh", normed, w_q, preferred_element_type=jnp.float32).astype(jnp.bfloat16)
    k_pre = jnp.einsum("bsd,dnh->bsnh", normed, w_k, preferred_element_type=jnp.float32).astype(jnp.bfloat16)
    v_act = jnp.einsum("bsd,dnh->bsnh", normed, w_v, preferred_element_type=jnp.float32).astype(jnp.bfloat16)
    q_rot = rotate(q_pre.astype(jnp.float32), cos_t, sin_t).astype(jnp.bfloat16)
    q_grp = q_rot.reshape(n_batch, seq_len, kv_heads, n_group, head_dim)
    k_rot = rotate(k_pre.astype(jnp.float32), cos_t, sin_t).astype(jnp.bfloat16)
    causal = jnp.arange(seq_len)[:, None] >= jnp.arange(seq_len)[None, :]
    scores = jnp.einsum("bskgd,btkd->bkgst", q_grp, k_rot, preferred_element_type=jnp.float32) * att_scale
    p_attn = jax.nn.softmax(jnp.where(causal, scores, -1e30), axis=-1)
    p_bf16 = p_attn.astype(jnp.bfloat16)
    attn_out = jnp.einsum("bkgst,btkd->bskgd", p_bf16, v_act, preferred_element_type=jnp.float32).astype(jnp.bfloat16)
    attn_out = attn_out.reshape(n_batch, seq_len, n_heads, head_dim)
    x_mid = (x_resid + jnp.einsum("bsnh,nhd->bsd", attn_out, w_o, preferred_element_type=jnp.float32)).astype(jnp.bfloat16)
    x_mid_f = x_mid.astype(jnp.float32)
    gain_ffn = g_ffn.astype(jnp.float32)
    inv_ffn = lax.rsqrt(jnp.mean(x_mid_f * x_mid_f, axis=-1, keepdims=True) + NORM_EPS)
    normed_ffn = (x_mid_f * inv_ffn * gain_ffn).astype(jnp.bfloat16)
    gate_act = jnp.einsum("bsd,df->bsf", normed_ffn, w_gate, preferred_element_type=jnp.float32).astype(jnp.bfloat16)
    up_act = jnp.einsum("bsd,df->bsf", normed_ffn, w_up, preferred_element_type=jnp.float32).astype(jnp.bfloat16)
    gate_f = gate_act.astype(jnp.float32)
    gate_sig = jax.nn.sigmoid(gate_f)
    silu_act = gate_f * gate_sig
    up_f = up_act.astype(jnp.float32)
    hidden = (silu_act * up_f).astype(jnp.bfloat16)

    grad_w_down = jnp.einsum("bsf,bsd->fd", hidden, d_out, preferred_element_type=jnp.float32)
    d_hidden = jnp.einsum("bsd,fd->bsf", d_out, w_down, preferred_element_type=jnp.float32).astype(jnp.bfloat16).astype(jnp.float32)
    d_gate = (d_hidden * up_f * gate_sig * (1.0 + gate_f * (1.0 - gate_sig))).astype(jnp.bfloat16)
    d_up = (d_hidden * silu_act).astype(jnp.bfloat16)
    grad_w_gate = jnp.einsum("bsd,bsf->df", normed_ffn, d_gate, preferred_element_type=jnp.float32)
    grad_w_up = jnp.einsum("bsd,bsf->df", normed_ffn, d_up, preferred_element_type=jnp.float32)
    d_normed_ffn = (jnp.einsum("bsf,df->bsd", d_gate, w_gate, preferred_element_type=jnp.float32) + jnp.einsum("bsf,df->bsd", d_up, w_up, preferred_element_type=jnp.float32)).astype(jnp.bfloat16).astype(jnp.float32)
    d_mid_norm, grad_g_ffn = norm_back(x_mid_f, inv_ffn, gain_ffn, d_normed_ffn)
    d_mid = (d_out.astype(jnp.float32) + d_mid_norm).astype(jnp.bfloat16)
    grad_w_o = jnp.einsum("bsnh,bsd->nhd", attn_out, d_mid, preferred_element_type=jnp.float32)
    d_attn = jnp.einsum("bsd,nhd->bsnh", d_mid, w_o, preferred_element_type=jnp.float32).astype(jnp.bfloat16)
    d_attn = d_attn.reshape(n_batch, seq_len, kv_heads, n_group, head_dim)
    d_prob = jnp.einsum("bskgd,btkd->bkgst", d_attn, v_act, preferred_element_type=jnp.float32).astype(jnp.bfloat16).astype(jnp.float32)
    d_v = jnp.einsum("bkgst,bskgd->btkd", p_bf16, d_attn, preferred_element_type=jnp.float32).astype(jnp.bfloat16)
    row_dot = jnp.sum(p_attn * d_prob, axis=-1, keepdims=True)
    d_scores = (p_attn * (d_prob - row_dot) * att_scale).astype(jnp.bfloat16)
    d_q = jnp.einsum("bkgst,btkd->bskgd", d_scores, k_rot, preferred_element_type=jnp.float32).astype(jnp.bfloat16).astype(jnp.float32)
    d_q = d_q.reshape(n_batch, seq_len, n_heads, head_dim)
    d_k = jnp.einsum("bkgst,bskgd->btkd", d_scores, q_grp, preferred_element_type=jnp.float32).astype(jnp.bfloat16).astype(jnp.float32)
    d_q_pre = rotate(d_q, cos_t, -sin_t).astype(jnp.bfloat16)
    d_k_pre = rotate(d_k, cos_t, -sin_t).astype(jnp.bfloat16)
    grad_w_q = jnp.einsum("bsd,bsnh->dnh", normed, d_q_pre, preferred_element_type=jnp.float32)
    grad_w_k = jnp.einsum("bsd,bsnh->dnh", normed, d_k_pre, preferred_element_type=jnp.float32)
    grad_w_v = jnp.einsum("bsd,bsnh->dnh", normed, d_v, preferred_element_type=jnp.float32)
    d_normed = (jnp.einsum("bsnh,dnh->bsd", d_q_pre, w_q, preferred_element_type=jnp.float32) + jnp.einsum("bsnh,dnh->bsd", d_k_pre, w_k, preferred_element_type=jnp.float32) + jnp.einsum("bsnh,dnh->bsd", d_v, w_v, preferred_element_type=jnp.float32)).astype(jnp.bfloat16).astype(jnp.float32)
    d_x_norm, grad_g_attn = norm_back(x_resid, inv_attn, gain_attn, d_normed)
    d_x = (d_mid.astype(jnp.float32) + d_x_norm).astype(jnp.bfloat16)
    return d_x, (grad_g_attn, grad_w_q, grad_w_k, grad_w_v, grad_w_o, grad_g_ffn, grad_w_gate, grad_w_up, grad_w_down)


def solution(mesh):
    num_devices = mesh.shape["dp"]
    act_spec = P("dp", None, None)
    rep_spec = P()

    def local_step(x_layer0, x_layer1, d_out, g_attn, w_q, w_k, w_v, w_o, g_ffn, w_gate, w_up, w_down):
        weights = (g_attn, w_q, w_k, w_v, w_o, g_ffn, w_gate, w_up, w_down)
        cos_t, sin_t = rope_tables(x_layer0.shape[1], w_q.shape[3])
        d_x1, grads_top = layer_backward(x_layer1, d_out, tuple(weight[1] for weight in weights), cos_t, sin_t)
        d_x0, grads_low = layer_backward(x_layer0, d_x1, tuple(weight[0] for weight in weights), cos_t, sin_t)
        local_sums = tuple(jnp.stack([low_grad, top_grad]) for low_grad, top_grad in zip(grads_low, grads_top))
        totals = lax.psum(local_sums, "dp")
        inv_count = 1.0 / num_devices
        return (d_x0, totals[0] * inv_count, totals[1] * inv_count, totals[2] * inv_count, totals[3] * inv_count, totals[4] * inv_count, totals[5] * inv_count, totals[6] * inv_count, totals[7] * inv_count, totals[8] * inv_count)

    return jax.shard_map(local_step, mesh=mesh, in_specs=(act_spec, act_spec, act_spec) + (rep_spec,) * 9, out_specs=(act_spec,) + (rep_spec,) * 9, check_vma=False)
```

profile of v0, /device:TPU:1, one launch (start us, length us, event | category | flops | bytes accessed | tf_op | source)
XLA Modules:
  0.0 767.5 jit_solution(8889907388781817502)
XLA Ops:
  41.5 8.0 %subtract_convert_fusion.1 = (bf16[1,1024,9,32,1]{1,4,3,2,0:T(2,128)(2,1)S(1)}, bf16[1,1024,9,32,1]{1,4,3,2,0:T(2,128)(2,1)S(1)}, bf16[1,1024,9,32,1]{1,4,3,2,0:T(2,128)(2,1)S(1)}, bf16[1,1024,9,32,1]{1,4,3,2,0:T(2,128)(2,1)S(1)}) fusion(f32[1,1024,9,32,2]{1,4,3,2,0:T(2,128)} %reshape.930, f32[1024,32]{0,1:T(8,128)} %get-tuple-element.74, ...), kind=kLoop, calls=%fused_computation.257 | loop fusion | flops 4718592 | bytes 7340032 | tf_op jit(solution)/shard_map/convert.28
  49.5 6.3 pad_maximum_fusion.5
  58.8 15.4 %fusion.16 = (f32[3,3,1024]{2,1,0:T(4,128)S(1)}, f32[3,1024,1024,3]{2,1,3,0:T(8,128)}) fusion(pred[1024,1024]{0,1:T(8,128)(4,1)S(1)} %iota_compare_fusion, bf16[1024,3,3,64]{0,3,2,1:T(8,128)(2,1)S(1)} %convert_element_type.505, bf16[1024,3,64,1]{0,2,1,3:T(8,128)(2,1)S(1)} %copy-done.24), kind=kOutput, calls=%fused_computation.22 | convolution fusion | flops 1236261888 | bytes 40407040 | tf_op jit(solution)/shard_map/bskgd,btkd->bkgst/dot_general | solution.py:53
  74.2 16.4 %fusion.13 = f32[3,3,1024]{2,1,0:T(4,128)S(1)} fusion(f32[3,1024,1024,3]{2,1,3,0:T(8,128)} %get-tuple-element.77, f32[3,3,1024]{2,1,0:T(4,128)S(1)} %get-tuple-element.76, pred[1024,1024]{0,1:T(8,128)(4,1)S(1)} %iota_compare_fusion), kind=kLoop, calls=%fused_computation.19 | loop fusion | flops 37739520 | bytes 38871040 | tf_op jit(solution)/shard_map/reduce_sum | solution.py:54
  90.6 17.1 %fusion.130 = bf16[3,64,3,1024]{3,1,2,0:T(8,128)(2,1)} fusion(f32[1024,3,64]{0,2,1:T(8,128)S(1)} %bitcast.648, f32[3,3,1024]{2,1,0:T(4,128)S(1)} %fusion.13, f32[3,3,1024]{2,1,0:T(4,128)S(1)} %get-tuple-element.76, f32[3,1024,1024,3]{2,1,3,0:T(8,128)} %get-tuple-element.77, pred[1024,1024]{0,1:T(8,128)(4,1)S(1)} %iota_compare_fusion), kind=kOutput, calls=%fused_computation.209 | convolution fusion | flops 1255931904 | bytes 40837120 | tf_op jit(solution)/shard_map/bkgst,btkd->bskgd/dot_general | solution.py:56
  121.6 5.1 fusion.30
  147.5 18.5 %fusion.153 = bf16[3,64,1024]{2,1,0:T(8,128)(2,1)} fusion(bf16[1024,3,3,64]{0,3,2,1:T(8,128)(2,1)} %bitcast.644, f32[3,3,1024]{2,1,0:T(4,128)S(1)} %fusion.13, f32[3,3,1024]{2,1,0:T(4,128)S(1)} %get-tuple-element.76, f32[3,1024,1024,3]{2,1,3,0:T(8,128)} %get-tuple-element.77, pred[1024,1024]{0,1:T(8,128)(4,1)S(1)} %iota_compare_fusion), kind=kOutput, calls=%fused_computation.228 | convolution fusion | flops 1255342080 | bytes 40443904 | tf_op jit(solution)/shard_map/bkgst,bskgd->btkd/dot_general | solution.py:84
  166.0 14.7 %fusion.191 = f32[3,1024,1024,3]{2,1,3,0:T(8,128)} fusion(bf16[1024,3,3,64]{0,3,2,1:T(8,128)(2,1)S(1)} %convert_element_type.558, bf16[1024,3,64,1]{0,2,1,3:T(8,128)(2,1)S(1)} %copy-done.22), kind=kOutput, calls=%fused_computation.284 | convolution fusion | flops 1207959552 | bytes 39321600 | tf_op jit(solution)/shard_map/bskgd,btkd->bkgst/dot_general | solution.py:53
  180.7 33.5 %fusion.8 = (f32[3,3,1024]{2,1,0:T(4,128)S(1)}, f32[3,3,1024]{2,1,0:T(4,128)S(1)}, bf16[3,1024,1024,3]{2,1,3,0:T(8,128)(2,1)}) fusion(f32[3,3,1024]{2,1,0:T(4,128)S(1)} %fusion.13, f32[3,3,1024]{2,1,0:T(4,128)S(1)} %get-tuple-element.76, f32[3,1024,1024,3]{2,1,3,0:T(8,128)} %get-tuple-element.77, pred[1024,1024]{0,1:T(8,128)(4,1)S(1)} %iota_compare_fusion, ...), kind=kOutput, calls=%fused_computation.12 | convolution fusion | flops 1311946752 | bytes 97533952 | tf_op jit(solution)/shard_map/bskgd,btkd->bkgst/dot_general | solution.py:83
  214.2 41.6 %fusion.18 = (bf16[3,3,1024,1024]{2,3,1,0:T(8,128)(2,1)}, f32[3,3,1024]{2,1,0:T(4,128)}) fusion(bf16[3,1024,1024,3]{2,1,3,0:T(8,128)(2,1)} %get-tuple-element.81, f32[3,3,1024]{2,1,0:T(4,128)S(1)} %get-tuple-element.18, f32[3,3,1024]{2,1,0:T(4,128)S(1)} %fusion.13, f32[3,3,1024]{2,1,0:T(4,128)S(1)} %get-tuple-element.76, ...), kind=kLoop, calls=%fused_computation.24 | loop fusion | flops 122674176 | bytes 114479104 | tf_op jit(solution)/shard_map/reshape.79
  255.8 13.1 %fusion.161 = f32[1,1024,3,64]{1,3,2,0:T(8,128)} fusion(bf16[1024,3,3,64]{0,3,2,1:T(8,128)(2,1)S(1)} %copy-done.3, bf16[3,3,1024,1024]{2,3,1,0:T(8,128)(2,1)} %get-tuple-element.51), kind=kOutput, calls=%fused_computation.234 | convolution fusion | flops 1208352768 | bytes 20840448 | tf_op jit(solution)/shard_map/bkgst,bskgd->btkd/dot_general | solution.py:89
  268.9 11.2 %convert_bitcast_fusion.7 = f32[1,1024,3,3,64]{1,4,3,2,0:T(8,128)} fusion(bf16[3,3,1024,1024]{2,3,1,0:T(8,128)(2,1)} %get-tuple-element.51, bf16[1024,3,64,1]{0,2,1,3:T(8,128)(2,1)S(1)} %copy-done.25), kind=kOutput, calls=%fused_computation.176 | convolution fusion | flops 1209139200 | bytes 21626880 | tf_op jit(solution)/shard_map/bkgst,btkd->bskgd/dot_general | solution.py:87
  287.4 4.3 multiply_subtract_fusion.1
  298.6 17.3 %fusion.133 = bf16[3,64,3,1024]{3,1,2,0:T(8,128)(2,1)} fusion(f32[1024,3,64]{0,2,1:T(8,128)S(1)} %bitcast.650, f32[3,3,1024]{2,1,0:T(4,128)S(1)} %copy-done.67, f32[3,3,1024]{2,1,0:T(4,128)S(1)} %copy-done.66, f32[3,1024,1024,3]{2,1,3,0:T(8,128)} %fusion.191, pred[1024,1024]{0,1:T(8,128)(4,1)S(1)} %iota_compare_fusion), kind=kOutput, calls=%fused_computation.210 | convolution fusion | flops 1255931904 | bytes 40837120 | tf_op jit(solution)/shard_map/bkgst,btkd->bskgd/dot_general | solution.py:56
  334.9 5.4 fusion.35
  358.9 17.7 %fusion.150 = bf16[3,64,1024]{2,1,0:T(8,128)(2,1)S(1)} fusion(bf16[1024,3,3,64]{0,3,2,1:T(8,128)(2,1)} %bitcast.646, f32[3,3,1024]{2,1,0:T(4,128)S(1)} %copy-done.67, f32[3,3,1024]{2,1,0:T(4,128)S(1)} %copy-done.66, f32[3,1024,1024,3]{2,1,3,0:T(8,128)} %fusion.191, pred[1024,1024]{0,1:T(8,128)(4,1)S(1)} %iota_compare_fusion), kind=kOutput, calls=%fused_computation.227 | convolution fusion | flops 1255342080 | bytes 40443904 | tf_op jit(solution)/shard_map/bkgst,bskgd->btkd/dot_general | solution.py:84
  376.6 22.6 %fusion.2 = (f32[3,3,1024]{2,1,0:T(4,128)S(1)}, bf16[3,1024,1024,3]{2,1,3,0:T(8,128)(2,1)}) fusion(f32[3,3,1024]{2,1,0:T(4,128)S(1)} %copy-done.67, f32[3,3,1024]{2,1,0:T(4,128)S(1)} %copy-done.66, f32[3,1024,1024,3]{2,1,3,0:T(8,128)} %fusion.191, pred[1024,1024]{0,1:T(8,128)(4,1)S(1)} %iota_compare_fusion, bf16[1024,3,3,64]{0,3,2,1:T(8,128)(2,1)S(1)} %bitcast.647, ...), kind=kOutput, calls=%fused_computation.5 | convolution fusion | flops 1283644416 | bytes 59748352 | tf_op jit(solution)/shard_map/bskgd,btkd->bkgst/dot_general | solution.py:83
  399.3 25.8 %fusion.19 = bf16[3,3,1024,1024]{2,3,1,0:T(8,128)(2,1)} fusion(bf16[3,1024,1024,3]{2,1,3,0:T(8,128)(2,1)} %get-tuple-element.87, f32[3,3,1024]{2,1,0:T(4,128)S(1)} %get-tuple-element.86, f32[3,3,1024]{2,1,0:T(4,128)S(1)} %copy-done.67, f32[3,3,1024]{2,1,0:T(4,128)S(1)} %copy-done.66, f32[3,1024,1024,3]{2,1,3,0:T(8,128)} %fusion.191, ...), kind=kLoop, calls=%fused_computation.25 | loop fusion | flops 84934656 | bytes 76656640 | tf_op jit(solution)/shard_map/reshape.141
  425.0 9.8 %fusion.158 = f32[1,1024,3,64]{1,3,2,0:T(8,128)S(1)} fusion(bf16[1024,3,3,64]{0,3,2,1:T(8,128)(2,1)S(1)} %copy-done.1, bf16[3,3,1024,1024]{2,3,1,0:T(8,128)(2,1)} %fusion.19), kind=kOutput, calls=%fused_computation.231 | convolution fusion | flops 1208352768 | bytes 20840448 | tf_op jit(solution)/shard_map/bkgst,bskgd->btkd/dot_general | solution.py:89
  434.9 11.3 %convert_bitcast_fusion.6 = f32[1,1024,3,3,64]{1,4,3,2,0:T(8,128)} fusion(bf16[3,3,1024,1024]{2,3,1,0:T(8,128)(2,1)} %fusion.19, bf16[1024,3,64,1]{0,2,1,3:T(8,128)(2,1)S(1)} %copy-done.23), kind=kOutput, calls=%fused_computation.175 | convolution fusion | flops 1209139200 | bytes 21626880 | tf_op jit(solution)/shard_map/bkgst,btkd->bskgd/dot_general | solution.py:87
  459.8 4.4 multiply_subtract_fusion
  502.5 70.9 %all-reduce = (f32[2,576]{1,0:T(2,128)}, f32[2,576]{1,0:T(2,128)}) all-reduce(f32[2,576]{1,0:T(2,128)S(1)} %pad_maximum_fusion.11, f32[2,576]{1,0:T(2,128)S(1)} %pad_maximum_fusion.12), channel_id=1, replica_groups=mesh['dp'=128] {'dp'}, use_global_device_ids=true, to_apply=%region_16.17 | all-reduce | flops 2304 | bytes 18432 | tf_op jit(solution)/shard_map/psum | solution.py:112
  579.1 159.2 %all-reduce.4.cloned.1.call-done = (f32[2,576,9,64]{1,3,2,0:T(8,128)}, f32[2,576,3,64]{1,3,2,0:T(8,128)}, f32[2,576,3,64]{1,3,2,0:T(8,128)}, f32[2,9,64,576]{3,2...) async-done(((f32[2,576,9,64]{1,3,2,0:T(8,128)}, f32[2,576,3,64]{1,3,2,0:T(8,128)}, f32[2,576,3,64]{1,3,2,0:T(8,128)}, ...) | async-done | bytes 28311568 | tf_op jit(solution)/shard_map/psum | solution.py:112
  747.5 4.4 broadcast_multiply_fusion.2
  (334 shorter events, 198.0 us)
Async XLA Ops:
  7.2 731.2 %all-reduce.4.cloned.1.call-start = ((), (), s32[]{:S(2)}) async-start(), calls=%async_computation | async-start | bytes 58195968 | tf_op jit(solution)/shard_map/psum | solution.py:112
  10.3 25.8 %copy-start.71 = (f32[1024]{0:T(1024)}, f32[1024]{0:T(1024)S(1)}, u32[]{:S(2)}) copy-start(f32[1024]{0:T(1024)S(1)} %get-tuple-element.70) | copy-start | bytes 12292
  10.9 21.3 %copy-start.68 = (f32[1024]{0:T(1024)}, f32[1024]{0:T(1024)S(1)}, u32[]{:S(2)}) copy-start(f32[1024]{0:T(1024)S(1)} %get-tuple-element.66) | copy-start | bytes 12292
  10.9 21.2 %copy-start.75 = (f32[576]{0:T(1024)}, f32[576]{0:T(1024)S(1)}, u32[]{:S(2)}) copy-start(f32[576]{0:T(1024)S(1)} %get-tuple-element.23) | copy-start | bytes 6916
  11.0 25.1 %copy-start.78 = (f32[576]{0:T(1024)}, f32[576]{0:T(1024)S(1)}, u32[]{:S(2)}) copy-start(f32[576]{0:T(1024)S(1)} %get-tuple-element.22) | copy-start | bytes 6916
  12.8 28.7 %copy-start.4 = (f32[1024,32]{0,1:T(8,128)}, f32[1024,32]{0,1:T(8,128)S(1)}, u32[]{:S(2)}) copy-start(f32[1024,32]{0,1:T(8,128)S(1)} %get-tuple-element.75) | copy-start | bytes 393220
  58.8 15.4 %copy-start.2 = (bf16[1024,3,3,64]{0,3,2,1:T(8,128)(2,1)}, bf16[1024,3,3,64]{0,3,2,1:T(8,128)(2,1)S(1)}, u32[]{:S(2)}) copy-start(bf16[1024,3,3,64]{0,3,2,1:T(8,128)(2,1)S(1)} %convert_element_type.505) | copy-start | bytes 3538948
  74.2 16.4 %copy-start.99 = (f32[1024,192]{0,1:S(1)}, f32[1024,192]{0,1}, u32[]{:S(2)}) copy-start(f32[1024,192]{0,1} %fusion.237) | copy-start | bytes 2359300
  90.6 17.1 %copy-start.11 = (bf16[1,1024,576]{1,2,0:T(8,128)(2,1)S(1)}, bf16[1,1024,576]{1,2,0:T(8,128)(2,1)}, u32[]{:S(2)}) copy-start(bf16[1,1024,576]{1,2,0:T(8,128)(2,1)} %param.13) | copy-start | bytes 3538948
  147.5 18.5 %copy-start = (bf16[1024,3,3,64]{0,3,2,1:T(8,128)(2,1)}, bf16[1024,3,3,64]{0,3,2,1:T(8,128)(2,1)S(1)}, u32[]{:S(2)}) copy-start(bf16[1024,3,3,64]{0,3,2,1:T(8,128)(2,1)S(1)} %convert_element_type.558) | copy-start | bytes 3538948
  147.5 18.5 %copy-start.22 = (bf16[1024,3,64,1]{0,2,1,3:T(8,128)(2,1)S(1)}, bf16[1024,3,64,1]{0,2,1,3:T(8,128)(2,1)}, u32[]{:S(2)}) copy-start(bf16[1024,3,64,1]{0,2,1,3:T(8,128)(2,1)} %reshape.975) | copy-start | bytes 1179652
  166.0 14.7 %copy-start.100 = (f32[1024,192]{0,1:S(1)}, f32[1024,192]{0,1}, u32[]{:S(2)}) copy-start(f32[1024,192]{0,1} %fusion.237) | copy-start | bytes 2359300
  214.2 41.6 %copy-start.65 = (f32[3,3,1024]{2,1,0:T(4,128)}, f32[3,3,1024]{2,1,0:T(4,128)S(1)}, u32[]{:S(2)}) copy-start(f32[3,3,1024]{2,1,0:T(4,128)S(1)} %get-tuple-element.19) | copy-start | bytes 110596
  214.2 41.6 %copy-start.3 = (bf16[1024,3,3,64]{0,3,2,1:T(8,128)(2,1)S(1)}, bf16[1024,3,3,64]{0,3,2,1:T(8,128)(2,1)}, u32[]{:S(2)}) copy-start(bf16[1024,3,3,64]{0,3,2,1:T(8,128)(2,1)} %copy-done.2) | copy-start | bytes 3538948
  255.8 13.1 %copy-start.25 = (bf16[1024,3,64,1]{0,2,1,3:T(8,128)(2,1)S(1)}, bf16[1024,3,64,1]{0,2,1,3:T(8,128)(2,1)}, u32[]{:S(2)}) copy-start(bf16[1024,3,64,1]{0,2,1,3:T(8,128)(2,1)} %reshape.960) | copy-start | bytes 1179652
  268.9 11.7 %copy-start.5 = (f32[1024,32]{0,1:T(8,128)S(1)}, f32[1024,32]{0,1:T(8,128)}, u32[]{:S(2)}) copy-start(f32[1024,32]{0,1:T(8,128)} %copy-done.4) | copy-start | bytes 393220
  268.9 11.7 %copy-start.34 = (f32[1024,32]{0,1:T(8,128)S(1)}, f32[1024,32]{0,1:T(8,128)}, u32[]{:S(2)}) copy-start(f32[1024,32]{0,1:T(8,128)} %get-tuple-element.73) | copy-start | bytes 393220
  298.5 17.3 %copy-start.101 = (f32[1024,192]{0,1}, f32[1024,192]{0,1:S(1)}, u32[]{:S(2)}) copy-start(f32[1024,192]{0,1:S(1)} %fusion.249) | copy-start | bytes 2359300
  358.9 17.7 %copy-start.98 = (bf16[1024,9,64]{0,2,1:T(8,128)(2,1)S(1)}, bf16[1024,9,64]{0,2,1:T(8,128)(2,1)}, u32[]{:S(2)}) copy-start(bf16[1024,9,64]{0,2,1:T(8,128)(2,1)} %convolution_convert_fusion.10) | copy-start | bytes 3538948
  376.6 74.9 %copy-start.62 = (bf16[3,64,1024]{2,1,0:T(8,128)(2,1)}, bf16[3,64,1024]{2,1,0:T(8,128)(2,1)S(1)}, u32[]{:S(2)}) copy-start(bf16[3,64,1024]{2,1,0:T(8,128)(2,1)S(1)} %fusion.150) | copy-start | bytes 1179652
  399.2 25.8 %copy-start.1 = (bf16[1024,3,3,64]{0,3,2,1:T(8,128)(2,1)S(1)}, bf16[1024,3,3,64]{0,3,2,1:T(8,128)(2,1)}, u32[]{:S(2)}) copy-start(bf16[1024,3,3,64]{0,3,2,1:T(8,128)(2,1)} %copy-done) | copy-start | bytes 3538948
  434.9 11.3 %copy-start.13 = (bf16[1,1024,576]{1,2,0:T(8,128)(2,1)S(1)}, bf16[1,1024,576]{1,2,0:T(8,128)(2,1)}, u32[]{:S(2)}) copy-start(bf16[1,1024,576]{1,2,0:T(8,128)(2,1)} %param.13) | copy-start | bytes 3538948
  434.9 11.3 %copy-start.61 = (bf16[3,64,1024]{2,1,0:T(8,128)(2,1)S(1)}, bf16[3,64,1024]{2,1,0:T(8,128)(2,1)}, u32[]{:S(2)}) copy-start(bf16[3,64,1024]{2,1,0:T(8,128)(2,1)} %fusion.153) | copy-start | bytes 1179652
  500.1 76.6 %copy-start.19 = (bf16[1,1024,576]{1,2,0:T(8,128)(2,1)S(1)}, bf16[1,1024,576]{1,2,0:T(8,128)(2,1)}, u32[]{:S(2)}) copy-start(bf16[1,1024,576]{1,2,0:T(8,128)(2,1)} %copy-done.18) | copy-start | bytes 3538948
  (85 other events, 304.4 us)
Sparse Core Ops, SparseCore 0:
  495.6 242.7 all-reduce.3
where the time goes:
time: 772 us; the launch traced here: 767 us
  matrix products  302 us (39%)
  other arithmetic  177 us (23%)
  waiting for transfers between devices  159 us (21%)
  blocking collectives  70.9 us (9%)
  local copies, waits for them, and re-layouts  42.4 us (5%)
  between operations  15.4 us (2%)
    psum x1, waiting for transfers between devices, local_step(): totals = lax.psum(local_sums, 'dp')  159 us
    another operation x4, other arithmetic  78.9 us
    psum x1, blocking collectives, local_step(): totals = lax.psum(local_sums, 'dp')  70.9 us
    dot_general x2, matrix products, layer_backward(): jnp.einsum('bskgd,btkd->bkgst', d_attn, v_act, preferred_element_type=jnp...  56.1 us
    dot_general x2, matrix products, layer_backward(): jnp.einsum('bkgst,bskgd->btkd', p_bf16, d_attn, preferred_element_type=jn...  36.2 us
    dot_general x2, matrix products, layer_backward(): jnp.einsum('bkgst,btkd->bskgd', p_bf16, v_act, preferred_element_type=jnp...  34.4 us
    dot_general x2, matrix products, layer_backward(): jnp.einsum('bskgd,btkd->bkgst', q_grp, k_rot, preferred_element_type=jnp....  30.1 us
    dot_general x2, matrix products, layer_backward(): jnp.einsum('bkgst,bskgd->btkd', d_scores, q_grp, preferred_element_type=j...  23 us
  transfers between devices with their start and end apart: 1, of which 1 were waited for; matrix products, arithmetic and copies ran while one was open for 1% of the time, Pallas kernels for 0%

commit v1 on v0

v1 whole, which is shorter than its diff:
```python
import functools

import jax
import jax.numpy as jnp
import numpy as np
from jax import lax
from jax.experimental import pallas as pl
from jax.experimental.pallas import tpu as pltpu
from jax.sharding import PartitionSpec as P

NORM_EPS = 1e-6
ROPE_THETA = 10000.0
BLK = 256
LOG2E = 1.4426950408889634
F32 = jnp.float32
BF16 = jnp.bfloat16


def rope_tables_np(seq_len, head_dim):
    positions = np.arange(seq_len, dtype=np.float32)
    inv_freq = np.float32(ROPE_THETA) ** (-np.arange(0, head_dim, 2, dtype=np.float32) / np.float32(head_dim))
    angles = (positions[None, :] * inv_freq.astype(np.float32)[:, None]).astype(np.float32)
    cos_t = np.repeat(np.cos(angles), 2, axis=0).astype(np.float32)
    sin_t = np.repeat(np.sin(angles), 2, axis=0).astype(np.float32)
    sin_t[0::2] *= -1.0
    return cos_t, sin_t


def pair_swap(values):
    rows = values.shape[0]
    even = lax.broadcasted_iota(jnp.int32, values.shape, 0) % 2 == 0
    return jnp.where(even, pltpu.roll(values, rows - 1, 0), pltpu.roll(values, 1, 0))


def dot_nn(lhs, rhs):
    return lax.dot_general(lhs, rhs, (((1,), (0,)), ((), ())), preferred_element_type=F32)


def dot_nt(lhs, rhs):
    return lax.dot_general(lhs, rhs, (((1,), (1,)), ((), ())), preferred_element_type=F32)


def diag_mask():
    keys = lax.broadcasted_iota(jnp.int32, (BLK, BLK), 0)
    queries = lax.broadcasted_iota(jnp.int32, (BLK, BLK), 1)
    return queries >= keys


def attn_fwd_kernel(n_group, head_dim, att_scale, q_ref, k_ref, v_ref, cos_ref, sin_ref, a_ref, qr_ref, kr_ref, st_ref, k_scr):
    seq_len = k_ref.shape[1]
    n_blk = seq_len // BLK
    cos_t = cos_ref[...]
    sin_t = sin_ref[...]
    k_f = k_ref[...].astype(F32)
    k_rot = (k_f * cos_t + pair_swap(k_f) * sin_t).astype(BF16)
    kr_ref[...] = k_rot
    k_scr[...] = k_rot.astype(F32).T.astype(BF16)
    coef = att_scale * LOG2E
    mask = diag_mask()
    st_ref[...] = jnp.zeros_like(st_ref)
    for head in range(n_group):
        rows = slice(head * head_dim, (head + 1) * head_dim)
        q_f = q_ref[rows, :].astype(F32)
        qr_ref[rows, :] = (q_f * cos_t + pair_swap(q_f) * sin_t).astype(BF16)
        for j in range(n_blk):
            cols = slice(j * BLK, (j + 1) * BLK)
            q_j = qr_ref[rows, cols]
            s_blocks = []
            for i in range(j + 1):
                s_i = dot_nn(k_scr[i * BLK:(i + 1) * BLK, :], q_j)
                if i == j:
                    s_i = jnp.where(mask, s_i, -1e30)
                s_blocks.append(s_i)
            top = functools.reduce(jnp.maximum, [jnp.max(s_i, axis=0, keepdims=True) for s_i in s_blocks])
            e_blocks = [jnp.exp2((s_i - top) * coef) for s_i in s_blocks]
            total = functools.reduce(jnp.add, [jnp.sum(e_i, axis=0, keepdims=True) for e_i in e_blocks])
            inv = 1.0 / total
            acc = None
            for i in range(j + 1):
                p_i = (e_blocks[i] * inv).astype(BF16)
                part = dot_nn(v_ref[:, i * BLK:(i + 1) * BLK], p_i)
                acc = part if acc is None else acc + part
            a_ref[rows, cols] = acc.astype(BF16)
            st_ref[0, head:head + 1, cols] = top
            st_ref[0, n_group + head:n_group + head + 1, cols] = inv


def attn_bwd_kernel(n_group, head_dim, att_scale, qr_ref, kr_ref, v_ref, do_ref, st_ref, cos_ref, sin_ref, dq_ref, dk_ref, dv_ref, k_scr, v_scr, dk_acc, dv_acc):
    seq_len = kr_ref.shape[1]
    n_blk = seq_len // BLK
    k_scr[...] = kr_ref[...].astype(F32).T.astype(BF16)
    v_scr[...] = v_ref[...].astype(F32).T.astype(BF16)
    dk_acc[...] = jnp.zeros_like(dk_acc)
    dv_acc[...] = jnp.zeros_like(dv_acc)
    coef = att_scale * LOG2E
    mask = diag_mask()
    for head in range(n_group):
        rows = slice(head * head_dim, (head + 1) * head_dim)
        for j in range(n_blk):
            cols = slice(j * BLK, (j + 1) * BLK)
            q_j = qr_ref[rows, cols]
            do_j = do_ref[rows, cols]
            top = st_ref[0, head:head + 1, cols]
            inv = st_ref[0, n_group + head:n_group + head + 1, cols]
            p_blocks = []
            dp_blocks = []
            row_dot = None
            for i in range(j + 1):
                keys = slice(i * BLK, (i + 1) * BLK)
                s_i = dot_nn(k_scr[keys, :], q_j)
                if i == j:
                    s_i = jnp.where(mask, s_i, -1e30)
                p_i = jnp.exp2((s_i - top) * coef) * inv
                dp_i = dot_nn(v_scr[keys, :], do_j).astype(BF16).astype(F32)
                part = jnp.sum(p_i * dp_i, axis=0, keepdims=True)
                row_dot = part if row_dot is None else row_dot + part
                dv_acc[:, keys] += dot_nt(do_j, p_i.astype(BF16))
                p_blocks.append(p_i)
                dp_blocks.append(dp_i)
            dq_j = None
            for i in range(j + 1):
                keys = slice(i * BLK, (i + 1) * BLK)
                ds_i = (p_blocks[i] * (dp_blocks[i] - row_dot) * att_scale).astype(BF16)
                part = dot_nn(kr_ref[:, keys], ds_i)
                dq_j = part if dq_j is None else dq_j + part
                dk_acc[:, keys] += dot_nt(q_j, ds_i)
            dq_j = dq_j.astype(BF16).astype(F32)
            dq_ref[rows, cols] = (dq_j * cos_ref[:, cols] - pair_swap(dq_j) * sin_ref[:, cols]).astype(BF16)
    d_k = dk_acc[...].astype(BF16).astype(F32)
    dk_ref[...] = (d_k * cos_ref[...] - pair_swap(d_k) * sin_ref[...]).astype(BF16)
    dv_ref[...] = dv_acc[...].astype(BF16)


def attn_specs(kv_heads, n_group, head_dim, seq_len):
    q_spec = pl.BlockSpec((n_group * head_dim, seq_len), lambda g: (g, 0))
    kv_spec = pl.BlockSpec((head_dim, seq_len), lambda g: (g, 0))
    tab_spec = pl.BlockSpec((head_dim, seq_len), lambda g: (0, 0))
    st_spec = pl.BlockSpec((1, 8, seq_len), lambda g: (g, 0, 0))
    return q_spec, kv_spec, tab_spec, st_spec


def attn_forward(q_t, k_t, v_t, cos_t, sin_t, kv_heads, head_dim):
    seq_len = q_t.shape[1]
    n_group = q_t.shape[0] // k_t.shape[0]
    q_spec, kv_spec, tab_spec, st_spec = attn_specs(kv_heads, n_group, head_dim, seq_len)
    flops = 2 * 2 * q_t.shape[0] * seq_len * seq_len
    return pl.pallas_call(
        functools.partial(attn_fwd_kernel, n_group, head_dim, head_dim ** -0.5),
        grid=(kv_heads,),
        in_specs=[q_spec, kv_spec, kv_spec, tab_spec, tab_spec],
        out_specs=[q_spec, q_spec, kv_spec, st_spec],
        out_shape=[jax.ShapeDtypeStruct(q_t.shape, BF16), jax.ShapeDtypeStruct(q_t.shape, BF16), jax.ShapeDtypeStruct(k_t.shape, BF16), jax.ShapeDtypeStruct((kv_heads, 8, seq_len), F32)],
        scratch_shapes=[pltpu.VMEM((seq_len, head_dim), BF16)],
        compiler_params=pltpu.CompilerParams(vmem_limit_bytes=40 * 1024 * 1024),
        cost_estimate=pl.CostEstimate(flops=8 * flops, bytes_accessed=8 * q_t.size, transcendentals=0),
        name="attn_fwd",
    )(q_t, k_t, v_t, cos_t, sin_t)


def attn_backward(qr_t, kr_t, v_t, do_t, stats, cos_t, sin_t, kv_heads, head_dim):
    seq_len = qr_t.shape[1]
    n_group = qr_t.shape[0] // kr_t.shape[0]
    q_spec, kv_spec, tab_spec, st_spec = attn_specs(kv_heads, n_group, head_dim, seq_len)
    flops = 5 * 2 * qr_t.shape[0] * seq_len * seq_len
    return pl.pallas_call(
        functools.partial(attn_bwd_kernel, n_group, head_dim, head_dim ** -0.5),
        grid=(kv_heads,),
        in_specs=[q_spec, kv_spec, kv_spec, q_spec, st_spec, tab_spec, tab_spec],
        out_specs=[q_spec, kv_spec, kv_spec],
        out_shape=[jax.ShapeDtypeStruct(qr_t.shape, BF16), jax.ShapeDtypeStruct(kr_t.shape, BF16), jax.ShapeDtypeStruct(kr_t.shape, BF16)],
        scratch_shapes=[pltpu.VMEM((seq_len, head_dim), BF16), pltpu.VMEM((seq_len, head_dim), BF16), pltpu.VMEM((head_dim, seq_len), F32), pltpu.VMEM((head_dim, seq_len), F32)],
        compiler_params=pltpu.CompilerParams(vmem_limit_bytes=48 * 1024 * 1024),
        cost_estimate=pl.CostEstimate(flops=8 * flops, bytes_accessed=8 * qr_t.size, transcendentals=0),
        name="attn_bwd",
    )(qr_t, kr_t, v_t, do_t, stats, cos_t, sin_t)


def dot_c(lhs, rhs, c_l, c_r):
    return lax.dot_general(lhs, rhs, (((c_l,), (c_r,)), ((), ())), preferred_element_type=F32)


def norm_back_t(x_f, inv_rms, gain, d_normed):
    scaled = d_normed * gain
    d_resid = inv_rms * scaled - x_f * (inv_rms ** 3) * jnp.mean(scaled * x_f, axis=0, keepdims=True)
    d_gain = jnp.sum(d_normed * x_f * inv_rms, axis=1)
    return d_resid, d_gain


def layer_forward_t(x_t, weights, cos_t, sin_t, kv_heads, head_dim):
    g_attn, wq_t, wk_t, wv_t, w_o, g_ffn, w_gate, w_up, wd_t = weights
    x_f = x_t.astype(F32)
    inv_attn = lax.rsqrt(jnp.mean(x_f * x_f, axis=0, keepdims=True) + NORM_EPS)
    normed = (x_f * inv_attn * g_attn.astype(F32)[:, None]).astype(BF16)
    q_t = dot_c(wq_t, normed, 1, 0).astype(BF16)
    k_t = dot_c(wk_t, normed, 1, 0).astype(BF16)
    v_t = dot_c(wv_t, normed, 1, 0).astype(BF16)
    a_t, qr_t, kr_t, stats = attn_forward(q_t, k_t, v_t, cos_t, sin_t, kv_heads, head_dim)
    m_t = (x_f + dot_c(w_o, a_t, 0, 0)).astype(BF16)
    m_f = m_t.astype(F32)
    inv_ffn = lax.rsqrt(jnp.mean(m_f * m_f, axis=0, keepdims=True) + NORM_EPS)
    normed_ffn = (m_f * inv_ffn * g_ffn.astype(F32)[:, None]).astype(BF16)
    gate_t = dot_c(w_gate, normed_ffn, 0, 0).astype(BF16)
    up_t = dot_c(w_up, normed_ffn, 0, 0).astype(BF16)
    return x_f, inv_attn, normed, v_t, a_t, qr_t, kr_t, stats, m_f, inv_ffn, normed_ffn, gate_t, up_t


def layer_backward_t(saved, d_out_t, weights, cos_t, sin_t, kv_heads, head_dim, scale):
    g_attn, wq_t, wk_t, wv_t, w_o, g_ffn, w_gate, w_up, wd_t = weights
    x_f, inv_attn, normed, v_t, a_t, qr_t, kr_t, stats, m_f, inv_ffn, normed_ffn, gate_t, up_t = saved
    gate_f = gate_t.astype(F32)
    gate_sig = jax.nn.sigmoid(gate_f)
    silu_act = gate_f * gate_sig
    up_f = up_t.astype(F32)
    hidden = (silu_act * up_f).astype(BF16)
    grad_wd_t = dot_c(d_out_t, hidden, 1, 1) * scale
    d_hidden = dot_c(wd_t, d_out_t, 0, 0).astype(BF16).astype(F32)
    d_gate = (d_hidden * up_f * gate_sig * (1.0 + gate_f * (1.0 - gate_sig))).astype(BF16)
    d_up = (d_hidden * silu_act).astype(BF16)
    grad_w_gate = dot_c(normed_ffn, d_gate, 1, 1) * scale
    grad_w_up = dot_c(normed_ffn, d_up, 1, 1) * scale
    d_normed_ffn = (dot_c(w_gate, d_gate, 1, 0) + dot_c(w_up, d_up, 1, 0)).astype(BF16).astype(F32)
    d_mid_norm, grad_g_ffn = norm_back_t(m_f, inv_ffn, g_ffn.astype(F32)[:, None], d_normed_ffn)
    d_mid = (d_out_t.astype(F32) + d_mid_norm).astype(BF16)
    grad_w_o = dot_c(a_t, d_mid, 1, 1) * scale
    d_attn = dot_c(w_o, d_mid, 1, 0).astype(BF16)
    dq_t, dk_t, dv_t = attn_backward(qr_t, kr_t, v_t, d_attn, stats, cos_t, sin_t, kv_heads, head_dim)
    grad_wq_t = dot_c(dq_t, normed, 1, 1) * scale
    grad_wk_t = dot_c(dk_t, normed, 1, 1) * scale
    grad_wv_t = dot_c(dv_t, normed, 1, 1) * scale
    d_normed = (dot_c(wq_t, dq_t, 0, 0) + dot_c(wk_t, dk_t, 0, 0) + dot_c(wv_t, dv_t, 0, 0)).astype(BF16).astype(F32)
    d_x_norm, grad_g_attn = norm_back_t(x_f, inv_attn, g_attn.astype(F32)[:, None], d_normed)
    d_x = (d_mid.astype(F32) + d_x_norm).astype(BF16)
    return d_x, (grad_wd_t, grad_w_gate, grad_w_up, grad_w_o, grad_wq_t, grad_wk_t, grad_wv_t, grad_g_attn * scale, grad_g_ffn * scale)


def solution(mesh):
    num_devices = mesh.shape["dp"]
    act_spec = P("dp", None, None)
    rep_spec = P()

    def local_step(x_layer0, x_layer1, d_out, g_attn, w_q, w_k, w_v, w_o, g_ffn, w_gate, w_up, w_down):
        _, seq_len, model_dim = x_layer0.shape
        n_heads, head_dim = w_q.shape[2], w_q.shape[3]
        kv_heads = w_k.shape[2]
        cos_np, sin_np = rope_tables_np(seq_len, head_dim)
        cos_t, sin_t = jnp.asarray(cos_np), jnp.asarray(sin_np)
        scale = 1.0 / num_devices

        def layer_weights(layer):
            def heads_out(w):
                return jnp.transpose(w[layer], (1, 2, 0)).reshape(-1, model_dim)
            return (g_attn[layer], heads_out(w_q), heads_out(w_k), heads_out(w_v), w_o[layer].reshape(-1, model_dim), g_ffn[layer], w_gate[layer], w_up[layer], jnp.transpose(w_down[layer], (1, 0)))

        x0_t = jnp.transpose(x_layer0[0], (1, 0))
        x1_t = jnp.transpose(x_layer1[0], (1, 0))
        d_top = jnp.transpose(d_out[0], (1, 0))
        w_low, w_top = layer_weights(0), layer_weights(1)
        saved_top = layer_forward_t(x1_t, w_top, cos_t, sin_t, kv_heads, head_dim)
        d_mid, grads_top = layer_backward_t(saved_top, d_top, w_top, cos_t, sin_t, kv_heads, head_dim, scale)
        saved_low = layer_forward_t(x0_t, w_low, cos_t, sin_t, kv_heads, head_dim)
        d_x0, grads_low = layer_backward_t(saved_low, d_mid, w_low, cos_t, sin_t, kv_heads, head_dim, scale)
        stacked = [jnp.stack([low, top]) for low, top in zip(grads_low, grads_top)]
        gd, gg, gu, go, gq, gk, gv, g1, g2 = stacked
        big_o = jnp.concatenate([go, jnp.zeros((2, 8, model_dim), F32).at[:, 0].set(g1).at[:, 1].set(g2)], axis=1)
        gd, gg, gu, big_o, gq, gk, gv = lax.psum((gd, gg, gu, big_o, gq, gk, gv), "dp")
        go = big_o[:, :n_heads * head_dim]
        g1 = big_o[:, n_heads * head_dim]
        g2 = big_o[:, n_heads * head_dim + 1]

        def heads_in(g):
            return jnp.transpose(g.reshape(2, -1, head_dim, model_dim), (0, 3, 1, 2))

        d_x = jnp.transpose(d_x0, (1, 0))[None]
        return (d_x, g1, heads_in(gq), heads_in(gk), heads_in(gv), go.reshape(2, n_heads, head_dim, model_dim), g2, gg, gu, jnp.transpose(gd, (0, 2, 1)))

    return jax.shard_map(local_step, mesh=mesh, in_specs=(act_spec, act_spec, act_spec) + (rep_spec,) * 9, out_specs=(act_spec,) + (rep_spec,) * 9, check_vma=False)
```

time: 772 us -> 520 us (0.67)
  matrix products: 302 us -> 104 us
  other arithmetic: 177 us -> 37.6 us
  Pallas kernels: 0 us -> 78.5 us
  waiting for transfers between devices: 159 us -> 235 us
  blocking collectives: 70.9 us -> 0 us
    dot_general x40, matrix products: 281 us -> 104 us  [dot_c(): lax.dot_general(lhs, rhs, (((c_l,), (c_r,)), ((), ())), preferred_element...]
    another operation x15 -> x7, other arithmetic: 105 us -> 13.3 us  [the longest x5 13.3 us: local_step(): stacked = [jnp.stack([low, top]) for low, top in zip(grads_low, grads_top)]]
    pallas_call x0 -> x4, Pallas kernels: none -> 78.5 us  [the longest x2 48.2 us: attn_backward(): pl.pallas_call(functools.partial(attn_bwd_kernel, n_group, head_dim, head...]
    psum x1, waiting for transfers between devices: 159 us -> 235 us  [local_step(): lax.psum((gd, gg, gu, big_o, gq, gk, gv), 'dp')]
    psum x1 -> x0, blocking collectives: 70.9 us -> none  [local_step(): totals = lax.psum(local_sums, 'dp')]
    mul x9 -> x4, other arithmetic: 23.9 us -> 0.01 us  [the longest x2 0.01 us: layer_backward_t(): grad_g_ffn * scale]
    unnamed x12 -> x0, matrix products: 20.9 us -> none
    unnamed x220 -> x182, local copies, waits for them, and re-layouts: 12 us -> 28.2 us
where the time goes in v1:
time: 520 us; the launch traced here: 516 us
  waiting for transfers between devices  235 us (45%)
  matrix products  104 us (20%)
  Pallas kernels  78.5 us (15%)
  local copies, waits for them, and re-layouts  45.4 us (9%)
  other arithmetic  37.6 us (7%)
  between operations  15.3 us (3%)
    psum x1, waiting for transfers between devices, local_step(): lax.psum((gd, gg, gu, big_o, gq, gk, gv), 'dp')  235 us
    dot_general x40, matrix products, dot_c(): lax.dot_general(lhs, rhs, (((c_l,), (c_r,)), ((), ())), preferred_element...  104 us
    pallas_call x2, Pallas kernels, attn_backward(): pl.pallas_call(functools.partial(attn_bwd_kernel, n_group, head_dim, head...  48.2 us
    pallas_call x2, Pallas kernels, attn_forward(): pl.pallas_call(functools.partial(attn_fwd_kernel, n_group, head_dim, head...  30.3 us
    unnamed x182, local copies, waits for them, and re-layouts  28.2 us
    another operation x5, other arithmetic, local_step(): stacked = [jnp.stack([low, top]) for low, top in zip(grads_low, grads_top)]  13.3 us
  transfers between devices with their start and end apart: 1, of which 1 were waited for; matrix products, arithmetic and copies ran while one was open for 1% of the time, Pallas kernels for 0%

profile of v1, /device:TPU:1, one launch (start us, length us, event | category | flops | bytes accessed | tf_op | source)
XLA Modules:
  0.0 516.0 jit_solution(13830938687884335603)
XLA Ops:
  18.0 15.0 %attn_fwd.3 = (bf16[576,1024]{1,0:T(8,128)(2,1)S(1)}, bf16[576,1024]{1,0:T(8,128)(2,1)S(1)}, bf16[192,1024]{1,0:T(8,128)(2,1)S(1)}, f32[3,8,1024]{2,1,0:T(8,128)S(1)}) custom-call(bf16[576,1024]{1,0:T(8,128)(2,1)S(1)} %fusion.125.q_ref, bf16[192,1024]{1,0:T(8,128)(2,1)S(1)} %fusion.133.k_ref, bf16[192,1024]{1,0:T(8,128)(2,1)S(1)} %fusion.134.v_ref, ...), custom_call_target="tpu_custom_call" | custom-call | flops 19327352832 | bytes 4718592 | tf_op jit(solution)/shard_map/attn_fwd/pallas_call | solution.py:147
  36.4 4.2 convolution_convert_fusion
  40.6 4.2 convolution_convert_fusion.1
  44.8 15.3 %attn_fwd.2 = (bf16[576,1024]{1,0:T(8,128)(2,1)S(1)}, bf16[576,1024]{1,0:T(8,128)(2,1)S(1)}, bf16[192,1024]{1,0:T(8,128)(2,1)S(1)}, f32[3,8,1024]{2,1,0:T(8,128)S(1)}) custom-call(bf16[576,1024]{1,0:T(8,128)(2,1)S(1)} %fusion.123.q_ref, bf16[192,1024]{1,0:T(8,128)(2,1)S(1)} %fusion.131.k_ref, bf16[192,1024]{1,0:T(8,128)(2,1)S(1)} %fusion.132.v_ref, ...), custom_call_target="tpu_custom_call" | custom-call | flops 19327352832 | bytes 4718592 | tf_op jit(solution)/shard_map/attn_fwd/pallas_call | solution.py:147
  70.6 4.2 multiply_bitcast_fusion
  74.7 9.1 %fusion.3 = (bf16[1536,1024]{1,0:T(8,128)(2,1)}, bf16[1536,1024]{1,0:T(8,128)(2,1)}) fusion(bf16[1024,1536]{0,1:T(8,128)(2,1)} %copy-done.80, bf16[1024,1536]{0,1:T(8,128)(2,1)} %copy-done.81, bf16[1,1024,576]{1,2,0:T(8,128)(2,1)S(1)} %copy-done.10, bf16[2,1536,576]{1,2,0:T(8,128)(2,1)S(1)} %copy-done.68), kind=kOutput, calls=%fused_computation.8 | convolution fusion | flops 1838678016 | bytes 15532032 | tf_op jit(solution)/shard_map/dot_general | solution.py:179
  83.8 4.0 fusion.102
  87.9 3.8 multiply_bitcast_fusion.4
  91.7 3.8 multiply_bitcast_fusion.2
  103.1 24.3 %attn_bwd.2 = (bf16[576,1024]{1,0:T(8,128)(2,1)S(1)}, bf16[192,1024]{1,0:T(8,128)(2,1)S(1)}, bf16[192,1024]{1,0:T(8,128)(2,1)S(1)}) custom-call(bf16[576,1024]{1,0:T(8,128)(2,1)S(1)} %get-tuple-element.49.qr_ref, bf16[192,1024]{1,0:T(8,128)(2,1)S(1)} %get-tuple-element.50.kr_ref, bf16[192,1024]{1,0:T(8,128)(2,1)S(1)} %fusion.132.v_ref, ...), custom_call_target="tpu_custom_call" | custom-call | flops 48318382080 | bytes 4718592 | tf_op jit(solution)/shard_map/attn_bwd/pallas_call | solution.py:165
  137.5 4.3 multiply_bitcast_fusion.1
  141.8 7.1 %fusion.12 = (bf16[1536,1024]{1,0:T(8,128)(2,1)S(1)}, bf16[1536,1024]{1,0:T(8,128)(2,1)S(1)}) fusion(bf16[1024,1536]{0,1:T(8,128)(2,1)S(1)} %copy-done.78, bf16[1024,1536]{0,1:T(8,128)(2,1)} %convolution_convert_fusion.1, bf16[576,1024]{1,0:T(8,128)(2,1)S(1)} %fusion.43, bf16[2,1536,576]{1,2,0:T(8,128)(2,1)S(1)} %copy-done.69), kind=kOutput, calls=%fused_computation.23 | convolution fusion | flops 1838678016 | bytes 15532032 | tf_op jit(solution)/shard_map/dot_general | solution.py:179
  158.9 3.9 multiply_bitcast_fusion.3
  162.8 3.9 multiply_bitcast_fusion.5
  166.7 23.9 %attn_bwd.3 = (bf16[576,1024]{1,0:T(8,128)(2,1)S(1)}, bf16[192,1024]{1,0:T(8,128)(2,1)S(1)}, bf16[192,1024]{1,0:T(8,128)(2,1)S(1)}) custom-call(bf16[576,1024]{1,0:T(8,128)(2,1)S(1)} %get-tuple-element.56.qr_ref, bf16[192,1024]{1,0:T(8,128)(2,1)S(1)} %get-tuple-element.57.kr_ref, bf16[192,1024]{1,0:T(8,128)(2,1)S(1)} %copy-done.5, ...), custom_call_target="tpu_custom_call" | custom-call | flops 48318382080 | bytes 4718592 | tf_op jit(solution)/shard_map/attn_bwd/pallas_call | solution.py:165
  205.1 3.7 copy.42
  208.8 4.4 fusion.78
  214.3 6.8 %maximum_bitcast_fusion = f32[2,1536,576]{1,2,0:T(8,128)} fusion(f32[1,576,1536]{2,1,0:T(8,128)} %multiply_bitcast_fusion, f32[1,576,1536]{2,1,0:T(8,128)} %multiply_bitcast_fusion.1), kind=kLoop, calls=%fused_computation.4 | loop fusion | flops 1769472 | bytes 14155776 | tf_op jit(solution)/shard_map/transpose | solution.py:274
  221.1 4.2 pad_maximum_fusion
  232.3 4.6 scatter.9
  236.9 3.7 pad_maximum_fusion.2
  241.4 6.8 %fusion.137 = bf16[1,1024,576]{1,2,0:T(8,128)(2,1)} fusion(f32[1024]{0:T(1024)S(1)} %broadcast_multiply_fusion.4, f32[1024]{0:T(1024)S(1)} %copy-done.64, f32[576]{0:T(1024)S(1)} %copy-done.63, bf16[1024,576]{0,1:T(8,128)(2,1)} %get-tuple-element.122, f32[1024]{0:T(1024)S(1)} %copy-done.56, f32[1024]{0:T(1024)S(1)} %broadcast_multiply_fusion.5, ...), kind=kLoop, calls=%fused_computation.206 | loop fusion | flops 25952256 | bytes 14214144 | tf_op jit(solution)/shard_map/broadcast_in_dim | solution.py:273
  248.2 235.2 %all-reduce.4.cloned.1.call-done = (f32[2,584,576]{1,2,0:T(8,128)}, f32[2,576,9,64]{1,3,2,0:T(8,128)}, f32[2,576,3,64]{1,3,2,0:T(8,128)}, f32[2,576,3,64]{1,3,2,...) async-done(((f32[2,584,576]{1,2,0:T(8,128)}, f32[2,576,9,64]{1,3,2,0:T(8,128)}, f32[2,576,3,64]{1,3,2,0:T(8,128)}, ...) | async-done | bytes 28348432 | tf_op jit(solution)/shard_map/psum | solution.py:265
  489.7 3.9 copy.59
  (250 shorter events, 96.6 us)
Async XLA Ops:
  7.2 476.2 %all-reduce.4.cloned.1.call-start = ((), (), s32[]{:S(2)}) async-start(), calls=%async_computation | async-start | bytes 58195968 | tf_op jit(solution)/shard_map/psum | solution.py:265
  11.5 29.1 %copy-start.60 = (f32[576]{0:T(1024)}, f32[576]{0:T(1024)S(1)}, u32[]{:S(2)}) copy-start(f32[576]{0:T(1024)S(1)} %get-tuple-element.83) | copy-start | bytes 6916
  11.5 87.2 %copy-start.58 = (f32[576]{0:T(1024)}, f32[576]{0:T(1024)S(1)}, u32[]{:S(2)}) copy-start(f32[576]{0:T(1024)S(1)} %get-tuple-element.82) | copy-start | bytes 6916
  18.0 15.1 %copy-start.19 = (bf16[1,9,64,576]{3,2,1,0:T(8,128)(2,1)}, bf16[1,9,64,576]{3,2,1,0:T(8,128)(2,1)S(1)}, u32[]{:S(2)}) copy-start(bf16[1,9,64,576]{3,2,1,0:T(8,128)(2,1)S(1)} %get-tuple-element.102) | copy-start | bytes 1990660
  35.8 4.9 copy-start.13
  62.7 36.0 %copy-start.49 = (f32[1024]{0:T(1024)}, f32[1024]{0:T(1024)S(1)}, u32[]{:S(2)}) copy-start(f32[1024]{0:T(1024)S(1)} %get-tuple-element.115) | copy-start | bytes 12292
  62.7 36.0 %copy-start.51 = (f32[1024]{0:T(1024)}, f32[1024]{0:T(1024)S(1)}, u32[]{:S(2)}) copy-start(f32[1024]{0:T(1024)S(1)} %get-tuple-element.116) | copy-start | bytes 12292
  74.7 9.1 %copy-start.71 = (bf16[2,576,1536]{2,1,0:T(8,128)(2,1)S(1)}, bf16[2,576,1536]{2,1,0:T(8,128)(2,1)}, u32[]{:S(2)}) copy-start(bf16[2,576,1536]{2,1,0:T(8,128)(2,1)} %param.27) | copy-start | bytes 10616836
  103.1 24.3 %copy-start.43 = (f32[1024]{0:T(1024)S(1)}, f32[1024]{0:T(1024)}, u32[]{:S(2)}) copy-start(f32[1024]{0:T(1024)} %copy-done.42) | copy-start | bytes 12292
  103.1 24.3 %copy-start.45 = (f32[576]{0:T(1024)S(1)}, f32[576]{0:T(1024)}, u32[]{:S(2)}) copy-start(f32[576]{0:T(1024)} %copy-done.44) | copy-start | bytes 6916
  134.9 6.8 %copy-start.9 = (bf16[1024,576]{0,1:T(8,128)(2,1)}, bf16[1024,576]{0,1:T(8,128)(2,1)S(1)}, u32[]{:S(2)}) copy-start(bf16[1024,576]{0,1:T(8,128)(2,1)S(1)} %get-tuple-element.119) | copy-start | bytes 3538948
  141.8 7.1 %copy-start.72 = (bf16[2,576,1536]{2,1,0:T(8,128)(2,1)S(1)}, bf16[2,576,1536]{2,1,0:T(8,128)(2,1)}, u32[]{:S(2)}) copy-start(bf16[2,576,1536]{2,1,0:T(8,128)(2,1)} %param.27) | copy-start | bytes 10616836
  166.7 23.9 %copy-start.8 = (bf16[1,1024,576]{1,2,0:T(8,128)(2,1)S(1)}, bf16[1,1024,576]{1,2,0:T(8,128)(2,1)}, u32[]{:S(2)}) copy-start(bf16[1,1024,576]{1,2,0:T(8,128)(2,1)} %param.18) | copy-start | bytes 3538948
  166.7 23.9 %copy-start.56 = (f32[1024]{0:T(1024)S(1)}, f32[1024]{0:T(1024)}, u32[]{:S(2)}) copy-start(f32[1024]{0:T(1024)} %copy-done.55) | copy-start | bytes 12292
  166.7 23.9 %copy-start.63 = (f32[576]{0:T(1024)S(1)}, f32[576]{0:T(1024)}, u32[]{:S(2)}) copy-start(f32[576]{0:T(1024)} %copy-done.62) | copy-start | bytes 6916
  214.3 6.8 %copy-start.15 = (f32[1,576,1536]{2,1,0:T(8,128)S(1)}, f32[1,576,1536]{2,1,0:T(8,128)}, u32[]{:S(2)}) copy-start(f32[1,576,1536]{2,1,0:T(8,128)} %multiply_bitcast_fusion.4) | copy-start | bytes 10616836
  214.3 6.8 %copy-start.18 = (f32[1,576,1536]{2,1,0:T(8,128)S(1)}, f32[1,576,1536]{2,1,0:T(8,128)}, u32[]{:S(2)}) copy-start(f32[1,576,1536]{2,1,0:T(8,128)} %multiply_bitcast_fusion.5) | copy-start | bytes 10616836
  221.1 5.6 %copy-start.17 = (f32[1,576,1536]{2,1,0:T(8,128)S(1)}, f32[1,576,1536]{2,1,0:T(8,128)}, u32[]{:S(2)}) copy-start(f32[1,576,1536]{2,1,0:T(8,128)} %multiply_bitcast_fusion.3) | copy-start | bytes 10616836
  486.1 10.8 %slice-start.4 = ((s8[7077888]{0:T(1024)(128)(4,1)}), s8[2883584]{0:T(1024)(128)(4,1)S(1)}, s32[]{:S(2)}) async-start(s8[7077888]{0:T(1024)(128)(4,1)} %bitcast.463), calls=%async_computation.5 | async-start | bytes 5767168
  489.7 6.2 %copy-start.24 = (f32[2,576,3,64]{1,3,2,0:T(8,128)S(1)}, f32[2,576,3,64]{1,3,2,0:T(8,128)}, u32[]{:S(2)}) copy-start(f32[2,576,3,64]{1,3,2,0:T(8,128)} %get-tuple-element.131) | copy-start | bytes 2654212
  489.7 7.2 %slice-start.5 = ((s8[7077888]{0:T(1024)(128)(4,1)}), s8[4194304]{0:T(1024)(128)(4,1)S(1)}, s32[]{:S(2)}) async-start(s8[7077888]{0:T(1024)(128)(4,1)} %bitcast.463), calls=%async_computation.6 | async-start | bytes 8388608
  493.6 6.9 %slice-start.2 = ((s8[7077888]{0:T(1024)(128)(4,1)}), s8[4194304]{0:T(1024)(128)(4,1)S(1)}, s32[]{:S(2)}) async-start(s8[7077888]{0:T(1024)(128)(4,1)} %bitcast.461), calls=%async_computation.3 | async-start | bytes 8388608
  496.9 7.5 %slice-start = ((s8[7077888]{0:T(1024)(128)(4,1)}), s8[4194304]{0:T(1024)(128)(4,1)S(1)}, s32[]{:S(2)}) async-start(s8[7077888]{0:T(1024)(128)(4,1)} %bitcast.459), calls=%async_computation.1 | async-start | bytes 8388608
  500.8 5.2 %slice-start.1 = ((s8[7077888]{0:T(1024)(128)(4,1)}), s8[2883584]{0:T(1024)(128)(4,1)S(1)}, s32[]{:S(2)}) async-start(s8[7077888]{0:T(1024)(128)(4,1)} %bitcast.459), calls=%async_computation.2 | async-start | bytes 5767168
  (65 other events, 167.9 us)
Sparse Core Ops, SparseCore 0:
  240.8 242.5 all-reduce.3

commit v2 on v1

v2 whole, which is shorter than its diff:
```python
import functools

import jax
import jax.numpy as jnp
import numpy as np
from jax import lax
from jax.experimental import pallas as pl
from jax.experimental.pallas import tpu as pltpu
from jax.sharding import PartitionSpec as P

NORM_EPS = 1e-6
ROPE_THETA = 10000.0
BLK = 256
LOG2E = 1.4426950408889634
F32 = jnp.float32
BF16 = jnp.bfloat16


def rope_tables_np(seq_len, head_dim):
    positions = np.arange(seq_len, dtype=np.float32)
    inv_freq = np.float32(ROPE_THETA) ** (-np.arange(0, head_dim, 2, dtype=np.float32) / np.float32(head_dim))
    angles = (positions[None, :] * inv_freq.astype(np.float32)[:, None]).astype(np.float32)
    cos_t = np.repeat(np.cos(angles), 2, axis=0).astype(np.float32)
    sin_t = np.repeat(np.sin(angles), 2, axis=0).astype(np.float32)
    sin_t[0::2] *= -1.0
    return cos_t, sin_t


def pair_swap(values):
    rows = values.shape[0]
    even = lax.broadcasted_iota(jnp.int32, values.shape, 0) % 2 == 0
    return jnp.where(even, pltpu.roll(values, rows - 1, 0), pltpu.roll(values, 1, 0))


def dot_nn(lhs, rhs):
    return lax.dot_general(lhs, rhs, (((1,), (0,)), ((), ())), preferred_element_type=F32)


def dot_nt(lhs, rhs):
    return lax.dot_general(lhs, rhs, (((1,), (1,)), ((), ())), preferred_element_type=F32)


def diag_mask():
    keys = lax.broadcasted_iota(jnp.int32, (BLK, BLK), 0)
    queries = lax.broadcasted_iota(jnp.int32, (BLK, BLK), 1)
    return queries >= keys


def attn_fwd_kernel(n_group, head_dim, att_scale, qkv_ref, cos_ref, sin_ref, a_ref, rot_ref, st_ref, k_scr):
    seq_len = qkv_ref.shape[1]
    n_blk = seq_len // BLK
    q_rows = n_group * head_dim
    cos_t = cos_ref[...]
    sin_t = sin_ref[...]
    k_f = qkv_ref[q_rows:q_rows + head_dim, :].astype(F32)
    k_rot = (k_f * cos_t + pair_swap(k_f) * sin_t).astype(BF16)
    rot_ref[q_rows:q_rows + head_dim, :] = k_rot
    k_scr[...] = k_rot.astype(F32).T.astype(BF16)
    coef = att_scale * LOG2E
    mask = diag_mask()
    st_ref[...] = jnp.zeros_like(st_ref)
    for head in range(n_group):
        rows = slice(head * head_dim, (head + 1) * head_dim)
        q_f = qkv_ref[rows, :].astype(F32)
        rot_ref[rows, :] = (q_f * cos_t + pair_swap(q_f) * sin_t).astype(BF16)
        for j in range(n_blk):
            cols = slice(j * BLK, (j + 1) * BLK)
            q_j = rot_ref[rows, cols]
            s_blocks = []
            for i in range(j + 1):
                s_i = dot_nn(k_scr[i * BLK:(i + 1) * BLK, :], q_j)
                if i == j:
                    s_i = jnp.where(mask, s_i, -1e30)
                s_blocks.append(s_i)
            top = functools.reduce(jnp.maximum, [jnp.max(s_i, axis=0, keepdims=True) for s_i in s_blocks])
            e_blocks = [jnp.exp2((s_i - top) * coef) for s_i in s_blocks]
            total = functools.reduce(jnp.add, [jnp.sum(e_i, axis=0, keepdims=True) for e_i in e_blocks])
            inv = 1.0 / total
            acc = None
            for i in range(j + 1):
                p_i = (e_blocks[i] * inv).astype(BF16)
                part = dot_nn(qkv_ref[q_rows + head_dim:q_rows + 2 * head_dim, i * BLK:(i + 1) * BLK], p_i)
                acc = part if acc is None else acc + part
            a_ref[rows, cols] = acc.astype(BF16)
            st_ref[0, head:head + 1, cols] = top
            st_ref[0, n_group + head:n_group + head + 1, cols] = inv


def attn_bwd_kernel(n_group, head_dim, att_scale, rot_ref, v_ref, do_ref, st_ref, cos_ref, sin_ref, dqkv_ref, k_scr, v_scr, dk_acc, dv_acc):
    seq_len = rot_ref.shape[1]
    n_blk = seq_len // BLK
    q_rows = n_group * head_dim
    k_rows = slice(q_rows, q_rows + head_dim)
    k_scr[...] = rot_ref[k_rows, :].astype(F32).T.astype(BF16)
    v_scr[...] = v_ref[...].astype(F32).T.astype(BF16)
    dk_acc[...] = jnp.zeros_like(dk_acc)
    dv_acc[...] = jnp.zeros_like(dv_acc)
    coef = att_scale * LOG2E
    mask = diag_mask()
    for head in range(n_group):
        rows = slice(head * head_dim, (head + 1) * head_dim)
        for j in range(n_blk):
            cols = slice(j * BLK, (j + 1) * BLK)
            q_j = rot_ref[rows, cols]
            do_j = do_ref[rows, cols]
            top = st_ref[0, head:head + 1, cols]
            inv = st_ref[0, n_group + head:n_group + head + 1, cols]
            p_blocks = []
            dp_blocks = []
            row_dot = None
            for i in range(j + 1):
                keys = slice(i * BLK, (i + 1) * BLK)
                s_i = dot_nn(k_scr[keys, :], q_j)
                if i == j:
                    s_i = jnp.where(mask, s_i, -1e30)
                p_i = jnp.exp2((s_i - top) * coef) * inv
                dp_i = dot_nn(v_scr[keys, :], do_j).astype(BF16).astype(F32)
                part = jnp.sum(p_i * dp_i, axis=0, keepdims=True)
                row_dot = part if row_dot is None else row_dot + part
                dv_acc[:, keys] += dot_nt(do_j, p_i.astype(BF16))
                p_blocks.append(p_i)
                dp_blocks.append(dp_i)
            dq_j = None
            for i in range(j + 1):
                keys = slice(i * BLK, (i + 1) * BLK)
                ds_i = (p_blocks[i] * (dp_blocks[i] - row_dot) * att_scale).astype(BF16)
                part = dot_nn(rot_ref[k_rows, keys], ds_i)
                dq_j = part if dq_j is None else dq_j + part
                dk_acc[:, keys] += dot_nt(q_j, ds_i)
            dq_j = dq_j.astype(BF16).astype(F32)
            dqkv_ref[rows, cols] = (dq_j * cos_ref[:, cols] - pair_swap(dq_j) * sin_ref[:, cols]).astype(BF16)
    d_k = dk_acc[...].astype(BF16).astype(F32)
    dqkv_ref[k_rows, :] = (d_k * cos_ref[...] - pair_swap(d_k) * sin_ref[...]).astype(BF16)
    dqkv_ref[q_rows + head_dim:q_rows + 2 * head_dim, :] = dv_acc[...].astype(BF16)


def attn_forward(qkv_t, cos_t, sin_t, kv_heads, n_group, head_dim):
    seq_len = qkv_t.shape[1]
    per = (n_group + 2) * head_dim
    tab_spec = pl.BlockSpec((head_dim, seq_len), lambda g: (0, 0))
    flops = 2 * 2 * kv_heads * n_group * head_dim * seq_len * seq_len
    return pl.pallas_call(
        functools.partial(attn_fwd_kernel, n_group, head_dim, head_dim ** -0.5),
        grid=(kv_heads,),
        in_specs=[pl.BlockSpec((per, seq_len), lambda g: (g, 0)), tab_spec, tab_spec],
        out_specs=[pl.BlockSpec((n_group * head_dim, seq_len), lambda g: (g, 0)), pl.BlockSpec(((n_group + 1) * head_dim, seq_len), lambda g: (g, 0)), pl.BlockSpec((1, 8, seq_len), lambda g: (g, 0, 0))],
        out_shape=[jax.ShapeDtypeStruct((kv_heads * n_group * head_dim, seq_len), BF16), jax.ShapeDtypeStruct((kv_heads * (n_group + 1) * head_dim, seq_len), BF16), jax.ShapeDtypeStruct((kv_heads, 8, seq_len), F32)],
        scratch_shapes=[pltpu.VMEM((seq_len, head_dim), BF16)],
        compiler_params=pltpu.CompilerParams(vmem_limit_bytes=40 * 1024 * 1024),
        cost_estimate=pl.CostEstimate(flops=8 * flops, bytes_accessed=8 * qkv_t.size, transcendentals=0),
        name="attn_fwd",
    )(qkv_t, cos_t, sin_t)


def attn_backward(rot_t, qkv_t, do_t, stats, cos_t, sin_t, kv_heads, n_group, head_dim):
    seq_len = qkv_t.shape[1]
    per = (n_group + 2) * head_dim
    tab_spec = pl.BlockSpec((head_dim, seq_len), lambda g: (0, 0))
    flops = 5 * 2 * kv_heads * n_group * head_dim * seq_len * seq_len
    return pl.pallas_call(
        functools.partial(attn_bwd_kernel, n_group, head_dim, head_dim ** -0.5),
        grid=(kv_heads,),
        in_specs=[
            pl.BlockSpec(((n_group + 1) * head_dim, seq_len), lambda g: (g, 0)),
            pl.BlockSpec((head_dim, seq_len), lambda g: (g * (n_group + 2) + n_group + 1, 0)),
            pl.BlockSpec((n_group * head_dim, seq_len), lambda g: (g, 0)),
            pl.BlockSpec((1, 8, seq_len), lambda g: (g, 0, 0)),
            tab_spec,
            tab_spec,
        ],
        out_specs=pl.BlockSpec((per, seq_len), lambda g: (g, 0)),
        out_shape=jax.ShapeDtypeStruct(qkv_t.shape, BF16),
        scratch_shapes=[pltpu.VMEM((seq_len, head_dim), BF16), pltpu.VMEM((seq_len, head_dim), BF16), pltpu.VMEM((head_dim, seq_len), F32), pltpu.VMEM((head_dim, seq_len), F32)],
        compiler_params=pltpu.CompilerParams(vmem_limit_bytes=48 * 1024 * 1024),
        cost_estimate=pl.CostEstimate(flops=8 * flops, bytes_accessed=8 * qkv_t.size, transcendentals=0),
        name="attn_bwd",
    )(rot_t, qkv_t, do_t, stats, cos_t, sin_t)


MESH = pl.DeviceIdType.MESH
N_RED = 3
N_ICI = 6


def add_rows(dst, src, rows, step):
    @pl.loop(0, rows // step)
    def _(i):
        part = pl.ds(pl.multiple_of(i * step, 8), step)
        dst[part, :] = dst[part, :] + src[part, :]


def all_reduce_kernel(a_rows, a_lanes, q_rows, o_rows, *refs):
    srcs = [refs[5 * layer:5 * layer + 5] for layer in range(2)]
    gain_ref = refs[10]
    out_a, out_q, out_o, out_g = refs[11:15]
    acc_a, acc_b = refs[15:17]
    bufs_a = refs[17:24]
    bufs_b = refs[24:31]
    gain_bufs = refs[31]
    (core_send, core_recv, load_sem, ici_send, ici_recv, ag_send, ag_recv, fin_send, fin_recv, fin_loc, g_send, g_recv, g_loc) = refs[32:45]

    me = lax.axis_index("dp")
    core = lax.rem(me, 2)
    coords = (lax.rem(me // 2, 4), lax.rem(me // 8, 4), me // 32)
    strides = (2, 8, 32)
    peer = me + 1 - 2 * core
    gens = []
    for kind in range(2):
        for axis in range(3):
            v = coords[axis]
            if kind == 0:
                partner, bit = v + 1 - 2 * lax.rem(v, 2), lax.rem(v + v // 2, 2)
            else:
                partner, bit = 3 - v, v // 2
            gens.append((me + (partner - v) * strides[axis], bit))

    barrier = pltpu.get_barrier_semaphore()
    for dev in [peer] + [g[0] for g in gens]:
        pl.semaphore_signal(barrier, inc=1, device_id=(dev,), device_id_type=MESH)
    pl.semaphore_wait(barrier, 1 + N_ICI)

    half = a_rows // 2
    lanes = a_lanes // 2
    o_half = o_rows // 12
    q_half = q_rows // 12
    b_rows = o_half + q_half

    def ds8(start, size):
        return pl.ds(pl.multiple_of(start, 8), size)

    def remote(src, dst, send, recv, dev):
        return pltpu.make_async_remote_copy(src_ref=src, dst_ref=dst, send_sem=send, recv_sem=recv, device_id=(dev,), device_id_type=MESH)

    flows = [(layer, k) for layer in (1, 0) for k in range(6)]
    core_copies = {}
    load_copies = {}
    for layer, k in flows:
        mat = srcs[layer][k // 2]
        q_src, o_src = srcs[layer][3:]
        lane = slice((k % 2) * lanes, (k % 2 + 1) * lanes)

        def parts(which):
            return (
                (mat.at[ds8(which * half, half), lane], lambda buf_a, buf_b: buf_a.at[layer, k]),
                (o_src.at[ds8(k * 2 * o_half + which * o_half, o_half), :], lambda buf_a, buf_b: buf_b.at[layer, k, 0:o_half, :]),
                (q_src.at[ds8(k * 2 * q_half + which * q_half, q_half), :], lambda buf_a, buf_b: buf_b.at[layer, k, o_half:b_rows, :]),
            )

        sends = [remote(src, dst(bufs_a[0], bufs_b[0]), core_send.at[layer, k, p], core_recv.at[layer, k, p], peer) for p, (src, dst) in enumerate(parts(1 - core))]
        loads = [pltpu.make_async_copy(src, dst(acc_a, acc_b), load_sem.at[layer, k, p]) for p, (src, dst) in enumerate(parts(core))]
        for copy in sends + loads:
            copy.start()
        core_copies[layer, k] = sends
        load_copies[layer, k] = loads
    gain_copy = remote(gain_ref, gain_bufs.at[0], g_send.at[0], g_recv.at[0], peer)
    gain_copy.start()

    def part_a(step, buf, bit_keep):
        if step == 0:
            return buf.at[ds8(bit_keep * (half // 2), half // 2), :]
        if step == 1:
            return buf.at[ds8(bit_keep * (half // 4), half // 4), :]
        return buf.at[:, pl.ds(pl.multiple_of(bit_keep * (lanes // 2), 128), lanes // 2)]

    def part_b(step, buf, bit_keep):
        size = b_rows >> (step + 1)
        return buf.at[ds8(bit_keep * size, size), :]

    a_size = [half, half // 2, half // 4] + [half // 4] * 4
    b_size = [b_rows >> min(step, N_RED) for step in range(N_ICI + 1)]
    a_step = 24
    ici_copies = {}
    pending = []

    def flush():
        while pending:
            for copy in pending.pop(0):
                copy.start()

    for step in range(N_ICI + 1):
        for layer, k in flows:
            cur_a, cur_b = bufs_a[step].at[layer, k], bufs_b[step].at[layer, k]
            if step == 0:
                for copy in load_copies[layer, k]:
                    copy.wait()
                for copy in core_copies[layer, k]:
                    copy.wait_recv()
                old_a, old_b = acc_a.at[layer, k], acc_b.at[layer, k]
            else:
                for copy in ici_copies[layer, k, step - 1]:
                    copy.wait_recv()
                old_a, old_b = bufs_a[step - 1].at[layer, k], bufs_b[step - 1].at[layer, k]
                if step <= N_RED:
                    bit = gens[(k + step - 1) % N_ICI][1]
                    old_a, old_b = part_a(step - 1, old_a, bit), part_b(step - 1, old_b, bit)
            add_rows(cur_a, old_a, a_size[step], a_step)
            add_rows(cur_b, old_b, b_size[step], 16)
            if step < N_ICI:
                dev, bit = gens[(k + step) % N_ICI]
                src_a, src_b = cur_a, cur_b
                if step < N_RED:
                    src_a, src_b = part_a(step, cur_a, 1 - bit), part_b(step, cur_b, 1 - bit)
                copies = [
                    remote(src_a, bufs_a[step + 1].at[layer, k], ici_send.at[layer, k, step, 0], ici_recv.at[layer, k, step, 0], dev),
                    remote(src_b, bufs_b[step + 1].at[layer, k], ici_send.at[layer, k, step, 1], ici_recv.at[layer, k, step, 1], dev),
                ]
                ici_copies[layer, k, step] = copies
                flush()
                pending.append(copies)
        flush()
        gain_copy.wait()
        gain_old = gain_ref if step == 0 else gain_bufs.at[step - 1]
        gain_bufs[step, :, :] = gain_bufs[step, :, :] + gain_old[...]
        if step < N_ICI:
            gain_copy = remote(gain_bufs.at[step], gain_bufs.at[step + 1], g_send.at[step + 1], g_recv.at[step + 1], gens[step][0])
            gain_copy.start()
    gain_out = pltpu.make_async_copy(gain_bufs.at[N_ICI], out_g, g_loc)
    gain_out.start()

    def ag_region(layer, k, step):
        bits = [gens[(k + s) % N_ICI][1] for s in range(N_RED)]
        a_off = sum([bits[s] * (half >> (s + 1)) for s in range(min(step, 1) + 1)])
        b_off = sum([bits[s] * (b_rows >> (s + 1)) for s in range(step + 1)])
        a_cnt = half >> (min(step, 1) + 1)
        view_a = acc_a.at[layer, k, ds8(a_off, a_cnt), :]
        if step == 2:
            view_a = acc_a.at[layer, k, ds8(a_off, a_cnt), pl.ds(pl.multiple_of(bits[2] * (lanes // 2), 128), lanes // 2)]
        return view_a, acc_b.at[layer, k, ds8(b_off, b_rows >> (step + 1)), :]

    ag_copies = {}
    for step in reversed(range(N_RED)):
        for layer, k in flows:
            view_a, view_b = ag_region(layer, k, step)
            if step == N_RED - 1:
                last_a, last_b = bufs_a[N_ICI], bufs_b[N_ICI]
                view_a[...] = last_a[layer, k, :, :]
                view_b[...] = last_b[layer, k, :, :]
            else:
                for copy in ag_copies[layer, k, step + 1]:
                    copy.wait_recv()
            dev = gens[(k + step) % N_ICI][0]
            copies = [
                remote(view_a, view_a, ag_send.at[layer, k, step, 0], ag_recv.at[layer, k, step, 0], dev),
                remote(view_b, view_b, ag_send.at[layer, k, step, 1], ag_recv.at[layer, k, step, 1], dev),
            ]
            ag_copies[layer, k, step] = copies
            flush()
            pending.append(copies)
        flush()

    finals = []
    for layer, k in flows:
        for copy in ag_copies[layer, k, 0]:
            copy.wait_recv()
        lane = slice((k % 2) * lanes, (k % 2 + 1) * lanes)
        moves = [
            (acc_a.at[layer, k], out_a.at[layer, k // 2, ds8(core * half, half), lane]),
            (acc_b.at[layer, k, 0:o_half, :], out_o.at[layer, ds8(k * 2 * o_half + core * o_half, o_half), :]),
            (acc_b.at[layer, k, o_half:b_rows, :], out_q.at[layer, ds8(k * 2 * q_half + core * q_half, q_half), :]),
        ]
        for p, (src, dst) in enumerate(moves):
            far = remote(src, dst, fin_send.at[layer, k, p], fin_recv.at[layer, k, p], peer)
            near = pltpu.make_async_copy(src, dst, fin_loc.at[layer, k, p])
            far.start()
            near.start()
            finals.append((far, near))
    gain_out.wait()
    for copies in core_copies.values():
        for copy in copies:
            copy.wait_send()
    for copies in list(ici_copies.values()) + list(ag_copies.values()):
        for copy in copies:
            copy.wait_send()
    for far, near in finals:
        far.wait()
        near.wait()


def all_reduce(grads_low, grads_top, gains):
    a_rows, a_lanes = grads_low[0].shape
    q_rows, width = grads_low[3].shape
    o_rows = grads_low[4].shape[0]
    half, lanes = a_rows // 2, a_lanes // 2
    b_rows = (o_rows + q_rows) // 12
    shapes_a = [(half, lanes), (half // 2, lanes), (half // 4, lanes)] + [(half // 4, lanes // 2)] * 4
    shapes_b = [(b_rows >> min(step, N_RED), width) for step in range(N_ICI + 1)]
    hbm = pl.BlockSpec(memory_space=pl.ANY)
    vmem = pl.BlockSpec(memory_space=pltpu.VMEM)
    dma = pltpu.SemaphoreType.DMA
    scratch = [pltpu.VMEM((2, 6, half, lanes), F32), pltpu.VMEM((2, 6, b_rows, width), F32)]
    scratch += [pltpu.VMEM((2, 6) + shape, F32) for shape in shapes_a]
    scratch += [pltpu.VMEM((2, 6) + shape, F32) for shape in shapes_b]
    scratch += [pltpu.VMEM((N_ICI + 1,) + gains.shape, F32)]
    scratch += [dma((2, 6, 3)), dma((2, 6, 3)), dma((2, 6, 3)), dma((2, 6, N_ICI, 2)), dma((2, 6, N_ICI, 2)), dma((2, 6, N_RED, 2)), dma((2, 6, N_RED, 2)), dma((2, 6, 3)), dma((2, 6, 3)), dma((2, 6, 3)), dma((N_ICI + 1,)), dma((N_ICI + 1,)), dma]
    return pl.pallas_call(
        functools.partial(all_reduce_kernel, a_rows, a_lanes, q_rows, o_rows),
        in_specs=[hbm] * 10 + [vmem],
        out_specs=[hbm] * 4,
        out_shape=[jax.ShapeDtypeStruct((2, 3, a_rows, a_lanes), F32), jax.ShapeDtypeStruct((2, q_rows, width), F32), jax.ShapeDtypeStruct((2, o_rows, width), F32), jax.ShapeDtypeStruct(gains.shape, F32)],
        scratch_shapes=scratch,
        compiler_params=pltpu.CompilerParams(vmem_limit_bytes=60 * 1024 * 1024, collective_id=0, has_side_effects=True),
        name="all_reduce",
    )(*grads_low, *grads_top, gains)


def dot_c(lhs, rhs, c_l, c_r):
    return lax.dot_general(lhs, rhs, (((c_l,), (c_r,)), ((), ())), preferred_element_type=F32)


def norm_back_t(x_f, inv_rms, gain, d_normed):
    scaled = d_normed * gain
    d_resid = inv_rms * scaled - x_f * (inv_rms ** 3) * jnp.mean(scaled * x_f, axis=0, keepdims=True)
    d_gain = jnp.sum(d_normed * x_f * inv_rms, axis=1)
    return d_resid, d_gain


def layer_forward_t(x_t, weights, cos_t, sin_t, kv_heads, n_group, head_dim):
    g_attn, wqkv_t, w_o, g_ffn, w_gate, w_up, wd_t = weights
    x_f = x_t.astype(F32)
    inv_attn = lax.rsqrt(jnp.mean(x_f * x_f, axis=0, keepdims=True) + NORM_EPS)
    normed = (x_f * inv_attn * g_attn.astype(F32)[:, None]).astype(BF16)
    qkv_t = dot_c(wqkv_t, normed, 1, 0).astype(BF16)
    a_t, rot_t, stats = attn_forward(qkv_t, cos_t, sin_t, kv_heads, n_group, head_dim)
    m_t = (x_f + dot_c(w_o, a_t, 0, 0)).astype(BF16)
    m_f = m_t.astype(F32)
    inv_ffn = lax.rsqrt(jnp.mean(m_f * m_f, axis=0, keepdims=True) + NORM_EPS)
    normed_ffn = (m_f * inv_ffn * g_ffn.astype(F32)[:, None]).astype(BF16)
    gate_t = dot_c(w_gate, normed_ffn, 0, 0).astype(BF16)
    up_t = dot_c(w_up, normed_ffn, 0, 0).astype(BF16)
    return x_f, inv_attn, normed, qkv_t, a_t, rot_t, stats, m_f, inv_ffn, normed_ffn, gate_t, up_t


def layer_backward_t(saved, d_out_t, weights, cos_t, sin_t, kv_heads, n_group, head_dim, scale):
    g_attn, wqkv_t, w_o, g_ffn, w_gate, w_up, wd_t = weights
    x_f, inv_attn, normed, qkv_t, a_t, rot_t, stats, m_f, inv_ffn, normed_ffn, gate_t, up_t = saved
    gate_f = gate_t.astype(F32)
    gate_sig = jax.nn.sigmoid(gate_f)
    silu_act = gate_f * gate_sig
    up_f = up_t.astype(F32)
    hidden = (silu_act * up_f).astype(BF16)
    grad_wd_t = dot_c(d_out_t, hidden, 1, 1) * scale
    d_hidden = dot_c(wd_t, d_out_t, 0, 0).astype(BF16).astype(F32)
    d_gate = (d_hidden * up_f * gate_sig * (1.0 + gate_f * (1.0 - gate_sig))).astype(BF16)
    d_up = (d_hidden * silu_act).astype(BF16)
    grad_w_gate = dot_c(normed_ffn, d_gate, 1, 1) * scale
    grad_w_up = dot_c(normed_ffn, d_up, 1, 1) * scale
    d_normed_ffn = (dot_c(w_gate, d_gate, 1, 0) + dot_c(w_up, d_up, 1, 0)).astype(BF16).astype(F32)
    d_mid_norm, grad_g_ffn = norm_back_t(m_f, inv_ffn, g_ffn.astype(F32)[:, None], d_normed_ffn)
    d_mid = (d_out_t.astype(F32) + d_mid_norm).astype(BF16)
    grad_w_o = dot_c(a_t, d_mid, 1, 1) * scale
    d_attn = dot_c(w_o, d_mid, 1, 0).astype(BF16)
    dqkv_t = attn_backward(rot_t, qkv_t, d_attn, stats, cos_t, sin_t, kv_heads, n_group, head_dim)
    grad_wqkv_t = dot_c(dqkv_t, normed, 1, 1) * scale
    d_normed = dot_c(wqkv_t, dqkv_t, 0, 0).astype(BF16).astype(F32)
    d_x_norm, grad_g_attn = norm_back_t(x_f, inv_attn, g_attn.astype(F32)[:, None], d_normed)
    d_x = (d_mid.astype(F32) + d_x_norm).astype(BF16)
    return d_x, (grad_w_gate, grad_w_up, grad_wd_t, grad_wqkv_t, grad_w_o), (grad_g_attn * scale, grad_g_ffn * scale)


def solution(mesh):
    num_devices = mesh.shape["dp"]
    act_spec = P("dp", None, None)
    rep_spec = P()

    def local_step(x_layer0, x_layer1, d_out, g_attn, w_q, w_k, w_v, w_o, g_ffn, w_gate, w_up, w_down):
        _, seq_len, model_dim = x_layer0.shape
        n_heads, head_dim = w_q.shape[2], w_q.shape[3]
        kv_heads = w_k.shape[2]
        n_group = n_heads // kv_heads
        per = (n_group + 2) * head_dim
        cos_np, sin_np = rope_tables_np(seq_len, head_dim)
        cos_t, sin_t = jnp.asarray(cos_np), jnp.asarray(sin_np)
        scale = 1.0 / num_devices

        def layer_weights(layer):
            def heads_out(w):
                return jnp.transpose(w[layer], (1, 2, 0)).reshape(kv_heads, -1, model_dim)
            wqkv_t = jnp.concatenate([heads_out(w_q), heads_out(w_k), heads_out(w_v)], axis=1).reshape(-1, model_dim)
            return (g_attn[layer], wqkv_t, w_o[layer].reshape(-1, model_dim), g_ffn[layer], w_gate[layer], w_up[layer], jnp.transpose(w_down[layer], (1, 0)))

        x0_t = jnp.transpose(x_layer0[0], (1, 0))
        x1_t = jnp.transpose(x_layer1[0], (1, 0))
        d_top = jnp.transpose(d_out[0], (1, 0))
        w_low, w_top = layer_weights(0), layer_weights(1)
        saved_top = layer_forward_t(x1_t, w_top, cos_t, sin_t, kv_heads, n_group, head_dim)
        d_mid, grads_top, gains_top = layer_backward_t(saved_top, d_top, w_top, cos_t, sin_t, kv_heads, n_group, head_dim, scale)
        saved_low = layer_forward_t(x0_t, w_low, cos_t, sin_t, kv_heads, n_group, head_dim)
        d_x0, grads_low, gains_low = layer_backward_t(saved_low, d_mid, w_low, cos_t, sin_t, kv_heads, n_group, head_dim, scale)
        zero_row = jnp.zeros((model_dim,), F32)
        gains = jnp.stack(gains_low + gains_top + (zero_row,) * 4)
        sum_a, sum_q, sum_o, sum_g = all_reduce(grads_low, grads_top, gains)
        by_group = sum_q.reshape(2, kv_heads, per, model_dim)

        def heads_in(g):
            return jnp.transpose(g.reshape(2, -1, head_dim, model_dim), (0, 3, 1, 2))

        q_end, k_end = n_group * head_dim, (n_group + 1) * head_dim
        d_x = jnp.transpose(d_x0, (1, 0))[None]
        return (d_x, sum_g[0:4:2], heads_in(by_group[:, :, :q_end]), heads_in(by_group[:, :, q_end:k_end]), heads_in(by_group[:, :, k_end:]), sum_o.reshape(2, n_heads, head_dim, model_dim), sum_g[1:4:2], sum_a[:, 0], sum_a[:, 1], jnp.transpose(sum_a[:, 2], (0, 2, 1)))

    return jax.shard_map(local_step, mesh=mesh, in_specs=(act_spec, act_spec, act_spec) + (rep_spec,) * 9, out_specs=(act_spec,) + (rep_spec,) * 9, check_vma=False)
```

time: 520 us -> 379 us (0.73)
  waiting for transfers between devices: 235 us -> 0 us
  Pallas kernels: 78.5 us -> 234 us
  other arithmetic: 37.6 us -> 15.4 us
  matrix products: 104 us -> 87.7 us
  between operations: 15.3 us -> 1.84 us
  local copies, waits for them, and re-layouts: 45.4 us -> 36.4 us
    psum x1 -> x0, waiting for transfers between devices: 235 us -> none  [local_step(): lax.psum((gd, gg, gu, big_o, gq, gk, gv), 'dp')]
    pallas_call x0 -> x1, Pallas kernels: none -> 154 us  [all_reduce(): pl.pallas_call(functools.partial(all_reduce_kernel, a_rows, a_lanes, q_ro...]
    transpose x0 -> x4, local copies, waits for them, and re-layouts: none -> 18.3 us  [the longest x1 15.3 us: local_step(): jnp.transpose(sum_a[:, 2], (0, 2, 1))]
    unnamed x182 -> x135, local copies, waits for them, and re-layouts: 28.2 us -> 10.2 us
    dot_general x40 -> x28, matrix products: 104 us -> 87.7 us  [dot_c(): lax.dot_general(lhs, rhs, (((c_l,), (c_r,)), ((), ())), preferred_element...]
    another operation x7 -> x0, other arithmetic: 13.3 us -> none  [the longest x5 13.3 us: local_step(): stacked = [jnp.stack([low, top]) for low, top in zip(grads_low, grads_top)]]
    transpose x1 -> x0, other arithmetic: 6.75 us -> none  [local_step(): jnp.transpose(gd, (0, 2, 1))]
    another operation x3 -> x2, local copies, waits for them, and re-layouts: 5.88 us -> 0.64 us  [local_step(): gains = jnp.stack(gains_low + gains_top + (zero_row,) * 4)]
  transfers between devices with their start and end apart: 1 -> 0, of which waited for: 1 -> 0; matrix products, arithmetic and copies ran while one was open for 1% -> 0% of each run, Pallas kernels for 0% -> 0%
where the time goes in v2:
time: 379 us; the launch traced here: 376 us
  Pallas kernels  234 us (62%)
  matrix products  87.7 us (23%)
  local copies, waits for them, and re-layouts  36.4 us (10%)
  other arithmetic  15.4 us (4%)
    pallas_call x1, Pallas kernels, all_reduce(): pl.pallas_call(functools.partial(all_reduce_kernel, a_rows, a_lanes, q_ro...  154 us
    dot_general x28, matrix products, dot_c(): lax.dot_general(lhs, rhs, (((c_l,), (c_r,)), ((), ())), preferred_element...  87.7 us
    pallas_call x2, Pallas kernels, attn_backward(): pl.pallas_call(functools.partial(attn_bwd_kernel, n_group, head_dim, head...  50.4 us
    pallas_call x2, Pallas kernels, attn_forward(): pl.pallas_call(functools.partial(attn_fwd_kernel, n_group, head_dim, head...  30.1 us
    transpose x1, local copies, waits for them, and re-layouts, local_step(): jnp.transpose(sum_a[:, 2], (0, 2, 1))  15.3 us
    unnamed x135, local copies, waits for them, and re-layouts  10.2 us

profile of v2, /device:TPU:1, one launch (start us, length us, event | category | flops | bytes accessed | tf_op | source)
XLA Modules:
  0.0 375.5 jit_solution(12386066375344870967)
XLA Ops:
  11.9 15.3 %attn_fwd.2 = (bf16[576,1024]{1,0:T(8,128)(2,1)S(1)}, bf16[768,1024]{1,0:T(8,128)(2,1)S(1)}, f32[3,8,1024]{2,1,0:T(8,128)S(1)}) custom-call(bf16[960,1024]{1,0:T(8,128)(2,1)S(1)} %convolution_convert_fusion.7.qkv_ref.v_ref, f32[64,1024]{1,0:T(8,128)S(1)} %copy-done.3, f32[64,1024]{1,0:T(8,128)S(1)} %copy-done.2), custom_call_target="tpu_custom_call" | custom-call | flops 19327352832 | bytes 7864320 | tf_op jit(solution)/shard_map/attn_fwd/pallas_call | solution.py:142
  27.3 14.8 %attn_fwd.3 = (bf16[576,1024]{1,0:T(8,128)(2,1)S(1)}, bf16[768,1024]{1,0:T(8,128)(2,1)S(1)}, f32[3,8,1024]{2,1,0:T(8,128)S(1)}) custom-call(bf16[960,1024]{1,0:T(8,128)(2,1)S(1)} %convolution_convert_fusion.6.qkv_ref.v_ref, f32[64,1024]{1,0:T(8,128)S(1)} %copy-done.3, f32[64,1024]{1,0:T(8,128)S(1)} %copy-done.2), custom_call_target="tpu_custom_call" | custom-call | flops 19327352832 | bytes 7864320 | tf_op jit(solution)/shard_map/attn_fwd/pallas_call | solution.py:142
  45.4 4.2 %convolution_convert_fusion = bf16[1024,1536]{0,1:T(8,128)(2,1)} fusion(bf16[2,576,1536]{2,1,0:T(8,128)(2,1)S(1)} %copy-done.54, bf16[576,1024]{1,0:T(8,128)(2,1)S(1)} %get-tuple-element.45, f32[576]{0:T(1024)S(1)} %get-tuple-element.39, f32[1024]{0:T(1024)S(1)} %get-tuple-element.66), kind=kOutput, calls=%fused_computation.43 | convolution fusion | flops 1815871488 | bytes 6103040 | tf_op jit(solution)/shard_map/dot_general | solution.py:407
  49.5 4.4 %convolution_convert_fusion.1 = bf16[1024,1536]{0,1:T(8,128)(2,1)} fusion(bf16[2,576,1536]{2,1,0:T(8,128)(2,1)S(1)} %copy-done.56, bf16[576,1024]{1,0:T(8,128)(2,1)S(1)} %get-tuple-element.45, f32[576]{0:T(1024)S(1)} %get-tuple-element.39, f32[1024]{0:T(1024)S(1)} %get-tuple-element.66), kind=kOutput, calls=%fused_computation.44 | convolution fusion | flops 1815871488 | bytes 6103040 | tf_op jit(solution)/shard_map/dot_general | solution.py:407
  56.5 3.1 convolution_convert_fusion.3
  59.6 3.1 convolution_convert_fusion.4
  64.4 4.3 %multiply_bitcast_fusion.refs_7_ = f32[576,1536]{1,0:T(8,128)} fusion(bf16[1024,1536]{0,1:T(8,128)(2,1)S(1)} %convolution_convert_fusion.4, bf16[1024,1536]{0,1:T(8,128)(2,1)S(1)} %convolution_convert_fusion.3, bf16[1,1024,576]{1,2,0:T(8,128)(2,1)S(1)} %copy-done.10), kind=kOutput, calls=%fused_computation.49 | convolution fusion | flops 1825406976 | bytes 11010048 | tf_op jit(solution)/shard_map/dot_general | solution.py:407
  68.7 8.0 %fusion.3 = (bf16[1536,1024]{1,0:T(8,128)(2,1)}, bf16[1536,1024]{1,0:T(8,128)(2,1)S(1)}) fusion(bf16[1024,1536]{0,1:T(8,128)(2,1)S(1)} %convolution_convert_fusion.3, bf16[1024,1536]{0,1:T(8,128)(2,1)} %copy-done.66, bf16[1,1024,576]{1,2,0:T(8,128)(2,1)S(1)} %copy-done.10, bf16[2,1536,576]{1,2,0:T(8,128)(2,1)S(1)} %copy-done.53), kind=kOutput, calls=%fused_computation.8 | convolution fusion | flops 1838678016 | bytes 15532032 | tf_op jit(solution)/shard_map/dot_general | solution.py:407
  82.9 3.9 %convolution_multiply_fusion.refs_6_ = f32[576,1536]{1,0:T(8,128)} fusion(bf16[1536,1024]{1,0:T(8,128)(2,1)S(1)} %copy-done.63, bf16[576,1024]{1,0:T(8,128)(2,1)S(1)} %get-tuple-element.43, f32[576]{0:T(1024)S(1)} %get-tuple-element.38, f32[1024]{0:T(1024)S(1)} %get-tuple-element.70), kind=kOutput, calls=%fused_computation.67 | convolution fusion | flops 1815183360 | bytes 7870720 | tf_op jit(solution)/shard_map/dot_general | solution.py:407
  86.8 3.8 %convolution_multiply_fusion.1.refs_5_ = f32[576,1536]{1,0:T(8,128)} fusion(bf16[1536,1024]{1,0:T(8,128)(2,1)S(1)} %get-tuple-element.52, bf16[576,1024]{1,0:T(8,128)(2,1)S(1)} %get-tuple-element.43, f32[576]{0:T(1024)S(1)} %get-tuple-element.38, f32[1024]{0:T(1024)S(1)} %get-tuple-element.70), kind=kOutput, calls=%fused_computation.68 | convolution fusion | flops 1815183360 | bytes 7870720 | tf_op jit(solution)/shard_map/dot_general | solution.py:407
  94.8 25.4 %attn_bwd.2 = bf16[960,1024]{1,0:T(8,128)(2,1)S(1)} custom-call(bf16[768,1024]{1,0:T(8,128)(2,1)S(1)} %get-tuple-element.21.rot_ref, bf16[960,1024]{1,0:T(8,128)(2,1)} %copy-done.5, bf16[576,1024]{1,0:T(8,128)(2,1)S(1)} %fusion.122.do_ref, f32[3,8,1024]{2,1,0:T(8,128)S(1)} %get-tuple-element.22.st_ref, f32[64,1024]{1,0:T(8,128)S(1)} %copy-done.3, ...), custom_call_target="tpu_custom_call" | custom-call | flops 48318382080 | bytes 7864320 | tf_op jit(solution)/shard_map/attn_bwd/pallas_call | solution.py:160
  123.1 3.2 convolution_multiply_fusion.5.refs_8_
  126.3 4.2 %convolution_multiply_fusion.2.refs_2_ = f32[576,1536]{1,0:T(8,128)} fusion(bf16[576,1024]{1,0:T(8,128)(2,1)S(1)} %fusion.43, bf16[1024,1536]{0,1:T(8,128)(2,1)S(1)} %copy-done.65, bf16[1024,1536]{0,1:T(8,128)(2,1)S(1)} %copy-done.64), kind=kOutput, calls=%fused_computation.69 | convolution fusion | flops 1825406976 | bytes 11010048 | tf_op jit(solution)/shard_map/dot_general | solution.py:407
  130.5 5.5 %fusion.12 = (bf16[1536,1024]{1,0:T(8,128)(2,1)S(1)}, bf16[1536,1024]{1,0:T(8,128)(2,1)S(1)}) fusion(bf16[1024,1536]{0,1:T(8,128)(2,1)S(1)} %copy-done.64, bf16[1024,1536]{0,1:T(8,128)(2,1)S(1)} %copy-done.65, bf16[576,1024]{1,0:T(8,128)(2,1)S(1)} %fusion.43, bf16[2,1536,576]{1,2,0:T(8,128)(2,1)S(1)} %copy-done.53), kind=kOutput, calls=%fused_computation.23 | convolution fusion | flops 1838678016 | bytes 15532032 | tf_op jit(solution)/shard_map/dot_general | solution.py:407
  148.4 25.0 %attn_bwd.3 = bf16[960,1024]{1,0:T(8,128)(2,1)S(1)} custom-call(bf16[768,1024]{1,0:T(8,128)(2,1)S(1)} %get-tuple-element.24.rot_ref, bf16[960,1024]{1,0:T(8,128)(2,1)} %copy-done.4, bf16[576,1024]{1,0:T(8,128)(2,1)S(1)} %fusion.123.do_ref, f32[3,8,1024]{2,1,0:T(8,128)S(1)} %get-tuple-element.25.st_ref, f32[64,1024]{1,0:T(8,128)S(1)} %copy-done.3, ...), custom_call_target="tpu_custom_call" | custom-call | flops 48318382080 | bytes 7864320 | tf_op jit(solution)/shard_map/attn_bwd/pallas_call | solution.py:160
  173.5 2.8 fusion.77
  176.9 7.5 %fusion.126 = bf16[1,1024,576]{1,2,0:T(8,128)(2,1)} fusion(f32[1024]{0:T(1024)S(1)} %broadcast_multiply_fusion.4, f32[1024]{0:T(1024)S(1)} %copy-done.50, f32[576]{0:T(1024)S(1)} %copy-done.49, bf16[576,1024]{1,0:T(8,128)(2,1)} %get-tuple-element.76, f32[1024]{0:T(1024)S(1)} %copy-done.47, f32[1024]{0:T(1024)S(1)} %broadcast_multiply_fusion.5, ...), kind=kLoop, calls=%fused_computation.185 | loop fusion | flops 25952256 | bytes 14214144 | tf_op jit(solution)/shard_map/broadcast_in_dim | solution.py:498
  184.5 3.8 %convolution_multiply_fusion.3.refs_1_ = f32[576,1536]{1,0:T(8,128)} fusion(bf16[1536,1024]{1,0:T(8,128)(2,1)S(1)} %copy-done.62, bf16[576,1024]{1,0:T(8,128)(2,1)S(1)} %copy-done.16, f32[576]{0:T(1024)S(1)} %copy-done.38, f32[1024]{0:T(1024)S(1)} %copy-done.29), kind=kOutput, calls=%fused_computation.70 | convolution fusion | flops 1815183360 | bytes 7870720 | tf_op jit(solution)/shard_map/dot_general | solution.py:407
  188.3 3.8 %convolution_multiply_fusion.4.refs_0_ = f32[576,1536]{1,0:T(8,128)} fusion(bf16[1536,1024]{1,0:T(8,128)(2,1)S(1)} %copy-done.60, bf16[576,1024]{1,0:T(8,128)(2,1)S(1)} %copy-done.16, f32[576]{0:T(1024)S(1)} %copy-done.38, f32[1024]{0:T(1024)S(1)} %copy-done.29), kind=kOutput, calls=%fused_computation.71 | convolution fusion | flops 1815183360 | bytes 7870720 | tf_op jit(solution)/shard_map/dot_general | solution.py:407
  192.2 3.2 convolution_multiply_fusion.6.refs_3_
  195.4 153.7 %all_reduce.1 = (f32[2,3,576,1536]{3,2,1,0:T(8,128)}, f32[2,960,576]{2,1,0:T(8,128)}, f32[2,576,576]{2,1,0:T(8,128)}, f32[8,576]{1,0:T(8,128)}) custom-call(f32[576,1536]{1,0:T(8,128)} %convolution_multiply_fusion.4.refs_0_, f32[576,1536]{1,0:T(8,128)} %convolution_multiply_fusion.3.refs_1_, f32[576,1536]{1,0:T(8,128)} %convolution_multiply_fusion.2.refs_2_, ...), custom_call_target="tpu_custom_call" | custom-call | tf_op jit(solution)/shard_map/all_reduce/pallas_call | solution.py:395
  351.8 2.9 slice_bitcast_fusion.3
  354.7 3.6 slice.104
  358.3 15.3 %slice_bitcast_fusion = (f32[2,1536,576]{1,2,0:T(8,128)}, f32[2,576,1536]{2,1,0:T(8,128)}, f32[2,576,1536]{2,1,0:T(8,128)}) fusion(f32[2,3,576,1536]{3,2,1,0:T(8,128)} %get-tuple-element.29), kind=kLoop, calls=%fused_computation.2 | loop fusion | bytes 42467328 | tf_op jit(solution)/shard_map/transpose | solution.py:499
  (178 shorter events, 48.8 us)
Async XLA Ops:
  0.7 4.8 %copy-start.27 = (bf16[2,576,3,64]{1,3,2,0:T(8,128)(2,1)S(1)}, bf16[2,576,3,64]{1,3,2,0:T(8,128)(2,1)}, u32[]{:S(2)}) copy-start(bf16[2,576,3,64]{1,3,2,0:T(8,128)(2,1)} %param.20) | copy-start | bytes 1327108
  0.7 4.8 %copy-start.20 = (bf16[2,576,9,64]{1,3,2,0:T(8,128)(2,1)S(1)}, bf16[2,576,9,64]{1,3,2,0:T(8,128)(2,1)}, u32[]{:S(2)}) copy-start(bf16[2,576,9,64]{1,3,2,0:T(8,128)(2,1)} %param.18) | copy-start | bytes 3981316
  4.5 5.5 %copy-start.39 = (f32[1024]{0:T(1024)}, f32[1024]{0:T(1024)S(1)}, u32[]{:S(2)}) copy-start(f32[1024]{0:T(1024)S(1)} %get-tuple-element.79) | copy-start | bytes 12292
  5.4 44.2 %copy-start.37 = (f32[576]{0:T(1024)}, f32[576]{0:T(1024)S(1)}, u32[]{:S(2)}) copy-start(f32[576]{0:T(1024)S(1)} %get-tuple-element.39) | copy-start | bytes 6916
  5.4 85.2 %copy-start.42 = (f32[576]{0:T(1024)}, f32[576]{0:T(1024)S(1)}, u32[]{:S(2)}) copy-start(f32[576]{0:T(1024)S(1)} %get-tuple-element.38) | copy-start | bytes 6916
  7.5 34.6 %copy-start.18 = (bf16[1,9,64,576]{3,2,1,0:T(8,128)(2,1)}, bf16[1,9,64,576]{3,2,1,0:T(8,128)(2,1)S(1)}, u32[]{:S(2)}) copy-start(bf16[1,9,64,576]{3,2,1,0:T(8,128)(2,1)S(1)} %get-tuple-element.56) | copy-start | bytes 1990660
  10.1 17.2 %copy-start.4 = (bf16[960,1024]{1,0:T(8,128)(2,1)}, bf16[960,1024]{1,0:T(8,128)(2,1)S(1)}, u32[]{:S(2)}) copy-start(bf16[960,1024]{1,0:T(8,128)(2,1)S(1)} %convolution_convert_fusion.6.qkv_ref.v_ref) | copy-start | bytes 5898244
  11.9 15.3 %copy-start.5 = (bf16[960,1024]{1,0:T(8,128)(2,1)}, bf16[960,1024]{1,0:T(8,128)(2,1)S(1)}, u32[]{:S(2)}) copy-start(bf16[960,1024]{1,0:T(8,128)(2,1)S(1)} %convolution_convert_fusion.7.qkv_ref.v_ref) | copy-start | bytes 5898244
  44.7 4.8 %copy-start.14 = (bf16[576,1024]{1,0:T(8,128)(2,1)}, bf16[576,1024]{1,0:T(8,128)(2,1)S(1)}, u32[]{:S(2)}) copy-start(bf16[576,1024]{1,0:T(8,128)(2,1)S(1)} %get-tuple-element.45) | copy-start | bytes 3538948
  56.5 34.1 %copy-start.31 = (f32[1024]{0:T(1024)}, f32[1024]{0:T(1024)S(1)}, u32[]{:S(2)}) copy-start(f32[1024]{0:T(1024)S(1)} %get-tuple-element.69) | copy-start | bytes 12292
  56.5 34.1 %copy-start.33 = (f32[1024]{0:T(1024)}, f32[1024]{0:T(1024)S(1)}, u32[]{:S(2)}) copy-start(f32[1024]{0:T(1024)S(1)} %get-tuple-element.70) | copy-start | bytes 12292
  82.2 8.4 %copy-start.11 = (bf16[1024,576]{0,1:T(8,128)(2,1)}, bf16[1024,576]{0,1:T(8,128)(2,1)S(1)}, u32[]{:S(2)}) copy-start(bf16[1024,576]{0,1:T(8,128)(2,1)S(1)} %get-tuple-element.72) | copy-start | bytes 3538948
  82.9 7.7 %copy-start.35 = (f32[1024]{0:T(1024)}, f32[1024]{0:T(1024)S(1)}, u32[]{:S(2)}) copy-start(f32[1024]{0:T(1024)S(1)} %broadcast_multiply_fusion.7) | copy-start | bytes 12292
  94.7 25.5 %copy-start.25 = (bf16[3,320,576]{2,1,0:T(8,128)(2,1)S(1)}, bf16[3,320,576]{2,1,0:T(8,128)(2,1)}, u32[]{:S(2)}) copy-start(bf16[3,320,576]{2,1,0:T(8,128)(2,1)} %copy-done.24) | copy-start | bytes 3317764
  94.7 25.5 %copy-start.40 = (f32[1024]{0:T(1024)S(1)}, f32[1024]{0:T(1024)}, u32[]{:S(2)}) copy-start(f32[1024]{0:T(1024)} %copy-done.39) | copy-start | bytes 12292
  94.7 25.5 %copy-start.45 = (f32[576]{0:T(1024)S(1)}, f32[576]{0:T(1024)}, u32[]{:S(2)}) copy-start(f32[576]{0:T(1024)} %copy-done.44) | copy-start | bytes 6916
  130.5 5.6 %copy-start.55 = (bf16[2,576,1536]{2,1,0:T(8,128)(2,1)S(1)}, bf16[2,576,1536]{2,1,0:T(8,128)(2,1)}, u32[]{:S(2)}) copy-start(bf16[2,576,1536]{2,1,0:T(8,128)(2,1)} %param.23) | copy-start | bytes 10616836
  148.4 25.0 %copy-start.8 = (bf16[1,1024,576]{1,2,0:T(8,128)(2,1)S(1)}, bf16[1,1024,576]{1,2,0:T(8,128)(2,1)}, u32[]{:S(2)}) copy-start(bf16[1,1024,576]{1,2,0:T(8,128)(2,1)} %param.14) | copy-start | bytes 3538948
  148.4 25.0 %copy-start.23 = (bf16[3,320,576]{2,1,0:T(8,128)(2,1)S(1)}, bf16[3,320,576]{2,1,0:T(8,128)(2,1)}, u32[]{:S(2)}) copy-start(bf16[3,320,576]{2,1,0:T(8,128)(2,1)} %copy-done.22) | copy-start | bytes 3317764
  148.4 25.0 %copy-start.47 = (f32[1024]{0:T(1024)S(1)}, f32[1024]{0:T(1024)}, u32[]{:S(2)}) copy-start(f32[1024]{0:T(1024)} %copy-done.46) | copy-start | bytes 12292
  148.4 25.0 %copy-start.49 = (f32[576]{0:T(1024)S(1)}, f32[576]{0:T(1024)}, u32[]{:S(2)}) copy-start(f32[576]{0:T(1024)} %copy-done.48) | copy-start | bytes 6916
  176.9 7.5 %copy-start.16 = (bf16[576,1024]{1,0:T(8,128)(2,1)S(1)}, bf16[576,1024]{1,0:T(8,128)(2,1)}, u32[]{:S(2)}) copy-start(bf16[576,1024]{1,0:T(8,128)(2,1)} %copy-done.14) | copy-start | bytes 3538948
  176.9 7.5 %copy-start.62 = (bf16[1536,1024]{1,0:T(8,128)(2,1)S(1)}, bf16[1536,1024]{1,0:T(8,128)(2,1)}, u32[]{:S(2)}) copy-start(bf16[1536,1024]{1,0:T(8,128)(2,1)} %copy-done.61) | copy-start | bytes 9437188
  358.3 15.3 %copy-start.17 = (f32[2,576,576]{2,1,0:T(8,128)S(1)}, f32[2,576,576]{2,1,0:T(8,128)}, u32[]{:S(2)}) copy-start(f32[2,576,576]{2,1,0:T(8,128)} %get-tuple-element.28) | copy-start | bytes 7962628
  (43 other events, 127.6 us)

commit v3 on v2

v3 whole, which is shorter than its diff:
```python
import functools

import jax
import jax.numpy as jnp
import numpy as np
from jax import lax
from jax.experimental import pallas as pl
from jax.experimental.pallas import tpu as pltpu
from jax.sharding import PartitionSpec as P

NORM_EPS = 1e-6
ROPE_THETA = 10000.0
BLK = 256
LOG2E = 1.4426950408889634
F32 = jnp.float32
BF16 = jnp.bfloat16


def rope_tables_np(seq_len, head_dim):
    positions = np.arange(seq_len, dtype=np.float32)
    inv_freq = np.float32(ROPE_THETA) ** (-np.arange(0, head_dim, 2, dtype=np.float32) / np.float32(head_dim))
    angles = (positions[None, :] * inv_freq.astype(np.float32)[:, None]).astype(np.float32)
    cos_t = np.repeat(np.cos(angles), 2, axis=0).astype(np.float32)
    sin_t = np.repeat(np.sin(angles), 2, axis=0).astype(np.float32)
    sin_t[0::2] *= -1.0
    return cos_t, sin_t


def pair_swap(values):
    rows = values.shape[0]
    even = lax.broadcasted_iota(jnp.int32, values.shape, 0) % 2 == 0
    return jnp.where(even, pltpu.roll(values, rows - 1, 0), pltpu.roll(values, 1, 0))


def dot_nn(lhs, rhs):
    return lax.dot_general(lhs, rhs, (((1,), (0,)), ((), ())), preferred_element_type=F32)


def dot_nt(lhs, rhs):
    return lax.dot_general(lhs, rhs, (((1,), (1,)), ((), ())), preferred_element_type=F32)


def diag_mask():
    keys = lax.broadcasted_iota(jnp.int32, (BLK, BLK), 0)
    queries = lax.broadcasted_iota(jnp.int32, (BLK, BLK), 1)
    return queries >= keys


def dot_tn(lhs, rhs):
    return lax.dot_general(lhs, rhs, (((0,), (0,)), ((), ())), preferred_element_type=F32)


def ds_of(start, size, align):
    return pl.ds(pl.multiple_of(start, align), size)


def attn_fwd_kernel(att_scale, q_ref, k_ref, v_ref, cos_ref, sin_ref, a_ref, qr_ref, kr_ref, st_ref, k_scr):
    seq_len = q_ref.shape[1]
    n_blk = seq_len // BLK
    cos_t = cos_ref[...]
    sin_t = sin_ref[...]

    @pl.when(pl.program_id(1) == 0)
    def _():
        k_f = k_ref[...].astype(F32)
        k_rot = (k_f * cos_t + pair_swap(k_f) * sin_t).astype(BF16)
        kr_ref[...] = k_rot
        k_scr[...] = k_rot.astype(F32).T.astype(BF16)

    coef = att_scale * LOG2E
    mask = diag_mask()
    q_f = q_ref[...].astype(F32)
    qr_ref[...] = (q_f * cos_t + pair_swap(q_f) * sin_t).astype(BF16)
    st_ref[...] = jnp.zeros_like(st_ref)
    for j in range(n_blk):
        cols = slice(j * BLK, (j + 1) * BLK)
        q_j = qr_ref[:, cols]
        s_blocks = []
        for i in range(j + 1):
            s_i = dot_nn(k_scr[i * BLK:(i + 1) * BLK, :], q_j)
            if i == j:
                s_i = jnp.where(mask, s_i, -1e30)
            s_blocks.append(s_i)
        top = functools.reduce(jnp.maximum, [jnp.max(s_i, axis=0, keepdims=True) for s_i in s_blocks])
        e_blocks = [jnp.exp2((s_i - top) * coef) for s_i in s_blocks]
        total = functools.reduce(jnp.add, [jnp.sum(e_i, axis=0, keepdims=True) for e_i in e_blocks])
        inv = 1.0 / total
        acc = None
        for i in range(j + 1):
            p_i = (e_blocks[i] * inv).astype(BF16)
            part = dot_nn(v_ref[:, i * BLK:(i + 1) * BLK], p_i)
            acc = part if acc is None else acc + part
        a_ref[:, cols] = acc.astype(BF16)
        st_ref[0, 0:1, cols] = top
        st_ref[0, 1:2, cols] = inv


def norm_back_cols(x_f, inv, gain, d_normed):
    scaled = d_normed * gain
    d_resid = inv * scaled - x_f * (inv * inv * inv) * jnp.mean(scaled * x_f, axis=0, keepdims=True)
    return d_resid, d_normed * x_f * inv


def fold_lanes(values):
    return functools.reduce(jnp.add, [values[:, i:i + 128] for i in range(0, values.shape[1], 128)])


def attn_bwd_kernel(att_scale, scale, kv_heads, n_group, qr_ref, kr_ref, v_ref, do_ref, st_ref, cos_ref, sin_ref, x_ref, dmid_ref, gain_ref, w_ref, dx_ref, gw_ref, gg_ref, k_scr, v_scr, dk_acc, dv_acc, dqkv, gacc):
    head_dim, seq_len = qr_ref.shape
    n_blk = seq_len // BLK
    g, h = pl.program_id(0), pl.program_id(1)
    base = g * ((n_group + 2) * head_dim)

    @pl.when(h == 0)
    def _():
        k_scr[...] = kr_ref[...].astype(F32).T.astype(BF16)
        v_scr[...] = v_ref[...].astype(F32).T.astype(BF16)
        dk_acc[...] = jnp.zeros_like(dk_acc)
        dv_acc[...] = jnp.zeros_like(dv_acc)

    coef = att_scale * LOG2E
    mask = diag_mask()
    for j in range(n_blk):
        cols = slice(j * BLK, (j + 1) * BLK)
        q_j = qr_ref[:, cols]
        do_j = do_ref[:, cols]
        top = st_ref[0, 0:1, cols]
        inv = st_ref[0, 1:2, cols]
        p_blocks = []
        dp_blocks = []
        row_dot = None
        for i in range(j + 1):
            keys = slice(i * BLK, (i + 1) * BLK)
            s_i = dot_nn(k_scr[keys, :], q_j)
            if i == j:
                s_i = jnp.where(mask, s_i, -1e30)
            p_i = jnp.exp2((s_i - top) * coef) * inv
            dp_i = dot_nn(v_scr[keys, :], do_j).astype(BF16).astype(F32)
            part = jnp.sum(p_i * dp_i, axis=0, keepdims=True)
            row_dot = part if row_dot is None else row_dot + part
            dv_acc[:, keys] += dot_nt(do_j, p_i.astype(BF16))
            p_blocks.append(p_i)
            dp_blocks.append(dp_i)
        dq_j = None
        for i in range(j + 1):
            keys = slice(i * BLK, (i + 1) * BLK)
            ds_i = (p_blocks[i] * (dp_blocks[i] - row_dot) * att_scale).astype(BF16)
            part = dot_nn(kr_ref[:, keys], ds_i)
            dq_j = part if dq_j is None else dq_j + part
            dk_acc[:, keys] += dot_nt(q_j, ds_i)
        dq_j = dq_j.astype(BF16).astype(F32)
        dqkv[ds_of(base + h * head_dim, head_dim, head_dim), cols] = (dq_j * cos_ref[:, cols] - pair_swap(dq_j) * sin_ref[:, cols]).astype(BF16)

    @pl.when(h == n_group - 1)
    def _():
        d_k = dk_acc[...].astype(BF16).astype(F32)
        dqkv[ds_of(base + n_group * head_dim, head_dim, head_dim), :] = (d_k * cos_ref[...] - pair_swap(d_k) * sin_ref[...]).astype(BF16)
        dqkv[ds_of(base + (n_group + 1) * head_dim, head_dim, head_dim), :] = dv_acc[...].astype(BF16)

    @pl.when((g == kv_heads - 1) & (h == n_group - 1))
    def _():
        gacc[...] = jnp.zeros_like(gacc)
        gw_ref[...] = jnp.zeros_like(gw_ref)
        gain = gain_ref[...]

        @pl.loop(0, n_blk)
        def _(j):
            cols = ds_of(j * BLK, BLK, BLK)
            x_f = x_ref[:, cols].astype(F32)
            inv = lax.rsqrt(jnp.mean(x_f * x_f, axis=0, keepdims=True) + NORM_EPS)
            normed = (x_f * inv * gain).astype(BF16)
            gw_ref[...] += dot_nt(dqkv[:, cols], normed)
            d_normed = dot_tn(w_ref[...], dqkv[:, cols]).astype(BF16).astype(F32)
            d_resid, d_gain = norm_back_cols(x_f, inv, gain, d_normed)
            gacc[...] += fold_lanes(d_gain)
            dx_ref[:, cols] = (dmid_ref[:, cols].astype(F32) + d_resid).astype(BF16)

        gw_ref[...] = gw_ref[...] * scale
        gg_ref[...] = jnp.sum(gacc[...], axis=1, keepdims=True) * scale


def ffn_kernel(scale, x_ref, a_ref, dout_ref, wo_ref, gain_ref, wg_ref, wu_ref, wd_ref, dmid_ref, dattn_ref, gwo_ref, gg_ref, gwg_ref, gwu_ref, gwd_ref, m_scr, n_scr, inv_scr, acc, hid, dg, du, gacc):
    model_dim, seq_len = x_ref.shape
    n_blk = seq_len // BLK
    step = pl.program_id(0)
    gain = gain_ref[...]

    @pl.when(step == 0)
    def _():
        @pl.loop(0, n_blk)
        def _(j):
            cols = ds_of(j * BLK, BLK, BLK)
            m_b = (x_ref[:, cols].astype(F32) + dot_tn(wo_ref[...], a_ref[:, cols])).astype(BF16)
            m_scr[:, cols] = m_b
            m_f = m_b.astype(F32)
            inv = lax.rsqrt(jnp.mean(m_f * m_f, axis=0, keepdims=True) + NORM_EPS)
            inv_scr[0:1, cols] = inv
            n_scr[:, cols] = (m_f * inv * gain).astype(BF16)
        acc[...] = jnp.zeros_like(acc)
        gacc[...] = jnp.zeros_like(gacc)

    w_g = wg_ref[...]
    w_u = wu_ref[...]
    for j in range(n_blk):
        cols = slice(j * BLK, (j + 1) * BLK)
        gate_f = dot_tn(w_g, n_scr[:, cols]).astype(BF16).astype(F32)
        up_f = dot_tn(w_u, n_scr[:, cols]).astype(BF16).astype(F32)
        d_hidden = dot_tn(wd_ref[...], dout_ref[:, cols]).astype(BF16).astype(F32)
        gate_sig = jax.nn.sigmoid(gate_f)
        silu_act = gate_f * gate_sig
        hid[:, cols] = (silu_act * up_f).astype(BF16)
        dg[:, cols] = (d_hidden * up_f * gate_sig * (1.0 + gate_f * (1.0 - gate_sig))).astype(BF16)
        du[:, cols] = (d_hidden * silu_act).astype(BF16)
        acc[:, cols] += dot_nn(w_g, dg[:, cols]) + dot_nn(w_u, du[:, cols])
    gwg_ref[...] = dot_nt(n_scr[...], dg[...]) * scale
    gwu_ref[...] = dot_nt(n_scr[...], du[...]) * scale
    gwd_ref[...] = dot_nt(dout_ref[...], hid[...]) * scale

    @pl.when(step == pl.num_programs(0) - 1)
    def _():
        gwo_ref[...] = jnp.zeros_like(gwo_ref)

        @pl.loop(0, n_blk)
        def _(j):
            cols = ds_of(j * BLK, BLK, BLK)
            d_normed = acc[:, cols].astype(BF16).astype(F32)
            d_resid, d_gain = norm_back_cols(m_scr[:, cols].astype(F32), inv_scr[0:1, cols], gain, d_normed)
            gacc[...] += fold_lanes(d_gain)
            d_mid = (dout_ref[:, cols].astype(F32) + d_resid).astype(BF16)
            dmid_ref[:, cols] = d_mid
            dattn_ref[:, cols] = dot_nn(wo_ref[...], d_mid).astype(BF16)
            gwo_ref[...] += dot_nt(a_ref[:, cols], d_mid)

        gwo_ref[...] = gwo_ref[...] * scale
        gg_ref[...] = jnp.sum(gacc[...], axis=1, keepdims=True) * scale


def whole(shape):
    return pl.BlockSpec(shape, lambda *_: (0,) * len(shape))


def attn_forward(qkv_t, cos_t, sin_t, kv_heads, n_group, head_dim):
    seq_len = qkv_t.shape[1]
    per = n_group + 2
    block = (head_dim, seq_len)
    flops = 2 * 2 * kv_heads * n_group * head_dim * seq_len * seq_len
    return pl.pallas_call(
        functools.partial(attn_fwd_kernel, head_dim ** -0.5),
        grid=(kv_heads, n_group),
        in_specs=[pl.BlockSpec(block, lambda g, h: (g * per + h, 0)), pl.BlockSpec(block, lambda g, h: (g * per + n_group, 0)), pl.BlockSpec(block, lambda g, h: (g * per + n_group + 1, 0)), whole(block), whole(block)],
        out_specs=[pl.BlockSpec(block, lambda g, h: (g * n_group + h, 0)), pl.BlockSpec(block, lambda g, h: (g * n_group + h, 0)), pl.BlockSpec(block, lambda g, h: (g, 0)), pl.BlockSpec((1, 8, seq_len), lambda g, h: (g * n_group + h, 0, 0))],
        out_shape=[jax.ShapeDtypeStruct((kv_heads * n_group * head_dim, seq_len), BF16), jax.ShapeDtypeStruct((kv_heads * n_group * head_dim, seq_len), BF16), jax.ShapeDtypeStruct((kv_heads * head_dim, seq_len), BF16), jax.ShapeDtypeStruct((kv_heads * n_group, 8, seq_len), F32)],
        scratch_shapes=[pltpu.VMEM((seq_len, head_dim), BF16)],
        compiler_params=pltpu.CompilerParams(vmem_limit_bytes=40 * 1024 * 1024),
        cost_estimate=pl.CostEstimate(flops=8 * flops, bytes_accessed=8 * qkv_t.size, transcendentals=0),
        name="attn_fwd",
    )(qkv_t, qkv_t, qkv_t, cos_t, sin_t)


def attn_backward(qr_t, kr_t, qkv_t, do_t, stats, cos_t, sin_t, x_t, d_mid, gain, wqkv_t, scale, kv_heads, n_group, head_dim):
    model_dim, seq_len = x_t.shape
    per = n_group + 2
    block = (head_dim, seq_len)
    flops = 5 * 2 * kv_heads * n_group * head_dim * seq_len * seq_len
    return pl.pallas_call(
        functools.partial(attn_bwd_kernel, head_dim ** -0.5, scale, kv_heads, n_group),
        grid=(kv_heads, n_group),
        in_specs=[
            pl.BlockSpec(block, lambda g, h: (g * n_group + h, 0)),
            pl.BlockSpec(block, lambda g, h: (g, 0)),
            pl.BlockSpec(block, lambda g, h: (g * per + n_group + 1, 0)),
            pl.BlockSpec(block, lambda g, h: (g * n_group + h, 0)),
            pl.BlockSpec((1, 8, seq_len), lambda g, h: (g * n_group + h, 0, 0)),
            whole(block),
            whole(block),
            whole(x_t.shape),
            whole(x_t.shape),
            whole((model_dim, 1)),
            whole(wqkv_t.shape),
        ],
        out_specs=[whole(x_t.shape), whole(wqkv_t.shape), whole((model_dim, 1))],
        out_shape=[jax.ShapeDtypeStruct(x_t.shape, BF16), jax.ShapeDtypeStruct(wqkv_t.shape, F32), jax.ShapeDtypeStruct((model_dim, 1), F32)],
        scratch_shapes=[pltpu.VMEM((seq_len, head_dim), BF16), pltpu.VMEM((seq_len, head_dim), BF16), pltpu.VMEM(block, F32), pltpu.VMEM(block, F32), pltpu.VMEM(qkv_t.shape, BF16), pltpu.VMEM((model_dim, 128), F32)],
        compiler_params=pltpu.CompilerParams(vmem_limit_bytes=50 * 1024 * 1024),
        cost_estimate=pl.CostEstimate(flops=8 * flops, bytes_accessed=8 * qkv_t.size, transcendentals=0),
        name="attn_bwd",
    )(qr_t, kr_t, qkv_t, do_t, stats, cos_t, sin_t, x_t, d_mid, gain, wqkv_t)


def ffn(x_t, a_t, d_out_t, w_o, gain, w_gate, w_up, wd_t, scale):
    model_dim, seq_len = x_t.shape
    ff_dim = w_gate.shape[1]
    w_spec = pl.BlockSpec((model_dim, BLK), lambda f: (0, f))
    act = jax.ShapeDtypeStruct(x_t.shape, BF16)
    grad = jax.ShapeDtypeStruct(w_gate.shape, F32)
    return pl.pallas_call(
        functools.partial(ffn_kernel, scale),
        grid=(ff_dim // BLK,),
        in_specs=[whole(x_t.shape), whole(a_t.shape), whole(x_t.shape), whole(w_o.shape), whole((model_dim, 1)), w_spec, w_spec, w_spec],
        out_specs=[whole(x_t.shape), whole(a_t.shape), whole(w_o.shape), whole((model_dim, 1)), w_spec, w_spec, w_spec],
        out_shape=[act, jax.ShapeDtypeStruct(a_t.shape, BF16), jax.ShapeDtypeStruct(w_o.shape, F32), jax.ShapeDtypeStruct((model_dim, 1), F32), grad, grad, grad],
        scratch_shapes=[pltpu.VMEM(x_t.shape, BF16), pltpu.VMEM(x_t.shape, BF16), pltpu.VMEM((8, seq_len), F32), pltpu.VMEM(x_t.shape, F32), pltpu.VMEM((BLK, seq_len), BF16), pltpu.VMEM((BLK, seq_len), BF16), pltpu.VMEM((BLK, seq_len), BF16), pltpu.VMEM((model_dim, 128), F32)],
        compiler_params=pltpu.CompilerParams(vmem_limit_bytes=55 * 1024 * 1024),
        cost_estimate=pl.CostEstimate(flops=18 * x_t.size * ff_dim, bytes_accessed=20 * w_gate.size, transcendentals=0),
        name="ffn",
    )(x_t, a_t, d_out_t, w_o, gain, w_gate, w_up, wd_t)


MESH = pl.DeviceIdType.MESH
N_RED = 3
N_ICI = 6


def add_rows(dst, src, rows, step):
    @pl.loop(0, rows // step)
    def _(i):
        part = pl.ds(pl.multiple_of(i * step, 8), step)
        dst[part, :] = dst[part, :] + src[part, :]


def all_reduce_kernel(a_rows, a_lanes, q_rows, o_rows, *refs):
    srcs = [refs[5 * layer:5 * layer + 5] for layer in range(2)]
    gain_ref = refs[10]
    outs_a = refs[11:14]
    out_q, out_o, out_g = refs[14:17]
    acc_a, acc_b = refs[17:19]
    bufs_a = refs[19:26]
    bufs_b = refs[26:33]
    gain_bufs = refs[33]
    (core_send, core_recv, load_sem, ici_send, ici_recv, ag_send, ag_recv, fin_send, fin_recv, fin_loc, g_send, g_recv, g_loc) = refs[34:47]

    me = lax.axis_index("dp")
    core = lax.rem(me, 2)
    coords = (lax.rem(me // 2, 4), lax.rem(me // 8, 4), me // 32)
    strides = (2, 8, 32)
    peer = me + 1 - 2 * core
    gens = []
    for kind in range(2):
        for axis in range(3):
            v = coords[axis]
            if kind == 0:
                partner, bit = v + 1 - 2 * lax.rem(v, 2), lax.rem(v + v // 2, 2)
            else:
                partner, bit = 3 - v, v // 2
            gens.append((me + (partner - v) * strides[axis], bit))

    barrier = pltpu.get_barrier_semaphore()
    for dev in [peer] + [g[0] for g in gens]:
        pl.semaphore_signal(barrier, inc=1, device_id=(dev,), device_id_type=MESH)
    pl.semaphore_wait(barrier, 1 + N_ICI)

    half = a_rows // 2
    lanes = a_lanes // 2
    o_half = o_rows // 12
    q_half = q_rows // 12
    b_rows = o_half + q_half

    def ds8(start, size):
        return pl.ds(pl.multiple_of(start, 8), size)

    def remote(src, dst, send, recv, dev):
        return pltpu.make_async_remote_copy(src_ref=src, dst_ref=dst, send_sem=send, recv_sem=recv, device_id=(dev,), device_id_type=MESH)

    flows = [(layer, k) for layer in (1, 0) for k in range(6)]
    core_copies = {}
    load_copies = {}
    for layer, k in flows:
        mat = srcs[layer][k // 2]
        q_src, o_src = srcs[layer][3:]
        lane = slice((k % 2) * lanes, (k % 2 + 1) * lanes)

        def parts(which):
            return (
                (mat.at[ds8(which * half, half), lane], lambda buf_a, buf_b: buf_a.at[layer, k]),
                (o_src.at[ds8(k * 2 * o_half + which * o_half, o_half), :], lambda buf_a, buf_b: buf_b.at[layer, k, 0:o_half, :]),
                (q_src.at[ds8(k * 2 * q_half + which * q_half, q_half), :], lambda buf_a, buf_b: buf_b.at[layer, k, o_half:b_rows, :]),
            )

        sends = [remote(src, dst(bufs_a[0], bufs_b[0]), core_send.at[layer, k, p], core_recv.at[layer, k, p], peer) for p, (src, dst) in enumerate(parts(1 - core))]
        loads = [pltpu.make_async_copy(src, dst(acc_a, acc_b), load_sem.at[layer, k, p]) for p, (src, dst) in enumerate(parts(core))]
        for copy in sends + loads:
            copy.start()
        core_copies[layer, k] = sends
        load_copies[layer, k] = loads
    gain_copy = remote(gain_ref, gain_bufs.at[0], g_send.at[0], g_recv.at[0], peer)
    gain_copy.start()

    def part_a(step, buf, bit_keep):
        if step == 0:
            return buf.at[ds8(bit_keep * (half // 2), half // 2), :]
        if step == 1:
            return buf.at[ds8(bit_keep * (half // 4), half // 4), :]
        return buf.at[:, pl.ds(pl.multiple_of(bit_keep * (lanes // 2), 128), lanes // 2)]

    def part_b(step, buf, bit_keep):
        size = b_rows >> (step + 1)
        return buf.at[ds8(bit_keep * size, size), :]

    a_size = [half, half // 2, half // 4] + [half // 4] * 4
    b_size = [b_rows >> min(step, N_RED) for step in range(N_ICI + 1)]
    a_step = 24
    ici_copies = {}
    pending = []

    def flush():
        while pending:
            for copy in pending.pop(0):
                copy.start()

    for step in range(N_ICI + 1):
        for layer, k in flows:
            cur_a, cur_b = bufs_a[step].at[layer, k], bufs_b[step].at[layer, k]
            if step == 0:
                for copy in load_copies[layer, k]:
                    copy.wait()
                for copy in core_copies[layer, k]:
                    copy.wait_recv()
                old_a, old_b = acc_a.at[layer, k], acc_b.at[layer, k]
            else:
                for copy in ici_copies[layer, k, step - 1]:
                    copy.wait_recv()
                old_a, old_b = bufs_a[step - 1].at[layer, k], bufs_b[step - 1].at[layer, k]
                if step <= N_RED:
                    bit = gens[(k + step - 1) % N_ICI][1]
                    old_a, old_b = part_a(step - 1, old_a, bit), part_b(step - 1, old_b, bit)
            add_rows(cur_a, old_a, a_size[step], a_step)
            add_rows(cur_b, old_b, b_size[step], 16)
            if step < N_ICI:
                dev, bit = gens[(k + step) % N_ICI]
                src_a, src_b = cur_a, cur_b
                if step < N_RED:
                    src_a, src_b = part_a(step, cur_a, 1 - bit), part_b(step, cur_b, 1 - bit)
                copies = [
                    remote(src_a, bufs_a[step + 1].at[layer, k], ici_send.at[layer, k, step, 0], ici_recv.at[layer, k, step, 0], dev),
                    remote(src_b, bufs_b[step + 1].at[layer, k], ici_send.at[layer, k, step, 1], ici_recv.at[layer, k, step, 1], dev),
                ]
                ici_copies[layer, k, step] = copies
                flush()
                pending.append(copies)
        flush()
        gain_copy.wait()
        gain_old = gain_ref if step == 0 else gain_bufs.at[step - 1]
        gain_bufs[step, :, :] = gain_bufs[step, :, :] + gain_old[...]
        if step < N_ICI:
            gain_copy = remote(gain_bufs.at[step], gain_bufs.at[step + 1], g_send.at[step + 1], g_recv.at[step + 1], gens[step][0])
            gain_copy.start()
    gain_out = pltpu.make_async_copy(gain_bufs.at[N_ICI], out_g, g_loc)
    gain_out.start()

    def ag_region(layer, k, step):
        bits = [gens[(k + s) % N_ICI][1] for s in range(N_RED)]
        a_off = sum([bits[s] * (half >> (s + 1)) for s in range(min(step, 1) + 1)])
        b_off = sum([bits[s] * (b_rows >> (s + 1)) for s in range(step + 1)])
        a_cnt = half >> (min(step, 1) + 1)
        view_a = acc_a.at[layer, k, ds8(a_off, a_cnt), :]
        if step == 2:
            view_a = acc_a.at[layer, k, ds8(a_off, a_cnt), pl.ds(pl.multiple_of(bits[2] * (lanes // 2), 128), lanes // 2)]
        return view_a, acc_b.at[layer, k, ds8(b_off, b_rows >> (step + 1)), :]

    ag_copies = {}
    for step in reversed(range(N_RED)):
        for layer, k in flows:
            view_a, view_b = ag_region(layer, k, step)
            if step == N_RED - 1:
                last_a, last_b = bufs_a[N_ICI], bufs_b[N_ICI]
                view_a[...] = last_a[layer, k, :, :]
                view_b[...] = last_b[layer, k, :, :]
            else:
                for copy in ag_copies[layer, k, step + 1]:
                    copy.wait_recv()
            dev = gens[(k + step) % N_ICI][0]
            copies = [
                remote(view_a, view_a, ag_send.at[layer, k, step, 0], ag_recv.at[layer, k, step, 0], dev),
                remote(view_b, view_b, ag_send.at[layer, k, step, 1], ag_recv.at[layer, k, step, 1], dev),
            ]
            ag_copies[layer, k, step] = copies
            flush()
            pending.append(copies)
        flush()

    finals = []
    for layer, k in flows:
        for copy in ag_copies[layer, k, 0]:
            copy.wait_recv()
        lane = slice((k % 2) * lanes, (k % 2 + 1) * lanes)
        moves = [
            (acc_a.at[layer, k], outs_a[k // 2].at[layer, ds8(core * half, half), lane]),
            (acc_b.at[layer, k, 0:o_half, :], out_o.at[layer, ds8(k * 2 * o_half + core * o_half, o_half), :]),
            (acc_b.at[layer, k, o_half:b_rows, :], out_q.at[layer, ds8(k * 2 * q_half + core * q_half, q_half), :]),
        ]
        for p, (src, dst) in enumerate(moves):
            far = remote(src, dst, fin_send.at[layer, k, p], fin_recv.at[layer, k, p], peer)
            near = pltpu.make_async_copy(src, dst, fin_loc.at[layer, k, p])
            far.start()
            near.start()
            finals.append((far, near))
    gain_out.wait()
    for copies in core_copies.values():
        for copy in copies:
            copy.wait_send()
    for copies in list(ici_copies.values()) + list(ag_copies.values()):
        for copy in copies:
            copy.wait_send()
    for far, near in finals:
        far.wait()
        near.wait()


def all_reduce(grads_low, grads_top, gains):
    a_rows, a_lanes = grads_low[0].shape
    q_rows, width = grads_low[3].shape
    o_rows = grads_low[4].shape[0]
    half, lanes = a_rows // 2, a_lanes // 2
    b_rows = (o_rows + q_rows) // 12
    shapes_a = [(half, lanes), (half // 2, lanes), (half // 4, lanes)] + [(half // 4, lanes // 2)] * 4
    shapes_b = [(b_rows >> min(step, N_RED), width) for step in range(N_ICI + 1)]
    hbm = pl.BlockSpec(memory_space=pl.ANY)
    vmem = pl.BlockSpec(memory_space=pltpu.VMEM)
    dma = pltpu.SemaphoreType.DMA
    scratch = [pltpu.VMEM((2, 6, half, lanes), F32), pltpu.VMEM((2, 6, b_rows, width), F32)]
    scratch += [pltpu.VMEM((2, 6) + shape, F32) for shape in shapes_a]
    scratch += [pltpu.VMEM((2, 6) + shape, F32) for shape in shapes_b]
    scratch += [pltpu.VMEM((N_ICI + 1,) + gains.shape, F32)]
    scratch += [dma((2, 6, 3)), dma((2, 6, 3)), dma((2, 6, 3)), dma((2, 6, N_ICI, 2)), dma((2, 6, N_ICI, 2)), dma((2, 6, N_RED, 2)), dma((2, 6, N_RED, 2)), dma((2, 6, 3)), dma((2, 6, 3)), dma((2, 6, 3)), dma((N_ICI + 1,)), dma((N_ICI + 1,)), dma]
    return pl.pallas_call(
        functools.partial(all_reduce_kernel, a_rows, a_lanes, q_rows, o_rows),
        in_specs=[hbm] * 10 + [vmem],
        out_specs=[hbm] * 6,
        out_shape=[jax.ShapeDtypeStruct((2, a_rows, a_lanes), F32)] * 3 + [jax.ShapeDtypeStruct((2, q_rows, width), F32), jax.ShapeDtypeStruct((2, o_rows, width), F32), jax.ShapeDtypeStruct(gains.shape, F32)],
        scratch_shapes=scratch,
        compiler_params=pltpu.CompilerParams(vmem_limit_bytes=60 * 1024 * 1024, collective_id=0, has_side_effects=True),
        name="all_reduce",
    )(*grads_low, *grads_top, gains)


def layer_qkv(x_t, weights):
    x_f = x_t.astype(F32)
    inv_attn = lax.rsqrt(jnp.mean(x_f * x_f, axis=0, keepdims=True) + NORM_EPS)
    normed = (x_f * inv_attn * weights[0]).astype(BF16)
    return lax.dot_general(weights[1], normed, (((1,), (0,)), ((), ())), preferred_element_type=F32).astype(BF16)


def layer_backward(x_t, d_out_t, weights, cos_t, sin_t, scale, dims):
    g_attn, wqkv_t, w_o, g_ffn, w_gate, w_up, wd_t = weights
    qkv_t = layer_qkv(x_t, weights)
    a_t, qr_t, kr_t, stats = attn_forward(qkv_t, cos_t, sin_t, *dims)
    d_mid, d_attn, grad_w_o, grad_g_ffn, grad_w_gate, grad_w_up, grad_wd_t = ffn(x_t, a_t, d_out_t, w_o, g_ffn, w_gate, w_up, wd_t, scale)
    d_x, grad_wqkv_t, grad_g_attn = attn_backward(qr_t, kr_t, qkv_t, d_attn, stats, cos_t, sin_t, x_t, d_mid, g_attn, wqkv_t, scale, *dims)
    return d_x, (grad_w_gate, grad_w_up, grad_wd_t, grad_wqkv_t, grad_w_o), (grad_g_attn[:, 0], grad_g_ffn[:, 0])


def solution(mesh):
    num_devices = mesh.shape["dp"]
    act_spec = P("dp", None, None)
    rep_spec = P()

    def local_step(x_layer0, x_layer1, d_out, g_attn, w_q, w_k, w_v, w_o, g_ffn, w_gate, w_up, w_down):
        _, seq_len, model_dim = x_layer0.shape
        n_heads, head_dim = w_q.shape[2], w_q.shape[3]
        kv_heads = w_k.shape[2]
        n_group = n_heads // kv_heads
        per = (n_group + 2) * head_dim
        cos_np, sin_np = rope_tables_np(seq_len, head_dim)
        cos_t, sin_t = jnp.asarray(cos_np), jnp.asarray(sin_np)
        scale = 1.0 / num_devices

        def layer_weights(layer):
            def heads_out(w):
                return jnp.transpose(w[layer], (1, 2, 0)).reshape(kv_heads, -1, model_dim)
            wqkv_t = jnp.concatenate([heads_out(w_q), heads_out(w_k), heads_out(w_v)], axis=1).reshape(-1, model_dim)
            return (g_attn[layer].astype(F32)[:, None], wqkv_t, w_o[layer].reshape(-1, model_dim), g_ffn[layer].astype(F32)[:, None], w_gate[layer], w_up[layer], jnp.transpose(w_down[layer], (1, 0)))

        x0_t = jnp.transpose(x_layer0[0], (1, 0))
        x1_t = jnp.transpose(x_layer1[0], (1, 0))
        d_top = jnp.transpose(d_out[0], (1, 0))
        w_low, w_top = layer_weights(0), layer_weights(1)
        dims = (kv_heads, n_group, head_dim)
        d_mid, grads_top, gains_top = layer_backward(x1_t, d_top, w_top, cos_t, sin_t, scale, dims)
        d_x0, grads_low, gains_low = layer_backward(x0_t, d_mid, w_low, cos_t, sin_t, scale, dims)
        zero_row = jnp.zeros((model_dim,), F32)
        gains = jnp.stack(gains_low + gains_top + (zero_row,) * 4)
        sum_gate, sum_up, sum_wd, sum_q, sum_o, sum_g = all_reduce(grads_low, grads_top, gains)
        by_group = sum_q.reshape(2, kv_heads, per, model_dim)

        def heads_in(g):
            return jnp.transpose(g.reshape(2, -1, head_dim, model_dim), (0, 3, 1, 2))

        q_end, k_end = n_group * head_dim, (n_group + 1) * head_dim
        d_x = jnp.transpose(d_x0, (1, 0))[None]
        return (d_x, sum_g[0:4:2], heads_in(by_group[:, :, :q_end]), heads_in(by_group[:, :, q_end:k_end]), heads_in(by_group[:, :, k_end:]), sum_o.reshape(2, n_heads, head_dim, model_dim), sum_g[1:4:2], sum_gate, sum_up, jnp.transpose(sum_wd, (0, 2, 1)))

    return jax.shard_map(local_step, mesh=mesh, in_specs=(act_spec, act_spec, act_spec) + (rep_spec,) * 9, out_specs=(act_spec,) + (rep_spec,) * 9, check_vma=False)
```

time: 379 us -> 375 us (0.989)
  Pallas kernels: 234 us -> 327 us
  matrix products: 87.7 us -> 3.55 us
  other arithmetic: 15.4 us -> 2.9 us
  local copies, waits for them, and re-layouts: 36.4 us -> 40.5 us
    pallas_call x4 -> x6, Pallas kernels: 80.4 us -> 173 us  [the longest x2 70.6 us: attn_backward(): pl.pallas_call(functools.partial(attn_bwd_kernel, head_dim ** (-0.5), sca...]
    dot_general x28 -> x2, matrix products: 87.7 us -> 3.55 us  [layer_qkv(): lax.dot_general(weights[1], normed, (((1,), (0,)), ((), ())), preferred_e...]
    transpose x1, local copies, waits for them, and re-layouts: 15.3 us -> 2.13 us  [layer_weights(): jnp.transpose(w_down[layer], (1, 0))]
    unnamed x135 -> x78, local copies, waits for them, and re-layouts: 10.2 us -> 21.5 us
    broadcast_in_dim x1 -> x0, other arithmetic: 7.5 us -> none  [local_step(): d_x = jnp.transpose(d_x0, (1, 0))[None]]
where the time goes in v3:
time: 375 us
  Pallas kernels  327 us (87%)
  local copies, waits for them, and re-layouts  40.5 us (11%)
    pallas_call x1, Pallas kernels, all_reduce(): pl.pallas_call(functools.partial(all_reduce_kernel, a_rows, a_lanes, q_ro...  154 us
    pallas_call x2, Pallas kernels, attn_backward(): pl.pallas_call(functools.partial(attn_bwd_kernel, head_dim ** (-0.5), sca...  70.6 us
    pallas_call x2, Pallas kernels, ffn(): pl.pallas_call(functools.partial(ffn_kernel, scale), grid=(ff_dim // BLK,...  66.7 us
    pallas_call x2, Pallas kernels, attn_forward(): pl.pallas_call(functools.partial(attn_fwd_kernel, head_dim ** (-0.5)), gr...  35.5 us
    unnamed x78, local copies, waits for them, and re-layouts  21.5 us

profile of v3, /device:TPU:1, one launch (start us, length us, event | category | flops | bytes accessed | tf_op | source)
XLA Modules:
  0.0 374.7 jit_solution(8252028731130473464)
XLA Ops:
  0.7 1.7 fusion
  5.4 1.5 copy-done.19
  6.9 1.2 fusion.14
  8.2 1.8 convolution_convert_fusion.q_ref.k_ref.v_ref
  10.0 1.8 convolution_convert_fusion.1.q_ref.k_ref.v_ref
  11.8 17.8 %attn_fwd.2 = (bf16[576,1024]{1,0:T(8,128)(2,1)S(1)}, bf16[576,1024]{1,0:T(8,128)(2,1)S(1)}, bf16[192,1024]{1,0:T(8,128)(2,1)S(1)}, f32[9,8,1024]{2,1,0:T(8,128)S(1)}) custom-call(bf16[960,1024]{1,0:T(8,128)(2,1)S(1)} %convolution_convert_fusion.1.q_ref.k_ref.v_ref, bf16[960,1024]{1,0:T(8,128)(2,1)S(1)} %convolution_convert_fusion.1.q_ref.k_ref.v_ref, ...), custom_call_target="tpu_custom_call" | custom-call | flops 19327352832 | bytes 7864320 | tf_op jit(solution)/shard_map/attn_fwd/pallas_call | solution.py:247
  31.5 17.7 %attn_fwd.3 = (bf16[576,1024]{1,0:T(8,128)(2,1)S(1)}, bf16[576,1024]{1,0:T(8,128)(2,1)S(1)}, bf16[192,1024]{1,0:T(8,128)(2,1)S(1)}, f32[9,8,1024]{2,1,0:T(8,128)S(1)}) custom-call(bf16[960,1024]{1,0:T(8,128)(2,1)S(1)} %convolution_convert_fusion.q_ref.k_ref.v_ref, bf16[960,1024]{1,0:T(8,128)(2,1)S(1)} %convolution_convert_fusion.q_ref.k_ref.v_ref, ...), custom_call_target="tpu_custom_call" | custom-call | flops 19327352832 | bytes 7864320 | tf_op jit(solution)/shard_map/attn_fwd/pallas_call | solution.py:247
  49.2 2.1 slice_bitcast_fusion
  52.2 1.2 copy-done.14
  54.4 3.1 slice_bitcast_fusion.1
  57.5 33.3 %ffn.2 = (bf16[576,1024]{1,0:T(8,128)(2,1)}, bf16[576,1024]{1,0:T(8,128)(2,1)}, f32[576,576]{1,0:T(8,128)}, f32[576,1]{1,0:T(8,128)}, f32[576,1536]{1,0:T(8,128)...) custom-call(bf16[576,1024]{1,0:T(8,128)(2,1)} %bitcast.107, bf16[576,1024]{1,0:T(8,128)(2,1)} %copy-done.6, ...), custom_call_target="tpu_custom_call" | custom-call | flops 16307453952 | bytes 17694720 | tf_op jit(solution)/shard_map/ffn/pallas_call | solution.py:296
  90.8 35.1 %attn_bwd.2 = (bf16[576,1024]{1,0:T(8,128)(2,1)S(1)}, f32[960,576]{1,0:T(8,128)}, f32[576,1]{1,0:T(8,128)S(1)}) custom-call(bf16[576,1024]{1,0:T(8,128)(2,1)} %copy-done.9, bf16[192,1024]{1,0:T(8,128)(2,1)S(1)} %get-tuple-element.48.kr_ref, bf16[960,1024]{1,0:T(8,128)(2,1)} %copy-done.3, bf16[576,1024]{1,0:T(8,128)(2,1)} %get-tuple-element.50.do_ref, ...), custom_call_target="tpu_custom_call" | custom-call | flops 48318382080 | bytes 7864320 | tf_op jit(solution)/shard_map/attn_bwd/pallas_call | solution.py:265
  127.3 33.4 %ffn.3 = (bf16[576,1024]{1,0:T(8,128)(2,1)}, bf16[576,1024]{1,0:T(8,128)(2,1)}, f32[576,576]{1,0:T(8,128)}, f32[576,1]{1,0:T(8,128)}, f32[576,1536]{1,0:T(8,128)...) custom-call(bf16[576,1024]{1,0:T(8,128)(2,1)} %bitcast.109, bf16[576,1024]{1,0:T(8,128)(2,1)} %copy-done.4, ...), custom_call_target="tpu_custom_call" | custom-call | flops 16307453952 | bytes 17694720 | tf_op jit(solution)/shard_map/ffn/pallas_call | solution.py:296
  160.8 35.5 %attn_bwd.3 = (bf16[576,1024]{1,0:T(8,128)(2,1)}, f32[960,576]{1,0:T(8,128)}, f32[576,1]{1,0:T(8,128)S(1)}) custom-call(bf16[576,1024]{1,0:T(8,128)(2,1)S(1)} %copy-done.8, bf16[192,1024]{1,0:T(8,128)(2,1)S(1)} %copy-done.11, bf16[960,1024]{1,0:T(8,128)(2,1)} %copy-done.2, bf16[576,1024]{1,0:T(8,128)(2,1)} %get-tuple-element.54.do_ref, ...), custom_call_target="tpu_custom_call" | custom-call | flops 48318382080 | bytes 7864320 | tf_op jit(solution)/shard_map/attn_bwd/pallas_call | solution.py:265
  197.3 153.7 %all_reduce.1 = (f32[2,576,1536]{2,1,0:T(8,128)}, f32[2,576,1536]{2,1,0:T(8,128)}, f32[2,576,1536]{2,1,0:T(8,128)}, f32[2,960,576]{2,1,0:T(8,128)}, f32[2,576,576]{2,1,0:T(8,128)}, /*index=5*/f32[8,576]{1,0:T(8,128)}) custom-call(f32[576,1536]{1,0:T(8,128)} %get-tuple-element.58.refs_0_, f32[576,1536]{1,0:T(8,128)} %get-tuple-element.59.refs_1_, ...), custom_call_target="tpu_custom_call" | custom-call | tf_op jit(solution)/shard_map/all_reduce/pallas_call | solution.py:525
  351.0 1.3 slice.91
  352.3 1.3 slice.87
  353.7 3.1 slice_bitcast_fusion.6
  356.7 3.9 %slice.92 = f32[2,3,192,576]{3,2,1,0:T(8,128)} slice(f32[2,3,320,576]{3,2,1,0:T(8,128)} %bitcast.98), slice={[0:2], [0:3], [0:192], [0:576]} | slice | bytes 5308416 | tf_op jit(solution)/shard_map/slice | solution.py:590
  360.7 1.6 copy.32
  362.3 3.6 copy.33
  365.9 1.6 slice-done.3
  367.5 3.4 copy.34
  371.7 3.0 copy.35
  (98 shorter events, 9.8 us)
Async XLA Ops:
  0.7 4.2 %copy-start.25 = (bf16[2,576,3,64]{1,3,2,0:T(8,128)(2,1)S(1)}, bf16[2,576,3,64]{1,3,2,0:T(8,128)(2,1)}, u32[]{:S(2)}) copy-start(bf16[2,576,3,64]{1,3,2,0:T(8,128)(2,1)} %param.19) | copy-start | bytes 1327108
  5.3 4.6 %copy-start.20 = (bf16[3,320,576]{2,1,0:T(8,128)(2,1)}, bf16[3,320,576]{2,1,0:T(8,128)(2,1)S(1)}, u32[]{:S(2)}) copy-start(bf16[3,320,576]{2,1,0:T(8,128)(2,1)S(1)} %get-tuple-element.100) | copy-start | bytes 3317764
  5.4 4.6 %copy-start.21 = (bf16[3,320,576]{2,1,0:T(8,128)(2,1)}, bf16[3,320,576]{2,1,0:T(8,128)(2,1)S(1)}, u32[]{:S(2)}) copy-start(bf16[3,320,576]{2,1,0:T(8,128)(2,1)S(1)} %get-tuple-element.101) | copy-start | bytes 3317764
  5.4 2.8 copy-start.23
  10.0 21.5 %copy-start.3 = (bf16[960,1024]{1,0:T(8,128)(2,1)}, bf16[960,1024]{1,0:T(8,128)(2,1)S(1)}, u32[]{:S(2)}) copy-start(bf16[960,1024]{1,0:T(8,128)(2,1)S(1)} %convolution_convert_fusion.q_ref.k_ref.v_ref) | copy-start | bytes 5898244
  11.8 17.9 %copy-start.2 = (bf16[960,1024]{1,0:T(8,128)(2,1)}, bf16[960,1024]{1,0:T(8,128)(2,1)S(1)}, u32[]{:S(2)}) copy-start(bf16[960,1024]{1,0:T(8,128)(2,1)S(1)} %convolution_convert_fusion.1.q_ref.k_ref.v_ref) | copy-start | bytes 5898244
  31.5 17.7 %copy-start.4 = (bf16[576,1024]{1,0:T(8,128)(2,1)}, bf16[576,1024]{1,0:T(8,128)(2,1)S(1)}, u32[]{:S(2)}) copy-start(bf16[576,1024]{1,0:T(8,128)(2,1)S(1)} %get-tuple-element.46.a_ref) | copy-start | bytes 3538948
  31.5 17.7 %copy-start.12 = (f32[9,8,1024]{2,1,0:T(8,128)}, f32[9,8,1024]{2,1,0:T(8,128)S(1)}, u32[]{:S(2)}) copy-start(f32[9,8,1024]{2,1,0:T(8,128)S(1)} %get-tuple-element.55.st_ref) | copy-start | bytes 884740
  31.5 17.7 %copy-start.16 = (bf16[2,1536,576]{1,2,0:T(8,128)(2,1)S(1)}, bf16[2,1536,576]{1,2,0:T(8,128)(2,1)}, u32[]{:S(2)}) copy-start(bf16[2,1536,576]{1,2,0:T(8,128)(2,1)} %param.25) | copy-start | bytes 10616836
  49.2 3.0 copy-start.9
  49.2 4.1 %copy-start.14 = (bf16[2,576,1536]{2,1,0:T(8,128)(2,1)S(1)}, bf16[2,576,1536]{2,1,0:T(8,128)(2,1)}, u32[]{:S(2)}) copy-start(bf16[2,576,1536]{2,1,0:T(8,128)(2,1)} %param.24) | copy-start | bytes 10616836
  49.2 5.2 %copy-start.15 = (bf16[2,576,1536]{2,1,0:T(8,128)(2,1)S(1)}, bf16[2,576,1536]{2,1,0:T(8,128)(2,1)}, u32[]{:S(2)}) copy-start(bf16[2,576,1536]{2,1,0:T(8,128)(2,1)} %param.23) | copy-start | bytes 10616836
  90.8 36.3 %copy-start.28 = (f32[576,1]{1,0:T(8,128)S(1)}, f32[576,1]{1,0:T(8,128)}, u32[]{:S(2)}) copy-start(f32[576,1]{1,0:T(8,128)} %get-tuple-element.71) | copy-start | bytes 6916
  127.3 33.4 %copy-start.8 = (bf16[576,1024]{1,0:T(8,128)(2,1)S(1)}, bf16[576,1024]{1,0:T(8,128)(2,1)}, u32[]{:S(2)}) copy-start(bf16[576,1024]{1,0:T(8,128)(2,1)} %copy-done.7) | copy-start | bytes 3538948
  127.3 33.4 %copy-start.11 = (bf16[192,1024]{1,0:T(8,128)(2,1)S(1)}, bf16[192,1024]{1,0:T(8,128)(2,1)}, u32[]{:S(2)}) copy-start(bf16[192,1024]{1,0:T(8,128)(2,1)} %copy-done.10) | copy-start | bytes 1179652
  127.3 33.4 %copy-start.13 = (f32[9,8,1024]{2,1,0:T(8,128)S(1)}, f32[9,8,1024]{2,1,0:T(8,128)}, u32[]{:S(2)}) copy-start(f32[9,8,1024]{2,1,0:T(8,128)} %copy-done.12) | copy-start | bytes 884740
  160.8 35.7 %copy-start.27 = (f32[576,1]{1,0:T(8,128)S(1)}, f32[576,1]{1,0:T(8,128)}, u32[]{:S(2)}) copy-start(f32[576,1]{1,0:T(8,128)} %get-tuple-element.69) | copy-start | bytes 6916
  353.7 7.0 %copy-start.17 = (f32[2,576,576]{2,1,0:T(8,128)S(1)}, f32[2,576,576]{2,1,0:T(8,128)}, u32[]{:S(2)}) copy-start(f32[2,576,576]{2,1,0:T(8,128)} %get-tuple-element.74) | copy-start | bytes 7962628
  353.7 8.6 %slice-start.4 = ((s8[7077888]{0:T(1024)(128)(4,1)}), s8[4194304]{0:T(1024)(128)(4,1)S(1)}, s32[]{:S(2)}) async-start(s8[7077888]{0:T(1024)(128)(4,1)} %bitcast.95), calls=%async_computation.4 | async-start | bytes 8388608
  356.7 5.5 %slice-start.5 = ((s8[7077888]{0:T(1024)(128)(4,1)}), s8[2883584]{0:T(1024)(128)(4,1)S(1)}, s32[]{:S(2)}) async-start(s8[7077888]{0:T(1024)(128)(4,1)} %bitcast.95), calls=%async_computation.5 | async-start | bytes 5767168
  360.7 5.2 %slice-start.2 = ((s8[7077888]{0:T(1024)(128)(4,1)}), s8[4194304]{0:T(1024)(128)(4,1)S(1)}, s32[]{:S(2)}) async-start(s8[7077888]{0:T(1024)(128)(4,1)} %bitcast.93), calls=%async_computation.2 | async-start | bytes 8388608
  362.3 5.2 %slice-start.3 = ((s8[7077888]{0:T(1024)(128)(4,1)}), s8[2883584]{0:T(1024)(128)(4,1)S(1)}, s32[]{:S(2)}) async-start(s8[7077888]{0:T(1024)(128)(4,1)} %bitcast.93), calls=%async_computation.3 | async-start | bytes 5767168
  362.3 8.6 %slice-start = ((s8[7077888]{0:T(1024)(128)(4,1)}), s8[4194304]{0:T(1024)(128)(4,1)S(1)}, s32[]{:S(2)}) async-start(s8[7077888]{0:T(1024)(128)(4,1)} %bitcast.90), calls=%async_computation | async-start | bytes 8388608
  367.5 4.2 %slice-start.1 = ((s8[7077888]{0:T(1024)(128)(4,1)}), s8[2883584]{0:T(1024)(128)(4,1)S(1)}, s32[]{:S(2)}) async-start(s8[7077888]{0:T(1024)(128)(4,1)} %bitcast.90), calls=%async_computation.1 | async-start | bytes 5767168
  (13 other events, 23.1 us)

commit v4 on v0

v4 whole, which is shorter than its diff:
```python
import functools

import jax
import jax.numpy as jnp
import numpy as np
from jax import lax
from jax.experimental import pallas as pl
from jax.experimental.pallas import tpu as pltpu
from jax.sharding import PartitionSpec as P

NORM_EPS = 1e-6
ROPE_THETA = 10000.0
BLK = 256
LOG2E = 1.4426950408889634
F32 = jnp.float32
BF16 = jnp.bfloat16


def rope_tables_np(seq_len, head_dim):
    positions = np.arange(seq_len, dtype=np.float32)
    inv_freq = np.float32(ROPE_THETA) ** (-np.arange(0, head_dim, 2, dtype=np.float32) / np.float32(head_dim))
    angles = (positions[None, :] * inv_freq.astype(np.float32)[:, None]).astype(np.float32)
    cos_t = np.repeat(np.cos(angles), 2, axis=0).astype(np.float32)
    sin_t = np.repeat(np.sin(angles), 2, axis=0).astype(np.float32)
    sin_t[0::2] *= -1.0
    return cos_t, sin_t


def pair_swap(values):
    rows = values.shape[0]
    even = lax.broadcasted_iota(jnp.int32, values.shape, 0) % 2 == 0
    return jnp.where(even, pltpu.roll(values, rows - 1, 0), pltpu.roll(values, 1, 0))


def dot_nn(lhs, rhs):
    return lax.dot_general(lhs, rhs, (((1,), (0,)), ((), ())), preferred_element_type=F32)


def dot_nt(lhs, rhs):
    return lax.dot_general(lhs, rhs, (((1,), (1,)), ((), ())), preferred_element_type=F32)


def diag_mask():
    keys = lax.broadcasted_iota(jnp.int32, (BLK, BLK), 0)
    queries = lax.broadcasted_iota(jnp.int32, (BLK, BLK), 1)
    return queries >= keys


def dot_tn(lhs, rhs):
    return lax.dot_general(lhs, rhs, (((0,), (0,)), ((), ())), preferred_element_type=F32)


def ds_of(start, size, align):
    return pl.ds(pl.multiple_of(start, align), size)


def norm_back_cols(x_f, inv, gain, d_normed):
    scaled = d_normed * gain
    d_resid = inv * scaled - x_f * (inv * inv * inv) * jnp.mean(scaled * x_f, axis=0, keepdims=True)
    return d_resid, d_normed * x_f * inv


def fold_lanes(values):
    return functools.reduce(jnp.add, [values[:, i:i + 128] for i in range(0, values.shape[1], 128)])


MESH = pl.DeviceIdType.MESH
N_RED = 3
N_ICI = 6
FLOWS = range(6)


def ds8(start, size):
    return pl.ds(pl.multiple_of(start, 8), size)


def remote(src, dst, send, recv, dev):
    return pltpu.make_async_remote_copy(src_ref=src, dst_ref=dst, send_sem=send, recv_sem=recv, device_id=(dev,), device_id_type=MESH)


def add_rows(dst, src, rows, step):
    @pl.loop(0, rows // step)
    def _(i):
        part = pl.ds(pl.multiple_of(i * step, 8), step)
        dst[part, :] = dst[part, :] + src[part, :]


class Comm:
    def __init__(self, dims, srcs, outs, refs):
        a_rows, a_lanes, q_rows, o_rows = dims
        self.srcs, self.outs = srcs, outs
        self.acc_a, self.acc_b = refs[0:2]
        self.bufs_a, self.bufs_b = refs[2:9], refs[9:16]
        (self.core_send, self.core_recv, self.load_sem, self.ici_send, self.ici_recv, self.ag_send, self.ag_recv, self.fin_send, self.fin_recv, self.fin_loc) = refs[16:26]
        self.half, self.lanes = a_rows // 2, a_lanes // 2
        self.o_half, self.q_half = o_rows // 12, q_rows // 12
        self.b_rows = self.o_half + self.q_half
        me = lax.axis_index("dp")
        self.core = lax.rem(me, 2)
        coords = (lax.rem(me // 2, 4), lax.rem(me // 8, 4), me // 32)
        strides = (2, 8, 32)
        self.peer = me + 1 - 2 * self.core
        self.gens = []
        for kind in range(2):
            for axis in range(3):
                v = coords[axis]
                if kind == 0:
                    partner, bit = v + 1 - 2 * lax.rem(v, 2), lax.rem(v + v // 2, 2)
                else:
                    partner, bit = 3 - v, v // 2
                self.gens.append((me + (partner - v) * strides[axis], bit))

    def barrier(self):
        barrier = pltpu.get_barrier_semaphore()
        for dev in [self.peer] + [g[0] for g in self.gens]:
            pl.semaphore_signal(barrier, inc=1, device_id=(dev,), device_id_type=MESH)
        pl.semaphore_wait(barrier, 1 + N_ICI)

    def gen(self, k, step):
        return self.gens[(k + step) % N_ICI]

    def core_parts(self, k, which, buf_a, buf_b):
        lane = slice((k % 2) * self.lanes, (k % 2 + 1) * self.lanes)
        q_src, o_src = self.srcs[3:]
        o_half, q_half = self.o_half, self.q_half
        return (
            (self.srcs[k // 2].at[ds8(which * self.half, self.half), lane], buf_a.at[k]),
            (o_src.at[ds8(k * 2 * o_half + which * o_half, o_half), :], buf_b.at[k, 0:o_half, :]),
            (q_src.at[ds8(k * 2 * q_half + which * q_half, q_half), :], buf_b.at[k, o_half:self.b_rows, :]),
        )

    def core_sends(self, k):
        return [remote(src, dst, self.core_send.at[k, p], self.core_recv.at[k, p], self.peer) for p, (src, dst) in enumerate(self.core_parts(k, 1 - self.core, self.bufs_a[0], self.bufs_b[0]))]

    def core_loads(self, k):
        return [pltpu.make_async_copy(src, dst, self.load_sem.at[k, p]) for p, (src, dst) in enumerate(self.core_parts(k, self.core, self.acc_a, self.acc_b))]

    def open(self):
        for k in FLOWS:
            for copy in self.core_sends(k) + self.core_loads(k):
                copy.start()

    def part_a(self, step, buf, bit):
        if step < 2:
            size = self.half >> (step + 1)
            return buf.at[ds8(bit * size, size), :]
        return buf.at[:, pl.ds(pl.multiple_of(bit * (self.lanes // 2), 128), self.lanes // 2)]

    def part_b(self, step, buf, bit):
        size = self.b_rows >> (step + 1)
        return buf.at[ds8(bit * size, size), :]

    def ici(self, k, step):
        dev, bit = self.gen(k, step)
        src_a, src_b = self.bufs_a[step].at[k], self.bufs_b[step].at[k]
        if step < N_RED:
            src_a, src_b = self.part_a(step, src_a, 1 - bit), self.part_b(step, src_b, 1 - bit)
        return [
            remote(src_a, self.bufs_a[step + 1].at[k], self.ici_send.at[k, step, 0], self.ici_recv.at[k, step, 0], dev),
            remote(src_b, self.bufs_b[step + 1].at[k], self.ici_send.at[k, step, 1], self.ici_recv.at[k, step, 1], dev),
        ]

    def ag_region(self, k, step):
        bits = [self.gen(k, s)[1] for s in range(N_RED)]
        a_off = sum([bits[s] * (self.half >> (s + 1)) for s in range(min(step, 1) + 1)])
        b_off = sum([bits[s] * (self.b_rows >> (s + 1)) for s in range(step + 1)])
        rows_a = ds8(a_off, self.half >> (min(step, 1) + 1))
        if step == 2:
            view_a = self.acc_a.at[k, rows_a, pl.ds(pl.multiple_of(bits[2] * (self.lanes // 2), 128), self.lanes // 2)]
        else:
            view_a = self.acc_a.at[k, rows_a, :]
        return view_a, self.acc_b.at[k, ds8(b_off, self.b_rows >> (step + 1)), :]

    def ag(self, k, step):
        dev = self.gen(k, step)[0]
        return [remote(view, view, self.ag_send.at[k, step, p], self.ag_recv.at[k, step, p], dev) for p, view in enumerate(self.ag_region(k, step))]

    def final(self, k):
        lane = slice((k % 2) * self.lanes, (k % 2 + 1) * self.lanes)
        out_q, out_o = self.outs[3:]
        o_half, q_half = self.o_half, self.q_half
        moves = (
            (self.acc_a.at[k], self.outs[k // 2].at[ds8(self.core * self.half, self.half), lane]),
            (self.acc_b.at[k, 0:o_half, :], out_o.at[ds8(k * 2 * o_half + self.core * o_half, o_half), :]),
            (self.acc_b.at[k, o_half:self.b_rows, :], out_q.at[ds8(k * 2 * q_half + self.core * q_half, q_half), :]),
        )
        far = [remote(src, dst, self.fin_send.at[k, p], self.fin_recv.at[k, p], self.peer) for p, (src, dst) in enumerate(moves)]
        near = [pltpu.make_async_copy(src, dst, self.fin_loc.at[k, p]) for p, (src, dst) in enumerate(moves)]
        return far, near

    def reduce(self, step):
        pending = []
        for k in FLOWS:
            if step == 0:
                for copy in self.core_loads(k):
                    copy.wait()
                for copy in self.core_sends(k):
                    copy.wait_recv()
                old_a, old_b = self.acc_a.at[k], self.acc_b.at[k]
            else:
                for copy in self.ici(k, step - 1):
                    copy.wait_recv()
                old_a, old_b = self.bufs_a[step - 1].at[k], self.bufs_b[step - 1].at[k]
                if step <= N_RED:
                    bit = self.gen(k, step - 1)[1]
                    old_a, old_b = self.part_a(step - 1, old_a, bit), self.part_b(step - 1, old_b, bit)
            cur_a, cur_b = self.bufs_a[step].at[k], self.bufs_b[step].at[k]
            add_rows(cur_a, old_a, cur_a.shape[0], 24)
            add_rows(cur_b, old_b, cur_b.shape[0], 16)
            if step < N_ICI:
                copies = self.ici(k, step)
            else:
                view_a, view_b = self.ag_region(k, N_RED - 1)
                view_a[...] = cur_a[...]
                view_b[...] = cur_b[...]
                copies = self.ag(k, N_RED - 1)
            for copy in pending:
                copy.start()
            pending = copies
        for copy in pending:
            copy.start()

    def grow(self, step):
        for k in FLOWS:
            for copy in self.ag(k, step + 1):
                copy.wait_recv()
            for copy in self.ag(k, step):
                copy.start()

    def finish(self):
        for k in FLOWS:
            for copy in self.ag(k, 0):
                copy.wait_recv()
            far, near = self.final(k)
            for copy in far + near:
                copy.start()

    def close(self):
        for k in FLOWS:
            for copy in self.core_sends(k):
                copy.wait_send()
            for step in range(N_ICI):
                for copy in self.ici(k, step):
                    copy.wait_send()
            for step in range(N_RED):
                for copy in self.ag(k, step):
                    copy.wait_send()
            far, near = self.final(k)
            for copy in far + near:
                copy.wait()


def comm_dims_of(grads):
    return grads[0].shape + (grads[3].shape[0], grads[4].shape[0])


def comm_scratch(dims):
    a_rows, a_lanes, q_rows, o_rows = dims
    half, lanes, b_rows = a_rows // 2, a_lanes // 2, (o_rows + q_rows) // 12
    width = o_rows
    shapes_a = [(half, lanes), (half // 2, lanes), (half // 4, lanes)] + [(half // 4, lanes // 2)] * 4
    shapes_b = [(b_rows >> min(step, N_RED), width) for step in range(N_ICI + 1)]
    dma = pltpu.SemaphoreType.DMA
    scratch = [pltpu.VMEM((6, half, lanes), F32), pltpu.VMEM((6, b_rows, width), F32)]
    scratch += [pltpu.VMEM((6,) + shape, F32) for shape in shapes_a]
    scratch += [pltpu.VMEM((6,) + shape, F32) for shape in shapes_b]
    return scratch + [dma((6, 3)), dma((6, 3)), dma((6, 3)), dma((6, N_ICI, 2)), dma((6, N_ICI, 2)), dma((6, N_RED, 2)), dma((6, N_RED, 2)), dma((6, 3)), dma((6, 3)), dma((6, 3))]


def all_reduce_kernel(dims, *refs):
    srcs, gain_ref = refs[0:5], refs[5]
    outs, out_g = refs[6:11], refs[11]
    comm = Comm(dims, srcs, outs, refs[12:38])
    gain_bufs, g_send, g_recv, g_loc = refs[38:42]

    def gain_copy(step):
        src = gain_ref if step == 0 else gain_bufs.at[step - 1]
        dev = comm.peer if step == 0 else comm.gens[step - 1][0]
        return remote(src, gain_bufs.at[step], g_send.at[step], g_recv.at[step], dev)

    comm.barrier()
    comm.open()
    gain_copy(0).start()
    for step in range(N_ICI + 1):
        comm.reduce(step)
        gain_copy(step).wait()
        gain_old = gain_ref if step == 0 else gain_bufs.at[step - 1]
        gain_bufs[step, :, :] = gain_bufs[step, :, :] + gain_old[...]
        if step < N_ICI:
            gain_copy(step + 1).start()
    gain_out = pltpu.make_async_copy(gain_bufs.at[N_ICI], out_g, g_loc)
    gain_out.start()
    comm.grow(1)
    comm.grow(0)
    comm.finish()
    gain_out.wait()
    comm.close()


def all_reduce(grads, gains):
    dims = comm_dims_of(grads)
    hbm = pl.BlockSpec(memory_space=pl.ANY)
    vmem = pl.BlockSpec(memory_space=pltpu.VMEM)
    dma = pltpu.SemaphoreType.DMA
    return pl.pallas_call(
        functools.partial(all_reduce_kernel, dims),
        in_specs=[hbm] * 5 + [vmem],
        out_specs=[hbm] * 6,
        out_shape=[jax.ShapeDtypeStruct(grad.shape, F32) for grad in grads] + [jax.ShapeDtypeStruct(gains.shape, F32)],
        scratch_shapes=comm_scratch(dims) + [pltpu.VMEM((N_ICI + 1,) + gains.shape, F32), dma((N_ICI + 1,)), dma((N_ICI + 1,)), dma],
        compiler_params=pltpu.CompilerParams(vmem_limit_bytes=40 * 1024 * 1024, collective_id=1, has_side_effects=True),
        name="all_reduce",
    )(*grads, gains)


def whole(shape):
    return pl.BlockSpec(shape, lambda *_: (0,) * len(shape))


def whole_once(shape):
    return pl.BlockSpec(shape, lambda *_: (0,) * len(shape), pipeline_mode=pl.Buffered(1))


def qkv_step(x_ref, gain_ref, w_ref, qkv):
    gain = gain_ref[...]

    @pl.loop(0, x_ref.shape[1] // BLK)
    def _(j):
        cols = ds_of(j * BLK, BLK, BLK)
        x_f = x_ref[:, cols].astype(F32)
        inv = lax.rsqrt(jnp.mean(x_f * x_f, axis=0, keepdims=True) + NORM_EPS)
        qkv[:, cols] = dot_nn(w_ref[...], (x_f * inv * gain).astype(BF16)).astype(BF16)


def attn_fwd_step(att_scale, first, q_ref, k_ref, v_ref, cos_ref, sin_ref, a_ref, qr_ref, kr_ref, st_ref, k_scr):
    n_blk = q_ref.shape[1] // BLK
    cos_t = cos_ref[...]
    sin_t = sin_ref[...]

    @pl.when(first)
    def _():
        k_f = k_ref[...].astype(F32)
        k_rot = (k_f * cos_t + pair_swap(k_f) * sin_t).astype(BF16)
        kr_ref[...] = k_rot
        k_scr[...] = k_rot.astype(F32).T.astype(BF16)

    coef = att_scale * LOG2E
    mask = diag_mask()
    q_f = q_ref[...].astype(F32)
    qr_ref[...] = (q_f * cos_t + pair_swap(q_f) * sin_t).astype(BF16)
    for j in range(n_blk):
        cols = slice(j * BLK, (j + 1) * BLK)
        q_j = qr_ref[:, cols]
        s_blocks = []
        for i in range(j + 1):
            s_i = dot_nn(k_scr[i * BLK:(i + 1) * BLK, :], q_j)
            if i == j:
                s_i = jnp.where(mask, s_i, -1e30)
            s_blocks.append(s_i)
        top = functools.reduce(jnp.maximum, [jnp.max(s_i, axis=0, keepdims=True) for s_i in s_blocks])
        e_blocks = [jnp.exp2((s_i - top) * coef) for s_i in s_blocks]
        total = functools.reduce(jnp.add, [jnp.sum(e_i, axis=0, keepdims=True) for e_i in e_blocks])
        inv = 1.0 / total
        acc = None
        for i in range(j + 1):
            p_i = (e_blocks[i] * inv).astype(BF16)
            part = dot_nn(v_ref[:, i * BLK:(i + 1) * BLK], p_i)
            acc = part if acc is None else acc + part
        a_ref[:, cols] = acc.astype(BF16)
        st_ref[0:1, cols] = top
        st_ref[1:2, cols] = inv


def attn_bwd_step(att_scale, first, last, qr_ref, kr_ref, v_ref, do_ref, st_ref, cos_ref, sin_ref, dq_ref, dk_ref, dv_ref, k_scr, v_scr, dk_acc, dv_acc):
    n_blk = qr_ref.shape[1] // BLK

    @pl.when(first)
    def _():
        k_scr[...] = kr_ref[...].astype(F32).T.astype(BF16)
        v_scr[...] = v_ref[...].astype(F32).T.astype(BF16)
        dk_acc[...] = jnp.zeros_like(dk_acc)
        dv_acc[...] = jnp.zeros_like(dv_acc)

    coef = att_scale * LOG2E
    mask = diag_mask()
    for j in range(n_blk):
        cols = slice(j * BLK, (j + 1) * BLK)
        q_j = qr_ref[:, cols]
        do_j = do_ref[:, cols]
        top = st_ref[0:1, cols]
        inv = st_ref[1:2, cols]
        p_blocks = []
        dp_blocks = []
        row_dot = None
        for i in range(j + 1):
            keys = slice(i * BLK, (i + 1) * BLK)
            s_i = dot_nn(k_scr[keys, :], q_j)
            if i == j:
                s_i = jnp.where(mask, s_i, -1e30)
            p_i = jnp.exp2((s_i - top) * coef) * inv
            dp_i = dot_nn(v_scr[keys, :], do_j).astype(BF16).astype(F32)
            part = jnp.sum(p_i * dp_i, axis=0, keepdims=True)
            row_dot = part if row_dot is None else row_dot + part
            dv_acc[:, keys] += dot_nt(do_j, p_i.astype(BF16))
            p_blocks.append(p_i)
            dp_blocks.append(dp_i)
        dq_j = None
        for i in range(j + 1):
            keys = slice(i * BLK, (i + 1) * BLK)
            ds_i = (p_blocks[i] * (dp_blocks[i] - row_dot) * att_scale).astype(BF16)
            part = dot_nn(kr_ref[:, keys], ds_i)
            dq_j = part if dq_j is None else dq_j + part
            dk_acc[:, keys] += dot_nt(q_j, ds_i)
        dq_j = dq_j.astype(BF16).astype(F32)
        dq_ref[:, cols] = (dq_j * cos_ref[:, cols] - pair_swap(dq_j) * sin_ref[:, cols]).astype(BF16)

    @pl.when(last)
    def _():
        d_k = dk_acc[...].astype(BF16).astype(F32)
        dk_ref[...] = (d_k * cos_ref[...] - pair_swap(d_k) * sin_ref[...]).astype(BF16)
        dv_ref[...] = dv_acc[...].astype(BF16)


def input_step(scale, x_ref, dmid_ref, gain_ref, w_ref, dqkv, dx_ref, gw_ref, gg_ref, w_t, gacc):
    gacc[...] = jnp.zeros_like(gacc)
    gw_ref[...] = jnp.zeros_like(gw_ref)
    gain = gain_ref[...]
    w_t[...] = w_ref[...].T

    @pl.loop(0, x_ref.shape[1] // BLK)
    def _(j):
        cols = ds_of(j * BLK, BLK, BLK)
        x_f = x_ref[:, cols].astype(F32)
        inv = lax.rsqrt(jnp.mean(x_f * x_f, axis=0, keepdims=True) + NORM_EPS)
        normed = (x_f * inv * gain).astype(BF16)
        gw_ref[...] += dot_nt(dqkv[:, cols], normed)
        d_normed = dot_nn(w_t[...], dqkv[:, cols]).astype(BF16).astype(F32)
        d_resid, d_gain = norm_back_cols(x_f, inv, gain, d_normed)
        gacc[...] += fold_lanes(d_gain)
        dx_ref[:, cols] = (dmid_ref[:, cols].astype(F32) + d_resid).astype(BF16)

    gw_ref[...] = gw_ref[...] * scale
    gg_ref[...] = jnp.sum(gacc[...], axis=1, keepdims=True) * scale


def ffn_step(scale, first, last, x_ref, a_ref, dout_ref, wo_ref, gain_ref, wg_ref, wu_ref, wd_ref, gwo_ref, gg_ref, gwg_ref, gwu_ref, gwd_ref, m_scr, n_scr, inv_scr, acc, hid, dg, du, wg_t, wu_t, wd_t, wo_t, gacc):
    n_blk = x_ref.shape[1] // BLK
    gain = gain_ref[...]

    @pl.when(first)
    def _():
        wo_t[...] = wo_ref[...].T

        @pl.loop(0, n_blk)
        def _(j):
            cols = ds_of(j * BLK, BLK, BLK)
            m_b = (x_ref[:, cols].astype(F32) + dot_nn(wo_t[...], a_ref[:, cols])).astype(BF16)
            m_scr[:, cols] = m_b
            m_f = m_b.astype(F32)
            inv = lax.rsqrt(jnp.mean(m_f * m_f, axis=0, keepdims=True) + NORM_EPS)
            inv_scr[0:1, cols] = inv
            n_scr[:, cols] = (m_f * inv * gain).astype(BF16)
        acc[...] = jnp.zeros_like(acc)
        gacc[...] = jnp.zeros_like(gacc)

    wg_t[...] = wg_ref[...].T
    wu_t[...] = wu_ref[...].T
    wd_t[...] = wd_ref[...].T
    for j in range(n_blk):
        cols = slice(j * BLK, (j + 1) * BLK)
        gate_f = dot_nn(wg_t[...], n_scr[:, cols]).astype(BF16).astype(F32)
        up_f = dot_nn(wu_t[...], n_scr[:, cols]).astype(BF16).astype(F32)
        d_hidden = dot_nn(wd_t[...], dout_ref[:, cols]).astype(BF16).astype(F32)
        gate_sig = jax.nn.sigmoid(gate_f)
        silu_act = gate_f * gate_sig
        hid[:, cols] = (silu_act * up_f).astype(BF16)
        dg[:, cols] = (d_hidden * up_f * gate_sig * (1.0 + gate_f * (1.0 - gate_sig))).astype(BF16)
        du[:, cols] = (d_hidden * silu_act).astype(BF16)
        acc[:, cols] += dot_nn(wg_ref[...], dg[:, cols]) + dot_nn(wu_ref[...], du[:, cols])
    gwg_ref[...] = dot_nt(n_scr[...], dg[...]) * scale
    gwu_ref[...] = dot_nt(n_scr[...], du[...]) * scale
    gwd_ref[...] = dot_nt(dout_ref[...], hid[...]) * scale

    @pl.when(last)
    def _():
        gwo_ref[...] = jnp.zeros_like(gwo_ref)

        @pl.loop(0, n_blk)
        def _(j):
            cols = ds_of(j * BLK, BLK, BLK)
            d_normed = acc[:, cols].astype(BF16).astype(F32)
            d_resid, d_gain = norm_back_cols(m_scr[:, cols].astype(F32), inv_scr[0:1, cols], gain, d_normed)
            gacc[...] += fold_lanes(d_gain)
            d_mid = (dout_ref[:, cols].astype(F32) + d_resid).astype(BF16)
            gwo_ref[...] += dot_nt(a_ref[:, cols], d_mid)
            m_scr[:, cols] = d_mid
            a_ref[:, cols] = dot_nn(wo_ref[...], d_mid).astype(BF16)

        gwo_ref[...] = gwo_ref[...] * scale
        gg_ref[...] = jnp.sum(gacc[...], axis=1, keepdims=True) * scale


COMM_AT = ((0, "open"), (5, 0), (11, 1), (13, 2), (14, 3), (15, 4), (17, 5), (19, 6), (21, "grow1"), (23, "grow0"))


def layer_kernel(scale, dims, comm_dims, *refs):
    kv_heads, n_group, head_dim = dims
    n_src = 5 if comm_dims else 0
    refs = list(refs)
    x_ref, dout_ref, wqkv_ref, wo_ref, ga_ref, gf_ref, cos_ref, sin_ref, wg_ref, wu_ref, wd_ref = refs[:11]
    srcs = refs[11:11 + n_src]
    pos = 11 + n_src
    dx_ref, gwqkv_ref, gwo_ref, gga_ref, ggf_ref, gwg_ref, gwu_ref, gwd_ref = refs[pos:pos + 8]
    outs = refs[pos + 8:pos + 8 + n_src]
    pos = pos + 8 + n_src
    qkv, a_scr, qr, kr, st, k_scr, v_scr, dk_acc, dv_acc, m_scr, n_scr, inv_scr, acc, hid, dg, du, wg_t, wu_t, wd_t, wo_t, wqkv_t, gacc = refs[pos:pos + 22]
    comm_refs = refs[pos + 22:]
    step = pl.program_id(0)
    heads = kv_heads * n_group
    n_ffn = pl.num_programs(0) - 2 * heads
    att_scale = head_dim ** -0.5
    per = (n_group + 2) * head_dim

    if comm_dims:
        comm = Comm(comm_dims, srcs, outs, comm_refs)
        for at, stage in COMM_AT:
            @pl.when(step == at)
            def _(stage=stage):
                if stage == "open":
                    comm.barrier()
                    comm.open()
                elif stage == "grow1":
                    comm.grow(1)
                elif stage == "grow0":
                    comm.grow(0)
                else:
                    comm.reduce(stage)

    @pl.when(step == 0)
    def _():
        qkv_step(x_ref, ga_ref, wqkv_ref, qkv)

    def head_views(idx):
        g, h = idx // n_group, lax.rem(idx, n_group)
        base = g * per
        rows_q = ds_of(base + h * head_dim, head_dim, head_dim)
        rows_k = ds_of(base + n_group * head_dim, head_dim, head_dim)
        rows_v = ds_of(base + (n_group + 1) * head_dim, head_dim, head_dim)
        return h, qkv.at[rows_q, :], qkv.at[rows_k, :], qkv.at[rows_v, :], a_scr.at[ds_of(idx * head_dim, head_dim, head_dim), :], qr.at[ds_of(idx * head_dim, head_dim, head_dim), :], kr.at[ds_of(g * head_dim, head_dim, head_dim), :], st.at[idx]

    @pl.when(step < heads)
    def _():
        h, q_v, k_v, v_v, a_v, qr_v, kr_v, st_v = head_views(step)
        attn_fwd_step(att_scale, h == 0, q_v, k_v, v_v, cos_ref, sin_ref, a_v, qr_v, kr_v, st_v, k_scr)

    @pl.when((step >= heads) & (step < heads + n_ffn))
    def _():
        ffn_step(scale, step == heads, step == heads + n_ffn - 1, x_ref, a_scr, dout_ref, wo_ref, gf_ref, wg_ref, wu_ref, wd_ref, gwo_ref, ggf_ref, gwg_ref, gwu_ref, gwd_ref, m_scr, n_scr, inv_scr, acc, hid, dg, du, wg_t, wu_t, wd_t, wo_t, gacc)

    @pl.when(step >= heads + n_ffn)
    def _():
        h, q_v, k_v, v_v, a_v, qr_v, kr_v, st_v = head_views(step - heads - n_ffn)
        attn_bwd_step(att_scale, h == 0, h == n_group - 1, qr_v, kr_v, v_v, a_v, st_v, cos_ref, sin_ref, q_v, k_v, v_v, k_scr, v_scr, dk_acc, dv_acc)

    @pl.when(step == pl.num_programs(0) - 1)
    def _():
        input_step(scale, x_ref, m_scr, ga_ref, wqkv_ref, qkv, dx_ref, gwqkv_ref, gga_ref, wqkv_t, gacc)
        if comm_dims:
            comm.finish()
            comm.close()


def layer_call(x_t, d_out_t, weights, cos_t, sin_t, scale, dims, other=None):
    g_attn, wqkv_t, w_o, g_ffn, w_gate, w_up, wd_t = weights
    kv_heads, n_group, head_dim = dims
    model_dim, seq_len = x_t.shape
    ff_dim = w_gate.shape[1]
    heads = kv_heads * n_group
    n_ffn = ff_dim // BLK
    w_spec = pl.BlockSpec((model_dim, BLK), lambda t: (0, jnp.minimum(jnp.maximum(t - heads, 0), n_ffn - 1)))
    hbm = pl.BlockSpec(memory_space=pl.ANY)
    col = (model_dim, 1)
    in_specs = [whole_once(x_t.shape), whole_once(x_t.shape), whole_once(wqkv_t.shape), whole_once(w_o.shape), whole_once(col), whole_once(col), whole_once(cos_t.shape), whole_once(cos_t.shape), w_spec, w_spec, w_spec]
    args = [x_t, d_out_t, wqkv_t, w_o, g_attn, g_ffn, cos_t, sin_t, w_gate, w_up, wd_t]
    out_specs = [whole_once(x_t.shape), whole_once(wqkv_t.shape), whole_once(w_o.shape), whole_once(col), whole_once(col), w_spec, w_spec, w_spec]
    shape = jax.ShapeDtypeStruct
    out_shape = [shape(x_t.shape, BF16), shape(wqkv_t.shape, F32), shape(w_o.shape, F32), shape(col, F32), shape(col, F32)] + [shape(w_gate.shape, F32)] * 3
    vm = pltpu.VMEM
    tok = (seq_len, head_dim)
    scratch = [vm(wqkv_t.shape[:1] + (seq_len,), BF16), vm((heads * head_dim, seq_len), BF16), vm((heads * head_dim, seq_len), BF16), vm((kv_heads * head_dim, seq_len), BF16), vm((heads, 8, seq_len), F32)]
    scratch += [vm(tok, BF16), vm(tok, BF16), vm(tok[::-1], F32), vm(tok[::-1], F32), vm(x_t.shape, BF16), vm(x_t.shape, BF16), vm((8, seq_len), F32), vm(x_t.shape, F32)]
    scratch += [vm((BLK, seq_len), BF16)] * 3 + [vm((BLK, model_dim), BF16)] * 3 + [vm(w_o.shape[::-1], BF16), vm(wqkv_t.shape[::-1], BF16), vm((model_dim, 128), F32)]
    comm_dims = None
    params = {}
    if other is not None:
        comm_dims = comm_dims_of(other)
        args += list(other)
        in_specs += [hbm] * 5
        out_specs += [hbm] * 5
        out_shape += [shape(grad.shape, F32) for grad in other]
        scratch += comm_scratch(comm_dims)
        params = dict(collective_id=0, has_side_effects=True)
    flops = 24 * x_t.size * ff_dim
    return pl.pallas_call(
        functools.partial(layer_kernel, scale, dims, comm_dims),
        grid=(2 * heads + n_ffn,),
        in_specs=in_specs,
        out_specs=out_specs,
        out_shape=out_shape,
        scratch_shapes=scratch,
        compiler_params=pltpu.CompilerParams(vmem_limit_bytes=67000000, **params),
        cost_estimate=pl.CostEstimate(flops=flops, bytes_accessed=20 * w_gate.size, transcendentals=0),
        name="layer" if other is None else "layer_and_sum",
    )(*args)


def solution(mesh):
    num_devices = mesh.shape["dp"]
    act_spec = P("dp", None, None)
    rep_spec = P()

    def local_step(x_layer0, x_layer1, d_out, g_attn, w_q, w_k, w_v, w_o, g_ffn, w_gate, w_up, w_down):
        _, seq_len, model_dim = x_layer0.shape
        n_heads, head_dim = w_q.shape[2], w_q.shape[3]
        kv_heads = w_k.shape[2]
        n_group = n_heads // kv_heads
        per = (n_group + 2) * head_dim
        cos_np, sin_np = rope_tables_np(seq_len, head_dim)
        cos_t, sin_t = jnp.asarray(cos_np), jnp.asarray(sin_np)
        scale = 1.0 / num_devices

        def layer_weights(layer):
            def heads_out(w):
                return jnp.transpose(w[layer], (1, 2, 0)).reshape(kv_heads, -1, model_dim)
            wqkv_t = jnp.concatenate([heads_out(w_q), heads_out(w_k), heads_out(w_v)], axis=1).reshape(-1, model_dim)
            return (g_attn[layer].astype(F32)[:, None], wqkv_t, w_o[layer].reshape(-1, model_dim), g_ffn[layer].astype(F32)[:, None], w_gate[layer], w_up[layer], jnp.transpose(w_down[layer], (1, 0)))

        x0_t = jnp.transpose(x_layer0[0], (1, 0))
        x1_t = jnp.transpose(x_layer1[0], (1, 0))
        d_top = jnp.transpose(d_out[0], (1, 0))
        w_low, w_top = layer_weights(0), layer_weights(1)
        dims = (kv_heads, n_group, head_dim)
        d_mid, gq1, go1, ga1, gf1, gg1, gu1, gd1 = layer_call(x1_t, d_top, w_top, cos_t, sin_t, scale, dims)
        low = layer_call(x0_t, d_mid, w_low, cos_t, sin_t, scale, dims, (gg1, gu1, gd1, gq1, go1))
        d_x0, gq0, go0, ga0, gf0, gg0, gu0, gd0 = low[:8]
        zero_col = jnp.zeros((model_dim, 4), F32)
        gains = jnp.concatenate([ga0, gf0, ga1, gf1, zero_col], axis=1).T
        sums = all_reduce((gg0, gu0, gd0, gq0, go0), gains)
        sum_g = sums[5]
        sum_gate, sum_up, sum_wd, sum_q, sum_o = [jnp.stack([first, second]) for first, second in zip(sums[:5], low[8:])]
        by_group = sum_q.reshape(2, kv_heads, per, model_dim)

        def heads_in(g):
            return jnp.transpose(g.reshape(2, -1, head_dim, model_dim), (0, 3, 1, 2))

        q_end, k_end = n_group * head_dim, (n_group + 1) * head_dim
        d_x = jnp.transpose(d_x0, (1, 0))[None]
        return (d_x, sum_g[0:4:2], heads_in(by_group[:, :, :q_end]), heads_in(by_group[:, :, q_end:k_end]), heads_in(by_group[:, :, k_end:]), sum_o.reshape(2, n_heads, head_dim, model_dim), sum_g[1:4:2], sum_gate, sum_up, jnp.transpose(sum_wd, (0, 2, 1)))

    return jax.shard_map(local_step, mesh=mesh, in_specs=(act_spec, act_spec, act_spec) + (rep_spec,) * 9, out_specs=(act_spec,) + (rep_spec,) * 9, check_vma=False)
```

time: 772 us -> 362 us (0.47)
  Pallas kernels: 0 us -> 308 us
  matrix products: 302 us -> 0 us
  waiting for transfers between devices: 159 us -> 0 us
  other arithmetic: 177 us -> 21.5 us
  blocking collectives: 70.9 us -> 0 us
  between operations: 15.4 us -> 0.78 us
  local copies, waits for them, and re-layouts: 42.4 us -> 31.2 us
    pallas_call x0 -> x3, Pallas kernels: none -> 308 us  [the longest x2 209 us: layer_call(): pl.pallas_call(functools.partial(layer_kernel, scale, dims, comm_dims), g...]
    dot_general x40 -> x0, matrix products: 281 us -> none  [the longest x2 56.1 us: layer_backward(): jnp.einsum('bskgd,btkd->bkgst', d_attn, v_act, preferred_element_type=jnp...]
    psum x1 -> x0, waiting for transfers between devices: 159 us -> none  [local_step(): totals = lax.psum(local_sums, 'dp')]
    another operation x15 -> x4, other arithmetic: 105 us -> 12 us  [local_step(): jnp.stack([first, second])]
    psum x1 -> x0, blocking collectives: 70.9 us -> none  [local_step(): totals = lax.psum(local_sums, 'dp')]
    mul x9 -> x0, other arithmetic: 23.9 us -> none  [the longest x1 4.37 us: local_step(): totals[6] * inv_count]
    unnamed x12 -> x0, matrix products: 20.9 us -> none
    reduce_sum x3 -> x0, other arithmetic: 18.4 us -> none  [the longest x1 16.4 us: layer_backward(): p_attn = jax.nn.softmax(jnp.where(causal, scores, -1e+30), axis=-1)]
  transfers between devices with their start and end apart: 1 -> 0, of which waited for: 1 -> 0; matrix products, arithmetic and copies ran while one was open for 1% -> 0% of each run, Pallas kernels for 0% -> 0%
where the time goes in v4:
time: 362 us; the launch traced here: 361 us
  Pallas kernels  308 us (85%)
  local copies, waits for them, and re-layouts  31.2 us (9%)
  other arithmetic  21.5 us (6%)
    pallas_call x2, Pallas kernels, layer_call(): pl.pallas_call(functools.partial(layer_kernel, scale, dims, comm_dims), g...  209 us
    pallas_call x1, Pallas kernels, all_reduce(): pl.pallas_call(functools.partial(all_reduce_kernel, dims), in_specs=[hbm]...  98.5 us
    unnamed x37, local copies, waits for them, and re-layouts  14.3 us
    another operation x4, other arithmetic, local_step(): jnp.stack([first, second])  12 us

profile of v4, /device:TPU:1, one launch (start us, length us, event | category | flops | bytes accessed | tf_op | source)
XLA Modules:
  0.0 361.5 jit_solution(6227751080306480910)
XLA Ops:
  5.9 1.1 slice_bitcast_fusion.7
  7.2 1.7 pad_maximum_fusion.3
  8.9 1.2 fusion.4
  10.9 2.1 slice_bitcast_fusion
  13.0 1.2 copy-done.5
  15.3 3.1 slice_bitcast_fusion.1
  18.4 87.4 %layer.1 = (bf16[576,1024]{1,0:T(8,128)(2,1)}, f32[960,576]{1,0:T(8,128)}, f32[576,576]{1,0:T(8,128)}, f32[576,1]{1,0:T(8,128)}, f32[576,1]{1,0:T(8,128)}, /*ind...) custom-call(bf16[576,1024]{1,0:T(8,128)(2,1)} %bitcast.111, bf16[576,1024]{1,0:T(8,128)(2,1)} %bitcast.112, ...), custom_call_target="tpu_custom_call" | custom-call | flops 21743271936 | bytes 17694720 | tf_op jit(solution)/shard_map/layer/pallas_call | solution.py:604
  106.9 1.1 copy.35
  108.0 122.1 %layer_and_sum.1 = (bf16[576,1024]{1,0:T(8,128)(2,1)}, f32[960,576]{1,0:T(8,128)}, f32[576,576]{1,0:T(8,128)}, f32[576,1]{1,0:T(8,128)}, f32[576,1]{1,0:T(8,128)...) custom-call(bf16[576,1024]{1,0:T(8,128)(2,1)} %bitcast.113, ...), custom_call_target="tpu_custom_call" | custom-call | flops 21743271936 | bytes 17694720 | tf_op jit(solution)/shard_map/layer_and_sum/pallas_call | solution.py:604
  230.0 1.1 copy.32
  231.1 1.1 copy.33
  232.3 1.7 copy-done.2
  234.0 1.4 copy-done.3
  235.4 98.5 %all_reduce.1 = (f32[576,1536]{1,0:T(8,128)S(1)}, f32[576,1536]{1,0:T(8,128)}, f32[576,1536]{1,0:T(8,128)}, f32[960,576]{1,0:T(8,128)S(1)}, f32[576,576]{1,0:T(8,128)S(1)}, /*index=5*/f32[8,576]{1,0:T(8,128)S(1)}) custom-call(f32[576,1536]{1,0:T(8,128)} %get-tuple-element.44.refs_0_, f32[576,1536]{1,0:T(8,128)} %get-tuple-element.45.refs_1_, ...), custom_call_target="tpu_custom_call" | custom-call | tf_op jit(solution)/shard_map/all_reduce/pallas_call | solution.py:305
  333.9 1.8 copy-done
  335.7 1.9 pad_maximum_fusion.2
  338.8 2.7 fusion.3
  341.5 1.8 fusion
  343.3 1.3 copy-done.1
  345.7 4.1 %pad_maximum_fusion = f32[2,576,1536]{2,1,0:T(8,128)} fusion(f32[1,576,1536]{2,1,0:T(8,128)S(1)} %bitcast.99, f32[1,576,1536]{2,1,0:T(8,128)S(1)} %bitcast.92), kind=kLoop, calls=%fused_computation | loop fusion | flops 1769472 | bytes 14155776 | tf_op jit(solution)/shard_map/stack | solution.py:650
  349.8 1.5 copy-done.11
  351.3 4.1 %pad_maximum_fusion.1 = f32[2,576,1536]{2,1,0:T(8,128)} fusion(f32[1,576,1536]{2,1,0:T(8,128)S(1)} %bitcast.98, f32[1,576,1536]{2,1,0:T(8,128)S(1)} %bitcast.101), kind=kLoop, calls=%fused_computation.1 | loop fusion | flops 1769472 | bytes 14155776 | tf_op jit(solution)/shard_map/stack | solution.py:650
  355.4 1.5 copy-done.10
  356.9 3.5 maximum_bitcast_fusion
  (43 shorter events, 11.7 us)
Async XLA Ops:
  0.6 6.3 %copy-start.17 = (bf16[2,576,3,64]{1,3,2,0:T(8,128)(2,1)S(1)}, bf16[2,576,3,64]{1,3,2,0:T(8,128)(2,1)}, u32[]{:S(2)}) copy-start(bf16[2,576,3,64]{1,3,2,0:T(8,128)(2,1)} %param.20) | copy-start | bytes 1327108
  0.7 6.4 %copy-start.13 = (bf16[2,576,9,64]{1,3,2,0:T(8,128)(2,1)S(1)}, bf16[2,576,9,64]{1,3,2,0:T(8,128)(2,1)}, u32[]{:S(2)}) copy-start(bf16[2,576,9,64]{1,3,2,0:T(8,128)(2,1)} %param.18) | copy-start | bytes 3981316
  7.0 1.9 copy-start.14
  7.2 3.8 %copy-start.12 = (bf16[2,1536,576]{1,2,0:T(8,128)(2,1)S(1)}, bf16[2,1536,576]{1,2,0:T(8,128)(2,1)}, u32[]{:S(2)}) copy-start(bf16[2,1536,576]{1,2,0:T(8,128)(2,1)} %param.25) | copy-start | bytes 10616836
  10.9 3.3 copy-start.5
  10.9 4.4 %copy-start.6 = (bf16[2,576,1536]{2,1,0:T(8,128)(2,1)S(1)}, bf16[2,576,1536]{2,1,0:T(8,128)(2,1)}, u32[]{:S(2)}) copy-start(bf16[2,576,1536]{2,1,0:T(8,128)(2,1)} %param.23) | copy-start | bytes 10616836
  232.3 1.7 copy-start.2
  234.0 1.4 copy-start.3
  235.4 100.3 %copy-start.15 = (f32[576,576]{1,0:T(8,128)S(1)}, f32[576,576]{1,0:T(8,128)}, u32[]{:S(2)}) copy-start(f32[576,576]{1,0:T(8,128)} %get-tuple-element.57) | copy-start | bytes 3981316
  333.9 1.8 copy-start
  338.8 2.7 copy-start.4
  341.5 3.1 copy-start.1
  341.5 4.1 %copy-start.9 = (f32[576,1536]{1,0:T(8,128)S(1)}, f32[576,1536]{1,0:T(8,128)}, u32[]{:S(2)}) copy-start(f32[576,1536]{1,0:T(8,128)} %get-tuple-element.59) | copy-start | bytes 10616836
  345.7 4.1 %copy-start.8 = (f32[576,1536]{1,0:T(8,128)S(1)}, f32[576,1536]{1,0:T(8,128)}, u32[]{:S(2)}) copy-start(f32[576,1536]{1,0:T(8,128)} %get-tuple-element.61) | copy-start | bytes 10616836
  345.7 5.6 %copy-start.11 = (f32[576,1536]{1,0:T(8,128)S(1)}, f32[576,1536]{1,0:T(8,128)}, u32[]{:S(2)}) copy-start(f32[576,1536]{1,0:T(8,128)} %get-tuple-element.60) | copy-start | bytes 10616836
  351.3 4.1 %copy-start.7 = (f32[576,1536]{1,0:T(8,128)S(1)}, f32[576,1536]{1,0:T(8,128)}, u32[]{:S(2)}) copy-start(f32[576,1536]{1,0:T(8,128)} %get-tuple-element.63) | copy-start | bytes 10616836
  351.3 5.6 %copy-start.10 = (f32[576,1536]{1,0:T(8,128)S(1)}, f32[576,1536]{1,0:T(8,128)}, u32[]{:S(2)}) copy-start(f32[576,1536]{1,0:T(8,128)} %get-tuple-element.62) | copy-start | bytes 10616836
  356.9 3.5 copy-start.16

commit v5 on v4

v5 whole, which is shorter than its diff:
```python
import functools

import jax
import jax.numpy as jnp
import numpy as np
from jax import lax
from jax.experimental import pallas as pl
from jax.experimental.pallas import tpu as pltpu
from jax.sharding import PartitionSpec as P

NORM_EPS = 1e-6
ROPE_THETA = 10000.0
BLK = 256
VMEM_ALL = 67000000
VMEM_PART = 67000000
LOG2E = 1.4426950408889634
F32 = jnp.float32
BF16 = jnp.bfloat16


def rope_tables_np(seq_len, head_dim):
    positions = np.arange(seq_len, dtype=np.float32)
    inv_freq = np.float32(ROPE_THETA) ** (-np.arange(0, head_dim, 2, dtype=np.float32) / np.float32(head_dim))
    angles = (positions[None, :] * inv_freq.astype(np.float32)[:, None]).astype(np.float32)
    cos_t = np.repeat(np.cos(angles), 2, axis=0).astype(np.float32)
    sin_t = np.repeat(np.sin(angles), 2, axis=0).astype(np.float32)
    sin_t[0::2] *= -1.0
    return cos_t, sin_t


def pair_swap(values):
    rows = values.shape[0]
    even = lax.broadcasted_iota(jnp.int32, values.shape, 0) % 2 == 0
    return jnp.where(even, pltpu.roll(values, rows - 1, 0), pltpu.roll(values, 1, 0))


def dot_nn(lhs, rhs):
    return lax.dot_general(lhs, rhs, (((1,), (0,)), ((), ())), preferred_element_type=F32)


def dot_nt(lhs, rhs):
    return lax.dot_general(lhs, rhs, (((1,), (1,)), ((), ())), preferred_element_type=F32)


def diag_mask():
    keys = lax.broadcasted_iota(jnp.int32, (BLK, BLK), 0)
    queries = lax.broadcasted_iota(jnp.int32, (BLK, BLK), 1)
    return queries >= keys


def ds_of(start, size, align):
    return pl.ds(pl.multiple_of(start, align), size)


def norm_back_cols(x_f, inv, gain, d_normed):
    scaled = d_normed * gain
    d_resid = inv * scaled - x_f * (inv * inv * inv) * jnp.mean(scaled * x_f, axis=0, keepdims=True)
    return d_resid, d_normed * x_f * inv


def fold_lanes(values):
    return functools.reduce(jnp.add, [values[:, i:i + 128] for i in range(0, values.shape[1], 128)])


MESH = pl.DeviceIdType.MESH
N_RED = 3
N_ICI = 6
SUM_SUB = 2
LAYER_SUB = 2
ADD_ROWS = 72
LANE = 128


def ds8(start, size):
    return ds_of(start, size, 8)


def remote(src, dst, send, recv, dev):
    return pltpu.make_async_remote_copy(src_ref=src, dst_ref=dst, send_sem=send, recv_sem=recv, device_id=(dev,), device_id_type=MESH)


def add_rows(dst, src):
    @pl.loop(0, dst.shape[0] // ADD_ROWS)
    def _(i):
        part = ds8(i * ADD_ROWS, ADD_ROWS)
        dst[part, :] = dst[part, :] + src[part, :]


class Comm:
    def __init__(self, n_sub, srcs, outs, refs):
        rows, width = srcs[0].shape
        self.n_sub, self.n_flow = n_sub, N_ICI * n_sub
        self.srcs, self.outs = srcs, outs
        self.acc, self.bufs = refs[0], refs[1:8]
        (self.core_send, self.core_recv, self.load_sem, self.ici_send, self.ici_recv, self.ag_send, self.ag_recv, self.fin_send, self.fin_recv, self.fin_loc) = refs[8:18]
        self.half, self.width, self.lanes = rows // 2, width, len(srcs) * width // self.n_flow
        me = lax.axis_index("dp")
        self.core = lax.rem(me, 2)
        self.peer = me + 1 - 2 * self.core
        self.gens = []
        for kind in range(2):
            for stride in (2, 8, 32):
                v = lax.rem(me // stride, 4)
                if kind == 0:
                    partner, bit = v + 1 - 2 * lax.rem(v, 2), lax.rem(v + v // 2, 2)
                else:
                    partner, bit = 3 - v, v // 2
                self.gens.append((me + (partner - v) * stride, bit))

    def barrier(self):
        barrier = pltpu.get_barrier_semaphore()
        for dev in [self.peer] + [g[0] for g in self.gens]:
            pl.semaphore_signal(barrier, inc=1, device_id=(dev,), device_id_type=MESH)
        pl.semaphore_wait(barrier, 1 + N_ICI)

    def flows(self, sub):
        return range(N_ICI * sub, N_ICI * (sub + 1))

    def gen(self, f, step):
        return self.gens[(f + step) % N_ICI]

    def bands(self, f):
        low, high = f * self.lanes, (f + 1) * self.lanes
        found = []
        while low < high:
            mat = low // self.width
            end = min(high, (mat + 1) * self.width)
            found.append((mat, slice(low - mat * self.width, end - mat * self.width), slice(low - f * self.lanes, end - f * self.lanes)))
            low = end
        return found

    def core_sends(self, f):
        rows = ds8((1 - self.core) * self.half, self.half)
        return [remote(self.srcs[mat].at[rows, cols], self.bufs[0].at[f, :, own], self.core_send.at[f, p], self.core_recv.at[f, p], self.peer) for p, (mat, cols, own) in enumerate(self.bands(f))]

    def core_loads(self, f):
        rows = ds8(self.core * self.half, self.half)
        return [pltpu.make_async_copy(self.srcs[mat].at[rows, cols], self.acc.at[f, :, own], self.load_sem.at[f, p]) for p, (mat, cols, own) in enumerate(self.bands(f))]

    def final(self, f):
        rows = ds8(self.core * self.half, self.half)
        moves = [(self.acc.at[f, :, own], self.outs[mat].at[rows, cols]) for mat, cols, own in self.bands(f)]
        far = [remote(src, dst, self.fin_send.at[f, p], self.fin_recv.at[f, p], self.peer) for p, (src, dst) in enumerate(moves)]
        near = [pltpu.make_async_copy(src, dst, self.fin_loc.at[f, p]) for p, (src, dst) in enumerate(moves)]
        return far, near

    def open(self, sub):
        for f in self.flows(sub):
            for copy in self.core_sends(f) + self.core_loads(f):
                copy.start()

    def part(self, step, buf, bit):
        if step < N_RED - 1:
            size = self.half >> (step + 1)
            return buf.at[ds8(bit * size, size), :]
        return buf.at[:, ds_of(bit * (self.lanes // 2), self.lanes // 2, LANE)]

    def ici(self, f, step):
        dev, bit = self.gen(f, step)
        src = self.bufs[step].at[f]
        if step < N_RED:
            src = self.part(step, src, 1 - bit)
        return remote(src, self.bufs[step + 1].at[f], self.ici_send.at[f, step], self.ici_recv.at[f, step], dev)

    def region(self, f, step):
        bits = [self.gen(f, s)[1] for s in range(N_RED)]
        top = min(step, N_RED - 2)
        rows = ds8(sum([bits[s] * (self.half >> (s + 1)) for s in range(top + 1)]), self.half >> (top + 1))
        if step < N_RED - 1:
            return self.acc.at[f, rows, :]
        return self.acc.at[f, rows, ds_of(bits[step] * (self.lanes // 2), self.lanes // 2, LANE)]

    def ag(self, f, step):
        view = self.region(f, step)
        return remote(view, view, self.ag_send.at[f, step], self.ag_recv.at[f, step], self.gen(f, step)[0])

    def reduce(self, step, sub):
        pending = None
        for f in self.flows(sub):
            if step == 0:
                for copy in self.core_loads(f):
                    copy.wait()
                for copy in self.core_sends(f):
                    copy.wait_recv()
                old = self.acc.at[f]
            else:
                self.ici(f, step - 1).wait_recv()
                old = self.bufs[step - 1].at[f]
                if step <= N_RED:
                    old = self.part(step - 1, old, self.gen(f, step - 1)[1])
            cur = self.bufs[step].at[f]
            add_rows(cur, old)
            if step < N_ICI:
                copy = self.ici(f, step)
            else:
                view = self.region(f, N_RED - 1)
                view[...] = cur[...]
                copy = self.ag(f, N_RED - 1)
            if pending is not None:
                pending.start()
            pending = copy
        pending.start()

    def grow(self, step, sub):
        for f in self.flows(sub):
            self.ag(f, step + 1).wait_recv()
            self.ag(f, step).start()

    def finish(self, sub):
        for f in self.flows(sub):
            self.ag(f, 0).wait_recv()
            far, near = self.final(f)
            for copy in far + near:
                copy.start()

    def serve(self, stage, sub):
        if stage == 0:
            self.open(sub)
        elif stage < N_ICI + 2:
            self.reduce(stage - 1, sub)
        elif stage < N_ICI + 4:
            self.grow(N_ICI + 3 - stage, sub)
        else:
            self.finish(sub)

    def close(self):
        for f in range(self.n_flow):
            for copy in self.core_sends(f):
                copy.wait_send()
            for step in range(N_ICI):
                self.ici(f, step).wait_send()
            for step in range(N_RED):
                self.ag(f, step).wait_send()
            far, near = self.final(f)
            for copy in far + near:
                copy.wait()


def comm_scratch(n_sub, srcs):
    rows, width = srcs[0].shape
    n = N_ICI * n_sub
    half, lanes = rows // 2, len(srcs) * width // n
    shapes = [(half, lanes), (half // 2, lanes), (half // 4, lanes)] + [(half // 4, lanes // 2)] * 4
    pieces = 3 - n_sub
    dma = pltpu.SemaphoreType.DMA
    return [pltpu.VMEM((n, half, lanes), F32)] + [pltpu.VMEM((n,) + shape, F32) for shape in shapes] + [dma((n, pieces))] * 3 + [dma((n, N_ICI))] * 2 + [dma((n, N_RED))] * 2 + [dma((n, pieces))] * 3


def all_reduce_kernel(n_mat, *refs):
    srcs, gain_low, gain_top = refs[:n_mat], refs[n_mat], refs[n_mat + 1]
    refs = refs[n_mat + 2:]
    outs, out_g = refs[:n_mat], refs[n_mat]
    gain_src, gain_bufs, g_send, g_recv, g_loc = refs[-5:]
    comm = Comm(SUM_SUB, srcs, outs, refs[n_mat + 1:])

    def gain_copy(step):
        src = gain_src if step == 0 else gain_bufs.at[step - 1]
        dev = comm.peer if step == 0 else comm.gens[step - 1][0]
        return remote(src, gain_bufs.at[step], g_send.at[step], g_recv.at[step], dev)

    gain_src[...] = gain_low[...]
    gain_src[2:4, :] = gain_top[0:2, :]
    comm.barrier()
    for sub in range(SUM_SUB):
        comm.open(sub)
    gain_copy(0).start()
    for step in range(N_ICI + 1):
        for sub in range(SUM_SUB):
            comm.reduce(step, sub)
        gain_copy(step).wait()
        gain_old = gain_src if step == 0 else gain_bufs.at[step - 1]
        gain_bufs[step, :, :] = gain_bufs[step, :, :] + gain_old[...]
        if step < N_ICI:
            gain_copy(step + 1).start()
    gain_out = pltpu.make_async_copy(gain_bufs.at[N_ICI], out_g, g_loc)
    gain_out.start()
    for step in (1, 0):
        for sub in range(SUM_SUB):
            comm.grow(step, sub)
    for sub in range(SUM_SUB):
        comm.finish(sub)
    gain_out.wait()
    comm.close()


def all_reduce(grads, gain_low, gain_top):
    hbm = pl.BlockSpec(memory_space=pl.ANY)
    vmem = pl.BlockSpec(memory_space=pltpu.VMEM)
    dma = pltpu.SemaphoreType.DMA
    n_mat = len(grads)
    return pl.pallas_call(
        functools.partial(all_reduce_kernel, n_mat),
        in_specs=[hbm] * n_mat + [vmem] * 2,
        out_specs=[hbm] * (n_mat + 1),
        out_shape=[jax.ShapeDtypeStruct(grad.shape, F32) for grad in grads] + [jax.ShapeDtypeStruct(gain_low.shape, F32)],
        scratch_shapes=comm_scratch(SUM_SUB, grads) + [pltpu.VMEM(gain_low.shape, F32), pltpu.VMEM((N_ICI + 1,) + gain_low.shape, F32), dma((N_ICI + 1,)), dma((N_ICI + 1,)), dma],
        compiler_params=pltpu.CompilerParams(vmem_limit_bytes=VMEM_PART, collective_id=1, has_side_effects=True),
        name="all_reduce",
    )(*grads, gain_low, gain_top)


def assemble_kernel(n_group, *refs):
    low, top, (sum_g, dx_in), outs = refs[:4], refs[4:8], refs[8:10], refs[10:17]
    grad_ga, grad_gf, dx_out, turned = refs[17:]
    layer, i = pl.program_id(0), pl.program_id(1)
    head_dim = outs[-1].shape[0]
    base = (i // n_group) * (n_group + 2)

    def fill(mats):
        for src, dst in zip(mats[:3], outs):
            dst[...] = src[...]

        @pl.when(i == 0)
        def _():
            turned[...] = mats[-1][...].T

    @pl.when(layer == 0)
    def _():
        fill(low)
        dx_out[...] = dx_in[...]
        for row in range(2):
            grad_ga[row:row + 1, :] = sum_g[2 * row:2 * row + 1, :]
            grad_gf[row:row + 1, :] = sum_g[2 * row + 1:2 * row + 2, :]

    @pl.when(layer == 1)
    def _():
        fill(top)

    spots = (base + lax.rem(i, n_group), base + n_group, base + n_group + 1, i + pl.num_programs(1) * (n_group + 2) // n_group)
    for spot, dst in zip(spots, outs[3:]):
        dst[...] = turned[ds_of(spot * head_dim, head_dim, head_dim), :]


def assemble(low, top, sum_g, d_x, n_group, head_dim):
    model_dim, ff_dim = low[0].shape
    heads = model_dim // head_dim
    kv_heads = heads // n_group

    def maps(layer):
        def at(l, i):
            return i * (1 - l) + (heads - 1) * l if layer == 0 else i * l
        return [pl.BlockSpec((head_dim, ff_dim), lambda l, i: (at(l, i), 0))] * 3 + [pl.BlockSpec(low[3].shape, lambda l, i: (0, 0), pipeline_mode=pl.Buffered(1))]

    out_big = pl.BlockSpec((None, head_dim, ff_dim), lambda l, i: (l, i, 0))
    out_small = pl.BlockSpec((None, head_dim, model_dim), lambda l, i: (l, i, 0))
    out_kv = pl.BlockSpec((None, head_dim, model_dim), lambda l, i: (l, i // n_group, 0))
    shape = jax.ShapeDtypeStruct
    gain_shape = shape((2, model_dim), F32)
    dx_spec = pl.BlockSpec((head_dim, d_x.shape[1]), lambda l, i: (i * (1 - l) + (heads - 1) * l, 0))
    big_shape, q_shape, kv_shape = shape((2, model_dim, ff_dim), F32), shape((2, model_dim, model_dim), F32), shape((2, kv_heads * head_dim, model_dim), F32)
    return pl.pallas_call(
        functools.partial(assemble_kernel, n_group),
        grid=(2, heads),
        in_specs=maps(0) + maps(1) + [whole_once(sum_g.shape), dx_spec],
        out_specs=[out_big] * 3 + [out_small, out_kv, out_kv, out_small, whole_once(gain_shape.shape), whole_once(gain_shape.shape), dx_spec],
        out_shape=[big_shape] * 3 + [q_shape, kv_shape, kv_shape, q_shape, gain_shape, gain_shape, shape(d_x.shape, d_x.dtype)],
        scratch_shapes=[pltpu.VMEM(low[3].shape[::-1], F32)],
        compiler_params=pltpu.CompilerParams(vmem_limit_bytes=VMEM_PART),
        name="assemble",
    )(*low, *top, sum_g, d_x)


def whole_once(shape):
    return pl.BlockSpec(shape, lambda *_: (0,) * len(shape), pipeline_mode=pl.Buffered(1))


def qkv_step(x_ref, gain_ref, w_ref, qkv):
    gain = gain_ref[...]

    @pl.loop(0, x_ref.shape[1] // BLK)
    def _(j):
        cols = ds_of(j * BLK, BLK, BLK)
        x_f = x_ref[:, cols].astype(F32)
        inv = lax.rsqrt(jnp.mean(x_f * x_f, axis=0, keepdims=True) + NORM_EPS)
        qkv[:, cols] = dot_nn(w_ref[...], (x_f * inv * gain).astype(BF16)).astype(BF16)


def attn_fwd_step(att_scale, first, q_ref, k_ref, v_ref, cos_ref, sin_ref, a_ref, qr_ref, kr_ref, st_ref, k_scr):
    n_blk = q_ref.shape[1] // BLK
    cos_t = cos_ref[...]
    sin_t = sin_ref[...]

    @pl.when(first)
    def _():
        k_f = k_ref[...].astype(F32)
        k_rot = (k_f * cos_t + pair_swap(k_f) * sin_t).astype(BF16)
        kr_ref[...] = k_rot
        k_scr[...] = k_rot.astype(F32).T.astype(BF16)

    coef = att_scale * LOG2E
    mask = diag_mask()
    q_f = q_ref[...].astype(F32)
    qr_ref[...] = (q_f * cos_t + pair_swap(q_f) * sin_t).astype(BF16)
    for j in range(n_blk):
        cols = slice(j * BLK, (j + 1) * BLK)
        q_j = qr_ref[:, cols]
        s_blocks = []
        for i in range(j + 1):
            s_i = dot_nn(k_scr[i * BLK:(i + 1) * BLK, :], q_j)
            if i == j:
                s_i = jnp.where(mask, s_i, -1e30)
            s_blocks.append(s_i)
        top = functools.reduce(jnp.maximum, [jnp.max(s_i, axis=0, keepdims=True) for s_i in s_blocks])
        e_blocks = [jnp.exp2((s_i - top) * coef) for s_i in s_blocks]
        total = functools.reduce(jnp.add, [jnp.sum(e_i, axis=0, keepdims=True) for e_i in e_blocks])
        inv = 1.0 / total
        acc = None
        for i in range(j + 1):
            p_i = (e_blocks[i] * inv).astype(BF16)
            part = dot_nn(v_ref[:, i * BLK:(i + 1) * BLK], p_i)
            acc = part if acc is None else acc + part
        a_ref[:, cols] = acc.astype(BF16)
        st_ref[0:1, cols] = top
        st_ref[1:2, cols] = inv


def clear(*targets):
    for ref in targets:
        ref[...] = jnp.zeros_like(ref)


def attn_bwd_step(att_scale, first, last, qr_ref, kr_ref, v_ref, do_ref, st_ref, cos_ref, sin_ref, dq_ref, dk_ref, dv_ref, k_scr, v_scr, dk_acc, dv_acc):
    n_blk = qr_ref.shape[1] // BLK

    @pl.when(first)
    def _():
        k_scr[...] = kr_ref[...].astype(F32).T.astype(BF16)
        v_scr[...] = v_ref[...].astype(F32).T.astype(BF16)
        clear(dk_acc)
        clear(dv_acc)

    coef = att_scale * LOG2E
    mask = diag_mask()
    for j in range(n_blk):
        cols = slice(j * BLK, (j + 1) * BLK)
        q_j = qr_ref[:, cols]
        do_j = do_ref[:, cols]
        top = st_ref[0:1, cols]
        inv = st_ref[1:2, cols]
        p_blocks = []
        dp_blocks = []
        row_dot = None
        for i in range(j + 1):
            keys = slice(i * BLK, (i + 1) * BLK)
            s_i = dot_nn(k_scr[keys, :], q_j)
            if i == j:
                s_i = jnp.where(mask, s_i, -1e30)
            p_i = jnp.exp2((s_i - top) * coef) * inv
            dp_i = dot_nn(v_scr[keys, :], do_j).astype(BF16).astype(F32)
            part = jnp.sum(p_i * dp_i, axis=0, keepdims=True)
            row_dot = part if row_dot is None else row_dot + part
            dv_acc[:, keys] += dot_nt(do_j, p_i.astype(BF16))
            p_blocks.append(p_i)
            dp_blocks.append(dp_i)
        dq_j = None
        for i in range(j + 1):
            keys = slice(i * BLK, (i + 1) * BLK)
            ds_i = (p_blocks[i] * (dp_blocks[i] - row_dot) * att_scale).astype(BF16)
            part = dot_nn(kr_ref[:, keys], ds_i)
            dq_j = part if dq_j is None else dq_j + part
            dk_acc[:, keys] += dot_nt(q_j, ds_i)
        dq_j = dq_j.astype(BF16).astype(F32)
        dq_ref[:, cols] = (dq_j * cos_ref[:, cols] - pair_swap(dq_j) * sin_ref[:, cols]).astype(BF16)

    @pl.when(last)
    def _():
        d_k = dk_acc[...].astype(BF16).astype(F32)
        dk_ref[...] = (d_k * cos_ref[...] - pair_swap(d_k) * sin_ref[...]).astype(BF16)
        dv_ref[...] = dv_acc[...].astype(BF16)


def input_step(scale, x_ref, dmid_ref, gain_ref, w_ref, dqkv, dx_ref, gw_ref, gg_ref, w_t, gacc):
    clear(gacc, gw_ref)
    gain = gain_ref[...]
    w_t[...] = w_ref[...].T

    @pl.loop(0, x_ref.shape[1] // BLK)
    def _(j):
        cols = ds_of(j * BLK, BLK, BLK)
        x_f = x_ref[:, cols].astype(F32)
        inv = lax.rsqrt(jnp.mean(x_f * x_f, axis=0, keepdims=True) + NORM_EPS)
        normed = (x_f * inv * gain).astype(BF16)
        gw_ref[...] += dot_nt(normed, dqkv[:, cols])
        d_normed = dot_nn(w_t[...], dqkv[:, cols]).astype(BF16).astype(F32)
        d_resid, d_gain = norm_back_cols(x_f, inv, gain, d_normed)
        gacc[...] += fold_lanes(d_gain)
        dx_ref[:, cols] = (dmid_ref[:, cols].astype(F32) + d_resid).astype(BF16)

    gw_ref[...] = gw_ref[...] * scale
    gg_ref[...] = jnp.sum(gacc[...].T, axis=0, keepdims=True) * scale


def ffn_step(scale, first, last, x_ref, a_ref, dout_ref, wo_ref, gain_ref, wg_ref, wu_ref, wd_ref, gwo_ref, gwo_acc, gg_ref, gwg_ref, gwu_ref, gwd_ref, m_scr, n_scr, inv_scr, acc, hid, dg, du, wg_t, wu_t, wd_t, wo_t, gacc):
    n_blk = x_ref.shape[1] // BLK
    gain = gain_ref[...]

    @pl.when(first)
    def _():
        wo_t[...] = wo_ref[...].T

        @pl.loop(0, n_blk)
        def _(j):
            cols = ds_of(j * BLK, BLK, BLK)
            m_b = (x_ref[:, cols].astype(F32) + dot_nn(wo_t[...], a_ref[:, cols])).astype(BF16)
            m_scr[:, cols] = m_b
            m_f = m_b.astype(F32)
            inv = lax.rsqrt(jnp.mean(m_f * m_f, axis=0, keepdims=True) + NORM_EPS)
            inv_scr[0:1, cols] = inv
            n_scr[:, cols] = (m_f * inv * gain).astype(BF16)
        clear(acc)
        clear(gacc)

    wg_t[...] = wg_ref[...].T
    wu_t[...] = wu_ref[...].T
    wd_t[...] = wd_ref[...].T
    for j in range(n_blk):
        cols = slice(j * BLK, (j + 1) * BLK)
        gate_f = dot_nn(wg_t[...], n_scr[:, cols]).astype(BF16).astype(F32)
        up_f = dot_nn(wu_t[...], n_scr[:, cols]).astype(BF16).astype(F32)
        d_hidden = dot_nn(wd_t[...], dout_ref[:, cols]).astype(BF16).astype(F32)
        gate_sig = jax.nn.sigmoid(gate_f)
        silu_act = gate_f * gate_sig
        hid[:, cols] = (silu_act * up_f).astype(BF16)
        dg[:, cols] = (d_hidden * up_f * gate_sig * (1.0 + gate_f * (1.0 - gate_sig))).astype(BF16)
        du[:, cols] = (d_hidden * silu_act).astype(BF16)
        acc[:, cols] += dot_nn(wg_ref[...], dg[:, cols]) + dot_nn(wu_ref[...], du[:, cols])
    gwg_ref[...] = dot_nt(n_scr[...], dg[...]) * scale
    gwu_ref[...] = dot_nt(n_scr[...], du[...]) * scale
    gwd_ref[...] = dot_nt(dout_ref[...], hid[...]) * scale

    @pl.when(last)
    def _():
        clear(gwo_acc)

        @pl.loop(0, n_blk)
        def _(j):
            cols = ds_of(j * BLK, BLK, BLK)
            d_normed = acc[:, cols].astype(BF16).astype(F32)
            d_resid, d_gain = norm_back_cols(m_scr[:, cols].astype(F32), inv_scr[0:1, cols], gain, d_normed)
            gacc[...] += fold_lanes(d_gain)
            d_mid = (dout_ref[:, cols].astype(F32) + d_resid).astype(BF16)
            gwo_acc[...] += dot_nt(d_mid, a_ref[:, cols])
            m_scr[:, cols] = d_mid
            a_ref[:, cols] = dot_nn(wo_ref[...], d_mid).astype(BF16)

        gwo_ref[...] = gwo_acc[...] * scale
        gg_ref[...] = jnp.sum(gacc[...].T, axis=0, keepdims=True) * scale


COMM_AT = ((0, 2, 7, 10, 11, 12, 13, 14, 15, 17, 20), (0, 5, 9, 11, 12, 13, 14, 15, 16, 19, 22))


def layer_kernel(layer, scale, dims, pl_steps, n_src, *refs):
    kv_heads, n_group, head_dim = dims
    refs = list(refs)
    x_ref, dout_ref, wq_ref, wk_ref, wv_ref, wo_ref, ga_in, gf_in, cos_ref, sin_ref, wg_ref, wu_ref, wd_ref = refs[:13]
    srcs = refs[13:13 + n_src]
    pos = 13 + n_src
    dx_ref, gb_ref, gains_ref, gwg_ref, gwu_ref, gwd_ref = refs[pos:pos + 6]
    outs = refs[pos + 6:pos + 6 + n_src]
    pos = pos + 6 + n_src
    qkv, a_scr, qr, kr, st, k_scr, v_scr, dk_acc, dv_acc, m_scr, n_scr, inv_scr, acc, hid, dg, du, wg_t, wu_t, wd_t, wo_t, wqkv_t, gacc, wqkv_ref, ga_ref, gf_ref, gwo_acc = refs[pos:pos + 26]
    comm_refs = refs[pos + 26:]
    step = pl.program_id(0)
    heads = kv_heads * n_group
    n_ffn = pl.num_programs(0) - 2 * heads
    att_scale = head_dim ** -0.5
    per = (n_group + 2) * head_dim

    if n_src:
        comm = Comm(LAYER_SUB, srcs, outs, comm_refs)
        for at in range(pl_steps):
            todo = [(stage, sub) for stage in range(len(COMM_AT[0])) for sub in range(LAYER_SUB) if COMM_AT[sub][stage] == at]
            if todo:
                @pl.when(step == at)
                def _(todo=todo, at=at):
                    if at == 0:
                        comm.barrier()
                    for stage, sub in todo:
                        comm.serve(stage, sub)

    @pl.when(step == 0)
    def _():
        q_rows = n_group * head_dim
        for g in range(kv_heads):
            wqkv_ref[g * per:g * per + q_rows, :] = wq_ref[g * q_rows:(g + 1) * q_rows, :]
            wqkv_ref[g * per + q_rows:g * per + q_rows + head_dim, :] = wk_ref[g * head_dim:(g + 1) * head_dim, :]
            wqkv_ref[g * per + q_rows + head_dim:(g + 1) * per, :] = wv_ref[g * head_dim:(g + 1) * head_dim, :]
        for src, dst in ((ga_in, ga_ref), (gf_in, gf_ref)):
            row = src[...].astype(F32)[layer:layer + 1, :]
            dst[...] = jnp.broadcast_to(row, (8, row.shape[1])).T[:, 0:1]
        clear(gains_ref)
        qkv_step(x_ref, ga_ref, wqkv_ref, qkv)

    def head_views(idx):
        g, h = idx // n_group, lax.rem(idx, n_group)
        base = g * per
        rows_q = ds_of(base + h * head_dim, head_dim, head_dim)
        rows_k = ds_of(base + n_group * head_dim, head_dim, head_dim)
        rows_v = ds_of(base + (n_group + 1) * head_dim, head_dim, head_dim)
        return h, qkv.at[rows_q, :], qkv.at[rows_k, :], qkv.at[rows_v, :], a_scr.at[ds_of(idx * head_dim, head_dim, head_dim), :], qr.at[ds_of(idx * head_dim, head_dim, head_dim), :], kr.at[ds_of(g * head_dim, head_dim, head_dim), :], st.at[idx]

    @pl.when(step < heads)
    def _():
        h, q_v, k_v, v_v, a_v, qr_v, kr_v, st_v = head_views(step)
        attn_fwd_step(att_scale, h == 0, q_v, k_v, v_v, cos_ref, sin_ref, a_v, qr_v, kr_v, st_v, k_scr)

    @pl.when((step >= heads) & (step < heads + n_ffn))
    def _():
        ffn_step(scale, step == heads, step == heads + n_ffn - 1, x_ref, a_scr, dout_ref, wo_ref, gf_ref, wg_ref, wu_ref, wd_ref, gb_ref.at[:, per * kv_heads:], gwo_acc, gains_ref.at[1:2, :], gwg_ref, gwu_ref, gwd_ref, m_scr, n_scr, inv_scr, acc, hid, dg, du, wg_t, wu_t, wd_t, wo_t, gacc)

    @pl.when(step >= heads + n_ffn)
    def _():
        h, q_v, k_v, v_v, a_v, qr_v, kr_v, st_v = head_views(step - heads - n_ffn)
        attn_bwd_step(att_scale, h == 0, h == n_group - 1, qr_v, kr_v, v_v, a_v, st_v, cos_ref, sin_ref, q_v, k_v, v_v, k_scr, v_scr, dk_acc, dv_acc)

    @pl.when(step == pl.num_programs(0) - 1)
    def _():
        input_step(scale, x_ref, m_scr, ga_ref, wqkv_ref, qkv, dx_ref, gb_ref.at[:, :per * kv_heads], gains_ref.at[0:1, :], wqkv_t, gacc)
        if n_src:
            comm.close()


def layer_call(layer, x_t, d_out_t, weights, cos_t, sin_t, scale, dims, other=None):
    g_attn, wq_t, wk_t, wv_t, w_o, g_ffn, w_gate, w_up, wd_t = weights
    kv_heads, n_group, head_dim = dims
    model_dim, seq_len = x_t.shape
    ff_dim = w_gate.shape[2]
    heads = kv_heads * n_group
    n_ffn = ff_dim // BLK
    qkv_rows = (heads + 2 * kv_heads) * head_dim
    w_spec = pl.BlockSpec((None, model_dim, BLK), lambda t: (layer, 0, jnp.minimum(jnp.maximum(t - heads, 0), n_ffn - 1)))
    g_spec = pl.BlockSpec((model_dim, BLK), lambda t: (0, jnp.minimum(jnp.maximum(t - heads, 0), n_ffn - 1)))
    hbm = pl.BlockSpec(memory_space=pl.ANY)

    def one(w):
        return pl.BlockSpec((None,) + w.shape[1:], lambda t: (layer, 0, 0), pipeline_mode=pl.Buffered(1))

    in_specs = [whole_once(x_t.shape), whole_once(x_t.shape), one(wq_t), one(wk_t), one(wv_t), one(w_o), whole_once(g_attn.shape), whole_once(g_ffn.shape), whole_once(cos_t.shape), whole_once(cos_t.shape), w_spec, w_spec, w_spec]
    args = [x_t, d_out_t, wq_t, wk_t, wv_t, w_o, g_attn, g_ffn, cos_t, sin_t, w_gate, w_up, wd_t]
    shape = jax.ShapeDtypeStruct
    qkv_w, o_w, grad_w, gain_w = (qkv_rows, model_dim), w_o.shape[1:], w_gate.shape[1:], (8, model_dim)
    out_specs = [whole_once(x_t.shape), whole_once(grad_w), whole_once(gain_w), g_spec, g_spec, g_spec]
    out_shape = [shape(x_t.shape, BF16), shape(grad_w, F32), shape(gain_w, F32)] + [shape(grad_w, F32)] * 3
    vm = pltpu.VMEM
    tok = (seq_len, head_dim)
    scratch = [vm((qkv_rows, seq_len), BF16), vm((heads * head_dim, seq_len), BF16), vm((heads * head_dim, seq_len), BF16), vm((kv_heads * head_dim, seq_len), BF16), vm((heads, 8, seq_len), F32)]
    scratch += [vm(tok, BF16), vm(tok, BF16), vm(tok[::-1], F32), vm(tok[::-1], F32), vm(x_t.shape, BF16), vm(x_t.shape, BF16), vm((8, seq_len), F32), vm(x_t.shape, F32)]
    scratch += [vm((BLK, seq_len), BF16)] * 3 + [vm((BLK, model_dim), BF16)] * 3 + [vm(o_w[::-1], BF16), vm(qkv_w[::-1], BF16), vm((model_dim, 128), F32), vm(qkv_w, BF16), vm((model_dim, 1), F32), vm((model_dim, 1), F32), vm(o_w, F32)]
    n_src = 0
    params = {}
    if other is not None:
        n_src = len(other)
        args += list(other)
        in_specs += [hbm] * n_src
        out_specs += [hbm] * n_src
        out_shape += [shape(grad.shape, F32) for grad in other]
        scratch += comm_scratch(LAYER_SUB, other)
        params = dict(collective_id=0, has_side_effects=True)
    return pl.pallas_call(
        functools.partial(layer_kernel, layer, scale, dims, 2 * heads + n_ffn, n_src),
        grid=(2 * heads + n_ffn,),
        in_specs=in_specs,
        out_specs=out_specs,
        out_shape=out_shape,
        scratch_shapes=scratch,
        compiler_params=pltpu.CompilerParams(vmem_limit_bytes=VMEM_ALL, **params),
        cost_estimate=pl.CostEstimate(flops=24 * x_t.size * ff_dim, bytes_accessed=20 * grad_w[0] * grad_w[1], transcendentals=0),
        name="layer" if other is None else "layer_and_sum",
    )(*args)


def solution(mesh):
    num_devices = mesh.shape["dp"]
    act_spec = P("dp", None, None)
    rep_spec = P()

    def local_step(x_layer0, x_layer1, d_out, g_attn, w_q, w_k, w_v, w_o, g_ffn, w_gate, w_up, w_down):
        _, seq_len, model_dim = x_layer0.shape
        n_heads, head_dim = w_q.shape[2], w_q.shape[3]
        kv_heads = w_k.shape[2]
        n_group = n_heads // kv_heads
        cos_np, sin_np = rope_tables_np(seq_len, head_dim)
        cos_t, sin_t = jnp.asarray(cos_np), jnp.asarray(sin_np)
        scale = 1.0 / num_devices

        def heads_out(w):
            return jnp.transpose(w, (0, 2, 3, 1)).reshape(2, -1, model_dim)

        weights = (g_attn, heads_out(w_q), heads_out(w_k), heads_out(w_v), w_o.reshape(2, -1, model_dim), g_ffn, w_gate, w_up, jnp.transpose(w_down, (0, 2, 1)))
        x0_t = jnp.transpose(x_layer0[0], (1, 0))
        x1_t = jnp.transpose(x_layer1[0], (1, 0))
        d_top = jnp.transpose(d_out[0], (1, 0))
        dims = (kv_heads, n_group, head_dim)
        d_mid, gb1, gains1, gg1, gu1, gd1 = layer_call(1, x1_t, d_top, weights, cos_t, sin_t, scale, dims)
        low = layer_call(0, x0_t, d_mid, weights, cos_t, sin_t, scale, dims, (gg1, gu1, gd1, gb1))
        d_x0, gb0, gains0, gg0, gu0, gd0 = low[:6]
        sums = all_reduce((gg0, gu0, gd0, gb0), gains0, gains1)
        sum_g = sums[4]
        sum_gate, sum_up, sum_wd, sum_q, sum_k, sum_v, sum_o, grad_ga, grad_gf, d_x0 = assemble(sums[:4], low[6:], sum_g, d_x0, n_group, head_dim)

        def heads_in(g):
            return jnp.transpose(g.reshape(2, -1, head_dim, model_dim), (0, 3, 1, 2))

        d_x = jnp.transpose(d_x0, (1, 0))[None]
        return (d_x, grad_ga, heads_in(sum_q), heads_in(sum_k), heads_in(sum_v), sum_o.reshape(2, n_heads, head_dim, model_dim), grad_gf, sum_gate, sum_up, jnp.transpose(sum_wd, (0, 2, 1)))

    return jax.shard_map(local_step, mesh=mesh, in_specs=(act_spec, act_spec, act_spec) + (rep_spec,) * 9, out_specs=(act_spec,) + (rep_spec,) * 9, check_vma=False)
```

time: 362 us -> 302 us (0.83)
  local copies, waits for them, and re-layouts: 31.2 us -> 0 us
  other arithmetic: 21.5 us -> 0 us
  Pallas kernels: 308 us -> 300 us
    unnamed x37 -> x0, local copies, waits for them, and re-layouts: 14.3 us -> none
    another operation x4 -> x0, other arithmetic: 12 us -> none  [local_step(): jnp.stack([first, second])]
    pallas_call x3 -> x4, Pallas kernels: 308 us -> 300 us  [the longest x2 195 us: layer_call(): pl.pallas_call(functools.partial(layer_kernel, layer, scale, dims, 2 * he...]
    transpose x2 -> x0, other arithmetic: 6.24 us -> none  [the longest x1 3.51 us: local_step(): jnp.transpose(sum_wd, (0, 2, 1))]
    pallas_call x4 -> x0, local copies, waits for them, and re-layouts: 4.39 us -> none  [layer_call(): pl.pallas_call(functools.partial(layer_kernel, scale, dims, comm_dims), g...]
where the time goes in v5:
time: 302 us; the launch traced here: 301 us
  Pallas kernels  300 us (99%)
    pallas_call x2, Pallas kernels, layer_call(): pl.pallas_call(functools.partial(layer_kernel, layer, scale, dims, 2 * he...  195 us
    pallas_call x1, Pallas kernels, all_reduce(): pl.pallas_call(functools.partial(all_reduce_kernel, n_mat), in_specs=[hbm...  78.4 us
    pallas_call x1, Pallas kernels, assemble(): pl.pallas_call(functools.partial(assemble_kernel, n_group), grid=(2, head...  27.5 us

profile of v5, /device:TPU:1, one launch (start us, length us, event | category | flops | bytes accessed | tf_op | source)
XLA Modules:
  0.0 301.2 jit_solution(8854620096387335563)
XLA Ops:
  0.6 87.6 %layer.1 = (bf16[576,1024]{1,0:T(8,128)(2,1)}, f32[576,1536]{1,0:T(8,128)}, f32[8,576]{1,0:T(8,128)}, f32[576,1536]{1,0:T(8,128)}, f32[576,1536]{1,0:T(8,128)}, /*index=5*/f32[576,1536]{1,0:T(8,128)}) custom-call(bf16[576,1024]{1,0:T(8,128)(2,1)} %bitcast.43, bf16[576,1024]{1,0:T(8,128)(2,1)} %bitcast.44, bf16[2,576,576]{2,1,0:T(8,128)(2,1)} %bitcast.39, ...), custom_call_target="tpu_custom_call" | custom-call | flops 21743271936 | bytes 17694720 | tf_op jit(solution)/shard_map/layer/pallas_call | solution.py:660
  88.2 106.9 %layer_and_sum.1 = (bf16[576,1024]{1,0:T(8,128)(2,1)}, f32[576,1536]{1,0:T(8,128)}, f32[8,576]{1,0:T(8,128)}, f32[576,1536]{1,0:T(8,128)}, f32[576,1536]{1,0:T(8...) custom-call(bf16[576,1024]{1,0:T(8,128)(2,1)} %bitcast.45, ...), custom_call_target="tpu_custom_call" | custom-call | flops 21743271936 | bytes 17694720 | tf_op jit(solution)/shard_map/layer_and_sum/pallas_call | solution.py:660
  195.2 78.4 %all_reduce.1 = (f32[576,1536]{1,0:T(8,128)}, f32[576,1536]{1,0:T(8,128)}, f32[576,1536]{1,0:T(8,128)}, f32[576,1536]{1,0:T(8,128)}, f32[8,576]{1,0:T(8,128)}) custom-call(f32[576,1536]{1,0:T(8,128)} %get-tuple-element.46.refs_0_, f32[576,1536]{1,0:T(8,128)} %get-tuple-element.47.refs_1_, f32[576,1536]{1,0:T(8,128)} %get-tuple-element.48.refs_2_, ...), custom_call_target="tpu_custom_call" | custom-call | tf_op jit(solution)/shard_map/all_reduce/pallas_call | solution.py:291
  273.5 27.5 %assemble.1 = (f32[2,576,1536]{2,1,0:T(8,128)}, f32[2,576,1536]{2,1,0:T(8,128)}, f32[2,576,1536]{2,1,0:T(8,128)}, f32[2,576,576]{2,1,0:T(8,128)}, f32[2,192,576]...) custom-call(f32[576,1536]{1,0:T(8,128)} %get-tuple-element.52.refs_0, ...), custom_call_target="tpu_custom_call" | custom-call | tf_op jit(solution)/shard_map/assemble/pallas_call | solution.py:351

commit v6 on v5

--- a/solution.py
+++ b/solution.py
@@ -303,8 +303,8 @@
     low, top, (sum_g, dx_in), outs = refs[:4], refs[4:8], refs[8:10], refs[10:17]
     grad_ga, grad_gf, dx_out, turned = refs[17:]
     layer, i = pl.program_id(0), pl.program_id(1)
-    head_dim = outs[-1].shape[0]
-    base = (i // n_group) * (n_group + 2)
+    rows, head_dim = outs[3].shape[0], outs[4].shape[0]
+    base = i * (n_group + 2) * head_dim
 
     def fill(mats):
         for src, dst in zip(mats[:3], outs):
@@ -326,31 +326,32 @@
     def _():
         fill(top)
 
-    spots = (base + lax.rem(i, n_group), base + n_group, base + n_group + 1, i + pl.num_programs(1) * (n_group + 2) // n_group)
+    spots = (base, base + rows, base + rows + head_dim, (pl.num_programs(1) * (n_group + 2) + i * n_group) * head_dim)
     for spot, dst in zip(spots, outs[3:]):
-        dst[...] = turned[ds_of(spot * head_dim, head_dim, head_dim), :]
+        dst[...] = turned[ds_of(spot, dst.shape[0], head_dim), :]
 
 
 def assemble(low, top, sum_g, d_x, n_group, head_dim):
     model_dim, ff_dim = low[0].shape
     heads = model_dim // head_dim
     kv_heads = heads // n_group
+    rows = n_group * head_dim
 
     def maps(layer):
         def at(l, i):
-            return i * (1 - l) + (heads - 1) * l if layer == 0 else i * l
-        return [pl.BlockSpec((head_dim, ff_dim), lambda l, i: (at(l, i), 0))] * 3 + [pl.BlockSpec(low[3].shape, lambda l, i: (0, 0), pipeline_mode=pl.Buffered(1))]
-
-    out_big = pl.BlockSpec((None, head_dim, ff_dim), lambda l, i: (l, i, 0))
-    out_small = pl.BlockSpec((None, head_dim, model_dim), lambda l, i: (l, i, 0))
-    out_kv = pl.BlockSpec((None, head_dim, model_dim), lambda l, i: (l, i // n_group, 0))
+            return i * (1 - l) + (kv_heads - 1) * l if layer == 0 else i * l
+        return [pl.BlockSpec((rows, ff_dim), lambda l, i: (at(l, i), 0))] * 3 + [pl.BlockSpec(low[3].shape, lambda l, i: (0, 0), pipeline_mode=pl.Buffered(1))]
+
+    out_big = pl.BlockSpec((None, rows, ff_dim), lambda l, i: (l, i, 0))
+    out_small = pl.BlockSpec((None, rows, model_dim), lambda l, i: (l, i, 0))
+    out_kv = pl.BlockSpec((None, head_dim, model_dim), lambda l, i: (l, i, 0))
     shape = jax.ShapeDtypeStruct
     gain_shape = shape((2, model_dim), F32)
-    dx_spec = pl.BlockSpec((head_dim, d_x.shape[1]), lambda l, i: (i * (1 - l) + (heads - 1) * l, 0))
+    dx_spec = pl.BlockSpec((rows, d_x.shape[1]), lambda l, i: (i * (1 - l) + (kv_heads - 1) * l, 0))
     big_shape, q_shape, kv_shape = shape((2, model_dim, ff_dim), F32), shape((2, model_dim, model_dim), F32), shape((2, kv_heads * head_dim, model_dim), F32)
     return pl.pallas_call(
         functools.partial(assemble_kernel, n_group),
-        grid=(2, heads),
+        grid=(2, kv_heads),
         in_specs=maps(0) + maps(1) + [whole_once(sum_g.shape), dx_spec],
         out_specs=[out_big] * 3 + [out_small, out_kv, out_kv, out_small, whole_once(gain_shape.shape), whole_once(gain_shape.shape), dx_spec],
         out_shape=[big_shape] * 3 + [q_shape, kv_shape, kv_shape, q_shape, gain_shape, gain_shape, shape(d_x.shape, d_x.dtype)],
@@ -469,8 +470,8 @@
         dv_ref[...] = dv_acc[...].astype(BF16)
 
 
-def input_step(scale, x_ref, dmid_ref, gain_ref, w_ref, dqkv, dx_ref, gw_ref, gg_ref, w_t, gacc):
-    clear(gacc, gw_ref)
+def input_step(scale, x_ref, dmid_ref, gain_ref, w_ref, dqkv, dx_ref, gw_ref, gg_ref, w_t, n_scr, gacc):
+    clear(gacc)
     gain = gain_ref[...]
     w_t[...] = w_ref[...].T
 
@@ -479,18 +480,17 @@
         cols = ds_of(j * BLK, BLK, BLK)
         x_f = x_ref[:, cols].astype(F32)
         inv = lax.rsqrt(jnp.mean(x_f * x_f, axis=0, keepdims=True) + NORM_EPS)
-        normed = (x_f * inv * gain).astype(BF16)
-        gw_ref[...] += dot_nt(normed, dqkv[:, cols])
+        n_scr[:, cols] = (x_f * inv * gain).astype(BF16)
         d_normed = dot_nn(w_t[...], dqkv[:, cols]).astype(BF16).astype(F32)
         d_resid, d_gain = norm_back_cols(x_f, inv, gain, d_normed)
         gacc[...] += fold_lanes(d_gain)
         dx_ref[:, cols] = (dmid_ref[:, cols].astype(F32) + d_resid).astype(BF16)
 
-    gw_ref[...] = gw_ref[...] * scale
+    gw_ref[...] = dot_nt(n_scr[...], dqkv[...]) * scale
     gg_ref[...] = jnp.sum(gacc[...].T, axis=0, keepdims=True) * scale
 
 
-def ffn_step(scale, first, last, x_ref, a_ref, dout_ref, wo_ref, gain_ref, wg_ref, wu_ref, wd_ref, gwo_ref, gwo_acc, gg_ref, gwg_ref, gwu_ref, gwd_ref, m_scr, n_scr, inv_scr, acc, hid, dg, du, wg_t, wu_t, wd_t, wo_t, gacc):
+def ffn_step(scale, first, last, x_ref, a_ref, dout_ref, wo_ref, gain_ref, wg_ref, wu_ref, wd_ref, gwo_ref, gg_ref, gwg_ref, gwu_ref, gwd_ref, m_scr, n_scr, inv_scr, acc, hid, dg, du, wg_t, wu_t, wd_t, wo_t, gacc):
     n_blk = x_ref.shape[1] // BLK
     gain = gain_ref[...]
 
@@ -530,7 +530,6 @@
 
     @pl.when(last)
     def _():
-        clear(gwo_acc)
 
         @pl.loop(0, n_blk)
         def _(j):
@@ -539,11 +538,10 @@
             d_resid, d_gain = norm_back_cols(m_scr[:, cols].astype(F32), inv_scr[0:1, cols], gain, d_normed)
             gacc[...] += fold_lanes(d_gain)
             d_mid = (dout_ref[:, cols].astype(F32) + d_resid).astype(BF16)
-            gwo_acc[...] += dot_nt(d_mid, a_ref[:, cols])
             m_scr[:, cols] = d_mid
-            a_ref[:, cols] = dot_nn(wo_ref[...], d_mid).astype(BF16)
-
-        gwo_ref[...] = gwo_acc[...] * scale
+
+        gwo_ref[...] = dot_nt(m_scr[...], a_ref[...]) * scale
+        a_ref[...] = dot_nn(wo_ref[...], m_scr[...]).astype(BF16)
         gg_ref[...] = jnp.sum(gacc[...].T, axis=0, keepdims=True) * scale
 
 
@@ -559,8 +557,8 @@
     dx_ref, gb_ref, gains_ref, gwg_ref, gwu_ref, gwd_ref = refs[pos:pos + 6]
     outs = refs[pos + 6:pos + 6 + n_src]
     pos = pos + 6 + n_src
-    qkv, a_scr, qr, kr, st, k_scr, v_scr, dk_acc, dv_acc, m_scr, n_scr, inv_scr, acc, hid, dg, du, wg_t, wu_t, wd_t, wo_t, wqkv_t, gacc, wqkv_ref, ga_ref, gf_ref, gwo_acc = refs[pos:pos + 26]
-    comm_refs = refs[pos + 26:]
+    qkv, a_scr, qr, kr, st, k_scr, v_scr, dk_acc, dv_acc, m_scr, n_scr, inv_scr, acc, hid, dg, du, wg_t, wu_t, wd_t, wo_t, wqkv_t, gacc, wqkv_ref, ga_ref, gf_ref = refs[pos:pos + 25]
+    comm_refs = refs[pos + 25:]
     step = pl.program_id(0)
     heads = kv_heads * n_group
     n_ffn = pl.num_programs(0) - 2 * heads
@@ -607,7 +605,7 @@
 
     @pl.when((step >= heads) & (step < heads + n_ffn))
     def _():
-        ffn_step(scale, step == heads, step == heads + n_ffn - 1, x_ref, a_scr, dout_ref, wo_ref, gf_ref, wg_ref, wu_ref, wd_ref, gb_ref.at[:, per * kv_heads:], gwo_acc, gains_ref.at[1:2, :], gwg_ref, gwu_ref, gwd_ref, m_scr, n_scr, inv_scr, acc, hid, dg, du, wg_t, wu_t, wd_t, wo_t, gacc)
+        ffn_step(scale, step == heads, step == heads + n_ffn - 1, x_ref, a_scr, dout_ref, wo_ref, gf_ref, wg_ref, wu_ref, wd_ref, gb_ref.at[:, per * kv_heads:], gains_ref.at[1:2, :], gwg_ref, gwu_ref, gwd_ref, m_scr, n_scr, inv_scr, acc, hid, dg, du, wg_t, wu_t, wd_t, wo_t, gacc)
 
     @pl.when(step >= heads + n_ffn)
     def _():
@@ -616,7 +614,7 @@
 
     @pl.when(step == pl.num_programs(0) - 1)
     def _():
-        input_step(scale, x_ref, m_scr, ga_ref, wqkv_ref, qkv, dx_ref, gb_ref.at[:, :per * kv_heads], gains_ref.at[0:1, :], wqkv_t, gacc)
+        input_step(scale, x_ref, m_scr, ga_ref, wqkv_ref, qkv, dx_ref, gb_ref.at[:, :per * kv_heads], gains_ref.at[0:1, :], wqkv_t, n_scr, gacc)
         if n_src:
             comm.close()
 
@@ -646,7 +644,7 @@
     tok = (seq_len, head_dim)
     scratch = [vm((qkv_rows, seq_len), BF16), vm((heads * head_dim, seq_len), BF16), vm((heads * head_dim, seq_len), BF16), vm((kv_heads * head_dim, seq_len), BF16), vm((heads, 8, seq_len), F32)]
     scratch += [vm(tok, BF16), vm(tok, BF16), vm(tok[::-1], F32), vm(tok[::-1], F32), vm(x_t.shape, BF16), vm(x_t.shape, BF16), vm((8, seq_len), F32), vm(x_t.shape, F32)]
-    scratch += [vm((BLK, seq_len), BF16)] * 3 + [vm((BLK, model_dim), BF16)] * 3 + [vm(o_w[::-1], BF16), vm(qkv_w[::-1], BF16), vm((model_dim, 128), F32), vm(qkv_w, BF16), vm((model_dim, 1), F32), vm((model_dim, 1), F32), vm(o_w, F32)]
+    scratch += [vm((BLK, seq_len), BF16)] * 3 + [vm((BLK, model_dim), BF16)] * 3 + [vm(o_w[::-1], BF16), vm(qkv_w[::-1], BF16), vm((model_dim, 128), F32), vm(qkv_w, BF16), vm((model_dim, 1), F32), vm((model_dim, 1), F32)]
     n_src = 0
     params = {}
     if other is not None:

time: 302 us -> 295 us (0.977)
  Pallas kernels: 300 us -> 294 us
    pallas_call x1, Pallas kernels: 27.5 us -> 22.9 us  [assemble(): pl.pallas_call(functools.partial(assemble_kernel, n_group), grid=(2, kv_h...]
where the time goes in v6:
time: 295 us; the launch traced here: 294 us
  Pallas kernels  294 us (100%)
    pallas_call x2, Pallas kernels, layer_call(): pl.pallas_call(functools.partial(layer_kernel, layer, scale, dims, 2 * he...  192 us
    pallas_call x1, Pallas kernels, all_reduce(): pl.pallas_call(functools.partial(all_reduce_kernel, n_mat), in_specs=[hbm...  78.5 us
    pallas_call x1, Pallas kernels, assemble(): pl.pallas_call(functools.partial(assemble_kernel, n_group), grid=(2, kv_h...  22.9 us

profile of v6, /device:TPU:1, one launch (start us, length us, event | category | flops | bytes accessed | tf_op | source)
XLA Modules:
  0.0 294.4 jit_solution(11711044395369056165)
XLA Ops:
  0.6 86.4 %layer.1 = (bf16[576,1024]{1,0:T(8,128)(2,1)}, f32[576,1536]{1,0:T(8,128)}, f32[8,576]{1,0:T(8,128)}, f32[576,1536]{1,0:T(8,128)}, f32[576,1536]{1,0:T(8,128)}, /*index=5*/f32[576,1536]{1,0:T(8,128)}) custom-call(bf16[576,1024]{1,0:T(8,128)(2,1)} %bitcast.43, bf16[576,1024]{1,0:T(8,128)(2,1)} %bitcast.44, bf16[2,576,576]{2,1,0:T(8,128)(2,1)} %bitcast.39, ...), custom_call_target="tpu_custom_call" | custom-call | flops 21743271936 | bytes 17694720 | tf_op jit(solution)/shard_map/layer/pallas_call | solution.py:658
  87.0 105.7 %layer_and_sum.1 = (bf16[576,1024]{1,0:T(8,128)(2,1)}, f32[576,1536]{1,0:T(8,128)}, f32[8,576]{1,0:T(8,128)}, f32[576,1536]{1,0:T(8,128)}, f32[576,1536]{1,0:T(8...) custom-call(bf16[576,1024]{1,0:T(8,128)(2,1)} %bitcast.45, ...), custom_call_target="tpu_custom_call" | custom-call | flops 21743271936 | bytes 17694720 | tf_op jit(solution)/shard_map/layer_and_sum/pallas_call | solution.py:658
  192.7 78.5 %all_reduce.1 = (f32[576,1536]{1,0:T(8,128)}, f32[576,1536]{1,0:T(8,128)}, f32[576,1536]{1,0:T(8,128)}, f32[576,1536]{1,0:T(8,128)}, f32[8,576]{1,0:T(8,128)}) custom-call(f32[576,1536]{1,0:T(8,128)} %get-tuple-element.46.refs_0_, f32[576,1536]{1,0:T(8,128)} %get-tuple-element.47.refs_1_, f32[576,1536]{1,0:T(8,128)} %get-tuple-element.48.refs_2_, ...), custom_call_target="tpu_custom_call" | custom-call | tf_op jit(solution)/shard_map/all_reduce/pallas_call | solution.py:291
  271.2 22.9 %assemble.1 = (f32[2,576,1536]{2,1,0:T(8,128)}, f32[2,576,1536]{2,1,0:T(8,128)}, f32[2,576,1536]{2,1,0:T(8,128)}, f32[2,576,576]{2,1,0:T(8,128)}, f32[2,192,576]...) custom-call(f32[576,1536]{1,0:T(8,128)} %get-tuple-element.52.refs_0, ...), custom_call_target="tpu_custom_call" | custom-call | tf_op jit(solution)/shard_map/assemble/pallas_call | solution.py:352
